TPU v7x, 256 devices: a whole 4x4x8 slice. The times are simulated.
256 devices in a mesh: row: 8 (over y, x_lo), col: 16 (over z, core), layer: 2 (over x_hi).
Axes of the slice: x: 4 (x_hi: 2, x_lo: 2; x = x_hi * 2 + x_lo), y: 4, z: 8, core: 2. Of those that a mesh axis runs over, the one named last changes fastest.
Arguments:
- tokens: bfloat16 [10240, 8192], P('row', 'col'), may hold values from -6 to 6
- up_weight: bfloat16 [8192, 16384], P('row', 'col'), may hold values from -0.0625 to 0.0625
Outputs:
- up: bfloat16 [10240, 16384], P('row', ('col', 'layer'))
All inputs are finite; a program needn't handle non-finite values.
Results may differ from a plain program's by a relative error of at most 0.001.
Values may be sent and summed in bfloat16 or wider, within the bound.
No kernel may reach another device: no remote copies, remote signals or barrier semaphores. Data moves between devices by JAX's collectives and lax.ppermute only.
A program may use at most 128 MiB of HBM per device.

v0:
```python
import functools

import jax
import jax.numpy as jnp
from jax import lax
from jax.experimental import pallas as pl
from jax.experimental.pallas import tpu as pltpu
from jax.sharding import Mesh
from jax.sharding import PartitionSpec as P


AXES = ("y", "xl", "z", "core", "xh")
NEAR = (0, 1, 2, -1, -2)
LATE = (3, -3, 4)


def ring(size, shift):
    return [(i, (i + shift) % size) for i in range(size)]


VMEM = pl.BlockSpec(memory_space=pltpu.VMEM)
ANYWHERE = pl.BlockSpec(memory_space=pl.ANY)


def meets(d, zn, yn):
    y, xl, z = (lax.axis_index(axis) for axis in ("y", "xl", "z"))
    block = lax.rem(z + d + zn, zn)
    across = lax.rem(block // 2 - y + yn, yn)
    return across, 2 * across + jnp.where(lax.rem(block, 2) == xl, 0, 1)


def places(rows, nb):
    xh = lax.axis_index("xh")
    return (
        pl.ds(2 * nb, rows - 2 * nb),
        pl.ds(pl.multiple_of(xh * nb, nb), nb),
        pl.ds(pl.multiple_of((1 - xh) * nb, nb), nb),
    )


def call(kernel, out_shape, blocks, tokens, weights, extra, scratch):
    rows, width = out_shape[-2:]
    depth = weights[0].shape[0]
    parts = [part for block in tokens for part, _ in block]
    return pl.pallas_call(
        kernel,
        out_shape=jax.ShapeDtypeStruct(out_shape, jnp.float32),
        in_specs=[VMEM] * (len(extra) + len(parts)) + [ANYWHERE] * len(weights),
        out_specs=VMEM,
        scratch_shapes=[pltpu.VMEM((2, depth, width), jnp.bfloat16), pltpu.SemaphoreType.DMA((2,))]
        + scratch,
        compiler_params=pltpu.CompilerParams(vmem_limit_bytes=8 * 1024 * 1024),
        cost_estimate=pl.CostEstimate(
            flops=2 * rows * width * depth * blocks,
            bytes_accessed=2 * blocks * depth * (rows + width) + 4 * rows * width,
            transcendentals=0,
        ),
    )(*extra, *parts, *weights)


def early_product(tokens, near_weights, rows, nb, zn, yn):
    width = near_weights[0][0][0].shape[1]
    arrays = [w for half in near_weights for w, _ in half]
    known = (0, 1, 2, 3, 2 * yn - 2, 2 * yn - 1)

    def kernel(*refs):
        parts, w_refs = refs[: 3 * len(NEAR)], refs[3 * len(NEAR) : -3]
        out_ref, w_buf, sem = refs[-3:]
        at = places(rows, nb)

        def copy(half, i, slot):
            return pltpu.make_async_copy(
                w_refs[6 * half + i].at[:, pl.ds(near_weights[half][i][1], width)],
                w_buf.at[slot],
                sem.at[slot],
            )

        def start(turn, d, slot):
            _, index = meets(d, zn, yn)
            for half in range(2):
                for i, number in enumerate(known):
                    @pl.when(jnp.logical_and(turn == half, index == number))
                    def _():
                        copy(half, i, slot).start()

        def both(turn, carry):
            out_ref[turn] = jnp.zeros((rows, width), jnp.float32)
            start(turn, NEAR[0], 0)
            for j, d in enumerate(NEAR):
                slot = j % 2
                if j + 1 < len(NEAR):
                    start(turn, NEAR[j + 1], 1 - slot)

                @pl.when(meets(d, zn, yn)[0] != yn // 2)
                def _():
                    copy(0, 0, slot).wait()
                    for ref, (part, first), where in zip(parts[3 * j : 3 * j + 3], tokens[j], at):
                        out_ref[turn, where, :] += jnp.dot(
                            ref[first : first + where.size, :],
                            w_buf[slot],
                            preferred_element_type=jnp.float32,
                        )

            return carry

        lax.fori_loop(0, 2, both, 0)

    return call(kernel, (2, rows, width), 6, tokens, arrays, [], [])


def final_product(half, total, late_tokens, near_tokens, weights, rows, nb, zn, yn):
    depth, width = weights[0][0].shape[0], total.shape[2]
    tokens = late_tokens + near_tokens
    late = len(LATE)

    def kernel(total_ref, *refs):
        parts, w_refs = refs[: 3 * len(tokens)], refs[3 * len(tokens) : -5]
        out_ref, w_buf, w_sem, t_buf, t_sem = refs[-5:]
        at = places(rows, nb)

        def weight_copy(i, slot):
            return pltpu.make_async_copy(
                w_refs[i].at[:, pl.ds(weights[i][1], width)], w_buf.at[slot], w_sem.at[slot]
            )

        def start_weight(index, slot, wanted):
            for i in range(len(weights)):
                @pl.when(jnp.logical_and(wanted, index == i))
                def _():
                    weight_copy(i, slot).start()

        def token_copies(j, slot):
            return [
                pltpu.make_async_copy(
                    ref.at[pl.ds(first, where.size)], t_buf.at[slot, where], t_sem.at[slot, k]
                )
                for k, (ref, (_, first), where) in enumerate(
                    zip(parts[3 * j : 3 * j + 3], tokens[j], at)
                )
            ]

        start_weight(meets(LATE[0], zn, yn)[1], 0, True)
        found, side = jnp.int32(0), [jnp.int32(0)] * 2
        for j, d in enumerate(NEAR):
            across, index = meets(d, zn, yn)
            for slot in range(2):
                here = jnp.logical_and(across == yn // 2, found == slot)
                side[slot] = jnp.where(here, index, side[slot])

                @pl.when(here)
                def _():
                    for copy in token_copies(late + j, slot):
                        copy.start()
            found = found + jnp.where(across == yn // 2, 1, 0)

        for j in range(late):
            slot = j % 2
            if j + 1 < late:
                start_weight(meets(LATE[j + 1], zn, yn)[1], 1 - slot, True)
            else:
                start_weight(side[0], 1 - slot, found > 0)
            weight_copy(0, slot).wait()
            for ref, (_, first), where in zip(parts[3 * j : 3 * j + 3], tokens[j], at):
                before = total_ref[half, where, :] if j == 0 else out_ref[where, :]
                out_ref[where, :] = before + jnp.dot(
                    ref[first : first + where.size, :],
                    w_buf[slot],
                    preferred_element_type=jnp.float32,
                )

        def rest(k, carry):
            slot = lax.rem(late + k, 2)

            @pl.when(jnp.logical_and(k == 0, found > 1))
            def _():
                start_weight(side[1], 1 - late % 2, True)

            weight_copy(0, slot).wait()
            for copy in token_copies(late, k):
                copy.wait()
            for first in range(0, rows, rows // 2):
                where = slice(first, first + rows // 2)
                out_ref[where, :] += jnp.dot(
                    t_buf[k, where, :], w_buf[slot], preferred_element_type=jnp.float32
                )
            return carry

        lax.fori_loop(0, found, rest, 0)

    scratch = [pltpu.VMEM((2, rows, depth), jnp.bfloat16), pltpu.SemaphoreType.DMA((2, 3))]
    arrays = [w for w, _ in weights]
    return call(kernel, (rows, width), 4, tokens, arrays, [total], scratch)


def per_device(tokens, up_weight):
    _, _, _, core, xh = (lax.axis_index(axis) for axis in AXES)
    zn, yn = lax.axis_size("z"), lax.axis_size("y")
    rows, depth = tokens.shape
    nb = 11 * rows // 40
    width = up_weight.shape[1] // 2

    def up(axis, a):
        return lax.ppermute(a, axis, ring(lax.axis_size(axis), 1))

    def down(axis, a):
        return lax.ppermute(a, axis, ring(lax.axis_size(axis), -1))

    def crossed(a, shift):
        pairs = [
            (2 * i + k, 2 * ((i + shift) % yn) + 1 - k) for i in range(yn) for k in range(2)
        ]
        return lax.ppermute(a, ("y", "core"), pairs)

    def quarter(parity, layer):
        return lax.dynamic_slice(
            up_weight, (parity * depth, layer * width), (depth, width)
        )

    b, c, a = {}, {}, {}
    b[0] = lax.dynamic_slice_in_dim(tokens, xh * nb, nb, 0)
    c[0] = lax.dynamic_slice_in_dim(tokens, (1 - xh) * nb, nb, 0)
    a[0] = tokens[2 * nb :]
    mine, given, far = quarter(core, xh), quarter(1 - core, xh), quarter(1 - core, 1 - xh)

    b[-1], b[1] = up("z", b[0]), down("z", b[0])
    a[-1], a[1] = up("z", a[0]), down("z", a[0])
    b[-2], b[2] = up("z", b[-1]), down("z", b[1])
    a[-2], a[2] = up("z", a[-1]), down("z", a[1])
    b[-3], b[3] = up("z", b[-2]), down("z", b[2])
    a[-3], a[3] = up("z", a[-2]), down("z", a[2])
    b[4], a[4] = down("z", b[3]), up("z", a[-3])
    for d in (1, 2, 3):
        pair = lax.ppermute(jnp.concatenate([b[-d], b[d]], 0), "xh", ring(2, 1))
        c[-d], c[d] = (pair, 0), (pair, nb)
    c[0], c[4] = (c[0], 0), (lax.ppermute(b[4], "xh", ring(2, 1)), 0)

    wa, wb, wo = {0: mine}, {}, {}
    wa[-1], wa[1] = up("y", mine), down("y", mine)
    wb[-1], wb[1] = crossed(given, 1), crossed(given, -1)
    near = lax.ppermute(mine, "xl", ring(2, 1))
    across = lax.ppermute(far, ("xl", "core", "xh"), [(i, 7 - i) for i in range(8)])
    wb[0] = lax.ppermute(given, "core", ring(2, 1))
    wo[0] = jnp.concatenate([near, across], 1)
    wo[-1], wo[1] = up("y", wo[0]), down("y", wo[0])
    wide = jnp.concatenate([wa[-1], wb[-1]], 1)
    wide = up("y", wide)
    wo[2] = down("y", wo[1])

    def block(d):
        return [(a[d], 0), (b[d], 0), c[d]]

    near, late = [block(d) for d in NEAR], [block(d) for d in LATE]

    def weights(half, distances):
        listed = []
        for dy in distances:
            own = (wide, half * width) if dy == 2 else ((wb if half else wa)[dy], 0)
            listed += [own, (wo[dy], half * width)]
        return listed

    sizes = (rows, nb, zn, yn)
    total = early_product(near, [weights(half, (0, 1, -1)) for half in range(2)], *sizes)
    rest = [
        functools.partial(
            final_product, half, total, late, near, weights(half, (0, 1, 2, -1)), *sizes
        )
        for half in range(2)
    ]
    swapped = lax.ppermute(rest[1](), "core", ring(2, 1))
    return (rest[0]() + swapped).astype(jnp.bfloat16)


def solution(mesh):
    split = Mesh(
        mesh.devices.reshape(4, 2, mesh.shape["col"] // 2, 2, mesh.shape["layer"]), AXES
    )
    spec = P(("y", "xl"), ("z", "core"))
    return jax.shard_map(
        per_device,
        mesh=split,
        in_specs=(spec, spec),
        out_specs=P(("y", "xl"), ("z", "core", "xh")),
        check_vma=False,
    )
```

profile of v0, /device:TPU:1, one launch (start us, length us, event | category | flops | bytes accessed | tf_op | source)
XLA Modules:
  0.0 151.2 jit_solution(4827975034360697656)
XLA Ops:
  0.0 1.1 constant_dynamic-slice_fusion
  1.1 2.5 %collective-permute-start.2 = (bf16[352,512]{1,0:T(8,128)(2,1)S(1)}, bf16[352,512]{1,0:T(8,128)(2,1)S(1)}, u32[]{:S(2)}, u32[]{:S(2)}) collective-permute-start(bf16[352,512]{1,0:T(8,128)(2,1)S(1)} %get-tuple-element.9.refs_1_.refs_10_), channel_id=1, source_target_pairs={{0,4},{4,8},{8,12},{12,16},{16,20},{20,24},{24,28},{28,0},{1,5},{5... | collective-permute-start | bytes 1081352 | tf_op jit(solution)/shard_map/ppermute | solution.py:203
  3.7 1.5 fusion
  5.1 3.4 %collective-permute-start.11 = (bf16[512,512]{1,0:T(8,128)(2,1)S(1)}, bf16[512,512]{1,0:T(8,128)(2,1)S(1)}, u32[]{:S(2)}, u32[]{:S(2)}) collective-permute-start(bf16[512,512]{1,0:T(8,128)(2,1)S(1)} %get-tuple-element.7), channel_id=1, source_target_pairs={{0,35},{1,34},{2,33},{3,32},{32,3},{33,2},{34,1},{35,0},{4,39},{5,... | collective-permute-start | bytes 1572872 | tf_op jit(solution)/shard_map/ppermute | solution.py:241
  8.5 3.7 %collective-permute-start.1 = (bf16[352,512]{1,0:T(8,128)(2,1)S(1)}, bf16[352,512]{1,0:T(8,128)(2,1)S(1)}, u32[]{:S(2)}, u32[]{:S(2)}) collective-permute-start(bf16[352,512]{1,0:T(8,128)(2,1)S(1)} %get-tuple-element.9.refs_1_.refs_10_), channel_id=1, source_target_pairs={{0,28},{4,0},{8,4},{12,8},{16,12},{20,16},{24,20},{28,24},{1,29},{... | collective-permute-start | bytes 1081352 | tf_op jit(solution)/shard_map/ppermute | solution.py:206
  12.2 1.3 collective-permute-start.18
  13.6 1.6 %collective-permute-start.17 = (bf16[512,512]{1,0:T(8,128)(2,1)S(1)}, bf16[512,512]{1,0:T(8,128)(2,1)S(1)}, u32[]{:S(2)}, u32[]{:S(2)}) collective-permute-start(bf16[512,512]{1,0:T(8,128)(2,1)S(1)} %get-tuple-element.5), channel_id=1, source_target_pairs={{0,194},{2,192},{64,2},{66,0},{128,66},{130,64},{192,130},{194,128... | collective-permute-start | bytes 1572872 | tf_op jit(solution)/shard_map/ppermute | solution.py:212
  15.2 0.5 collective-permute-done.2.refs_10_.refs_19_
  15.7 1.3 collective-permute-start.16
  17.0 3.2 %collective-permute-done.1.refs_4_.refs_13_ = bf16[352,512]{1,0:T(8,128)(2,1)S(1)} collective-permute-done((bf16[352,512]{1,0:T(8,128)(2,1)S(1)}, bf16[352,512]{1,0:T(8,128)(2,1)S(1)}, u32[]{:S(2)}, u32[]{:S(2)}) %collective-permute-start.1) | collective-permute-done | bytes 360480 | tf_op jit(solution)/shard_map/ppermute | solution.py:206
  20.2 1.3 collective-permute-start.14
  21.5 2.5 %collective-permute-start.12 = (bf16[512,512]{1,0:T(8,128)(2,1)S(1)}, bf16[512,512]{1,0:T(8,128)(2,1)S(1)}, u32[]{:S(2)}, u32[]{:S(2)}) collective-permute-start(bf16[512,512]{1,0:T(8,128)(2,1)S(1)} %get-tuple-element.6.refs_15_.refs_24_), channel_id=1, source_target_pairs={{0,192},{64,0},{128,64},{192,128},{1,193},{65,1},{129,65},{193,129... | collective-permute-start | bytes 1572872 | tf_op jit(solution)/shard_map/ppermute | solution.py:206
  24.0 3.7 %collective-permute-done.18.refs_25_.refs_30_ = bf16[512,512]{1,0:T(8,128)(2,1)S(1)} collective-permute-done((bf16[512,512]{1,0:T(8,128)(2,1)S(1)}, bf16[512,512]{1,0:T(8,128)(2,1)S(1)}, u32[]{:S(2)}, u32[]{:S(2)}) %collective-permute-start.18) | collective-permute-done | bytes 524320 | tf_op jit(solution)/shard_map/ppermute | solution.py:212
  27.7 0.4 collective-permute-done.17.refs_23_.refs_26_
  28.1 1.1 slice.3.refs_0_.refs_9_
  29.2 0.1 collective-permute-start.8
  29.3 8.9 %collective-permute-done.14.refs_19_.refs_30_ = bf16[512,512]{1,0:T(8,128)(2,1)S(1)} collective-permute-done((bf16[512,512]{1,0:T(8,128)(2,1)S(1)}, bf16[512,512]{1,0:T(8,128)(2,1)S(1)}, u32[]{:S(2)}, u32[]{:S(2)}) %collective-permute-start.14) | collective-permute-done | bytes 524320 | tf_op jit(solution)/shard_map/ppermute | solution.py:203
  38.2 1.7 %collective-permute-start = (bf16[576,512]{1,0:T(8,128)(2,1)S(1)}, bf16[576,512]{1,0:T(8,128)(2,1)S(1)}, u32[]{:S(2)}, u32[]{:S(2)}) collective-permute-start(bf16[576,512]{1,0:T(8,128)(2,1)S(1)} %slice.3.refs_0_.refs_9_), channel_id=1, source_target_pairs={{0,28},{4,0},{8,4},{12,8},{16,12},{20,16},{24,20},{28,24},{1,29},{... | collective-permute-start | bytes 1769480 | tf_op jit(solution)/shard_map/ppermute | solution.py:206
  39.9 0.7 collective-permute-start.5
  40.6 0.7 collective-permute-start.21
  41.4 0.1 collective-permute-done.10
  41.5 0.7 collective-permute-start.3
  42.1 0.1 constant_dynamic-update-slice_fusion.1
  42.2 0.1 constant_dynamic-update-slice_fusion.refs_16_.refs_22_.refs_25_
  42.3 9.8 %collective-permute-done.8.refs_9_.refs_18_ = bf16[576,512]{1,0:T(8,128)(2,1)S(1)} collective-permute-done((bf16[576,512]{1,0:T(8,128)(2,1)S(1)}, bf16[576,512]{1,0:T(8,128)(2,1)S(1)}, u32[]{:S(2)}, u32[]{:S(2)}) %collective-permute-start.8) | collective-permute-done | bytes 589856 | tf_op jit(solution)/shard_map/ppermute | solution.py:203
  52.1 2.1 %collective-permute-start.13 = (bf16[512,1024]{1,0:T(8,128)(2,1)S(1)}, bf16[512,1024]{1,0:T(8,128)(2,1)S(1)}, u32[]{:S(2)}, u32[]{:S(2)}) collective-permute-start(bf16[512,1024]{1,0:T(8,128)(2,1)S(1)} %constant_dynamic-update-slice_fusion.refs_16_.refs_22_.refs_25_), channel_id=1, source_target_pairs={{0,192},{64,0},{128,64},{192,128},{1,193},{65,1},{129,65},{193,129... | collective-permute-start | bytes 3145736 | tf_op jit(solution)/shard_map/ppermute | solution.py:206
  54.3 5.6 %collective-permute-done.5.refs_7_.refs_16_ = bf16[352,512]{1,0:T(8,128)(2,1)S(1)} collective-permute-done((bf16[352,512]{1,0:T(8,128)(2,1)S(1)}, bf16[352,512]{1,0:T(8,128)(2,1)S(1)}, u32[]{:S(2)}, u32[]{:S(2)}) %collective-permute-start.5) | collective-permute-done | bytes 360480 | tf_op jit(solution)/shard_map/ppermute | solution.py:206
  59.9 2.9 %collective-permute-start.4 = (bf16[576,512]{1,0:T(8,128)(2,1)S(1)}, bf16[576,512]{1,0:T(8,128)(2,1)S(1)}, u32[]{:S(2)}, u32[]{:S(2)}) collective-permute-start(bf16[576,512]{1,0:T(8,128)(2,1)S(1)} %collective-permute-done.refs_3_.refs_12_), channel_id=1, source_target_pairs={{0,28},{4,0},{8,4},{12,8},{16,12},{20,16},{24,20},{28,24},{1,29},{... | collective-permute-start | bytes 1769480 | tf_op jit(solution)/shard_map/ppermute | solution.py:206
  62.8 0.0 collective-permute-start.20
  62.8 0.1 pad_maximum_fusion
  63.0 18.5 %collective-permute-done.20.refs_1_ = bf16[352,512]{1,0:T(8,128)(2,1)S(1)} collective-permute-done((bf16[352,512]{1,0:T(8,128)(2,1)S(1)}, bf16[352,512]{1,0:T(8,128)(2,1)S(1)}, u32[]{:S(2)}, u32[]{:S(2)}) %collective-permute-start.20) | collective-permute-done | bytes 360480 | tf_op jit(solution)/shard_map/ppermute | solution.py:206
  81.5 3.4 %collective-permute-start.25 = (bf16[352,512]{1,0:T(8,128)(2,1)S(1)}, bf16[352,512]{1,0:T(8,128)(2,1)S(1)}, u32[]{:S(2)}, u32[]{:S(2)}) collective-permute-start(bf16[352,512]{1,0:T(8,128)(2,1)S(1)} %collective-permute-done.20.refs_1_), channel_id=1, source_target_pairs={{0,28},{4,0},{8,4},{12,8},{16,12},{20,16},{24,20},{28,24},{1,29},{... | collective-permute-start | bytes 1081352 | tf_op jit(solution)/shard_map/ppermute | solution.py:206
  84.9 0.9 collective-permute-start.7
  85.8 1.3 collective-permute-start.15
  87.1 2.9 %collective-permute-done.25.refs_7_ = bf16[352,512]{1,0:T(8,128)(2,1)S(1)} collective-permute-done((bf16[352,512]{1,0:T(8,128)(2,1)S(1)}, bf16[352,512]{1,0:T(8,128)(2,1)S(1)}, u32[]{:S(2)}, u32[]{:S(2)}) %collective-permute-start.25) | collective-permute-done | bytes 360480 | tf_op jit(solution)/shard_map/ppermute | solution.py:206
  90.0 2.4 %collective-permute-start.28 = (bf16[512,1024]{1,0:T(8,128)(2,1)S(1)}, bf16[512,1024]{1,0:T(8,128)(2,1)S(1)}, u32[]{:S(2)}, u32[]{:S(2)}) collective-permute-start(bf16[512,1024]{1,0:T(8,128)(2,1)S(1)} %collective-permute-done.13.refs_18_.refs_24_.refs_27_), channel_id=1, source_target_pairs={{0,192},{64,0},{128,64},{192,128},{1,193},{65,1},{129,65},{193,129... | collective-permute-start | bytes 3145736 | tf_op jit(solution)/shard_map/ppermute | solution.py:206
  92.5 8.8 %collective-permute-done.7.refs_8_.refs_14_.refs_17_.refs_23_ = bf16[704,512]{1,0:T(8,128)(2,1)S(1)} collective-permute-done((bf16[704,512]{1,0:T(8,128)(2,1)S(1)}, bf16[704,512]{1,0:T(8,128)(2,1)S(1)}, u32[]{:S(2)}, u32[]{:S(2)}) %collective-permute-start.7) | collective-permute-done | bytes 720928 | tf_op jit(solution)/shard_map/ppermute | solution.py:233
  101.3 0.6 collective-permute-start.22
  101.9 2.8 %collective-permute-done.27.refs_28_ = bf16[512,1024]{1,0:T(8,128)(2,1)S(1)} collective-permute-done((bf16[512,1024]{1,0:T(8,128)(2,1)S(1)}, bf16[512,1024]{1,0:T(8,128)(2,1)S(1)}, u32[]{:S(2)}, u32[]{:S(2)}) %collective-permute-start.27) | collective-permute-done | bytes 1048608 | tf_op jit(solution)/shard_map/ppermute | solution.py:203
  104.8 3.4 %collective-permute-start.19 = (bf16[576,512]{1,0:T(8,128)(2,1)S(1)}, bf16[576,512]{1,0:T(8,128)(2,1)S(1)}, u32[]{:S(2)}, u32[]{:S(2)}) collective-permute-start(bf16[576,512]{1,0:T(8,128)(2,1)S(1)} %collective-permute-done.4.refs_6_.refs_15_), channel_id=1, source_target_pairs={{0,28},{4,0},{8,4},{12,8},{16,12},{20,16},{24,20},{28,24},{1,29},{... | collective-permute-start | bytes 1769480 | tf_op jit(solution)/shard_map/ppermute | solution.py:206
  108.2 19.1 %collective-permute-done.15.refs_20_.refs_26_.refs_31_ = bf16[512,1024]{1,0:T(8,128)(2,1)S(1)} collective-permute-done((bf16[512,1024]{1,0:T(8,128)(2,1)S(1)}, bf16[512,1024]{1,0:T(8,128)(2,1)S(1)}, u32[]{:S(2)}, u32[]{:S(2)}) %collective-permute-start.15) | collective-permute-done | bytes 1048608 | tf_op jit(solution)/shard_map/ppermute | solution.py:203
  127.2 0.8 collective-permute-start.26
  128.0 10.1 %shard_map.28.total_ref = f32[2,1280,512]{2,1,0:T(8,128)S(1)} custom-call(bf16[576,512]{1,0:T(8,128)(2,1)S(1)} %slice.3.refs_0_.refs_9_, bf16[352,512]{1,0:T(8,128)(2,1)S(1)} %get-tuple-element.9.refs_1_.refs_10_, bf16[352,512]{1,0:T(8,128)(2,1)S(1)} %get-tuple-element.8.refs_2_.refs_11_, bf16[576,512]{1,0:T(8,128)(2,1)S(1)} %collective-permute-done.refs_3_.refs_12_, ...), custom_call_target="tpu_custom_call" | custom-call | flops 4026531840 | bytes 13631488 | tf_op jit(solution)/shard_map/pallas_call | solution.py:45
  138.2 3.2 %shard_map.30 = f32[1280,512]{1,0:T(8,128)S(1)} custom-call(f32[2,1280,512]{2,1,0:T(8,128)S(1)} %shard_map.28.total_ref, bf16[576,512]{1,0:T(8,128)(2,1)S(1)} %collective-permute-done.19.refs_0_, bf16[352,512]{1,0:T(8,128)(2,1)S(1)} %collective-permute-done.20.refs_1_, bf16[704,512]{1,0:T(8,128)(2,1)S(1)} %collective-permute-done.22.refs_2_.refs_5_, ...), custom_call_target="tpu_custom_call" | custom-call | flops 2684354560 | bytes 9961472 | tf_op jit(solution)/shard_map/pallas_call | solution.py:45
  141.4 3.8 %collective-permute-start.29 = (f32[1280,512]{1,0:T(8,128)S(1)}, f32[1280,512]{1,0:T(8,128)S(1)}, u32[]{:S(2)}, u32[]{:S(2)}) collective-permute-start(f32[1280,512]{1,0:T(8,128)S(1)} %shard_map.30), channel_id=1, source_target_pairs={{0,2},{2,0},{1,3},{3,1},{4,6},{6,4},{5,7},{7,5},{8,10},{10,8},{9,1... | collective-permute-start | bytes 7864328 | tf_op jit(solution)/shard_map/ppermute | solution.py:269
  145.1 3.3 %shard_map.29 = f32[1280,512]{1,0:T(8,128)S(1)} custom-call(f32[2,1280,512]{2,1,0:T(8,128)S(1)} %shard_map.28.total_ref, bf16[576,512]{1,0:T(8,128)(2,1)S(1)} %collective-permute-done.19.refs_0_, bf16[352,512]{1,0:T(8,128)(2,1)S(1)} %collective-permute-done.20.refs_1_, bf16[704,512]{1,0:T(8,128)(2,1)S(1)} %collective-permute-done.22.refs_2_.refs_5_, ...), custom_call_target="tpu_custom_call" | custom-call | flops 2684354560 | bytes 9961472 | tf_op jit(solution)/shard_map/pallas_call | solution.py:45
  148.5 1.2 collective-permute-done.29
  149.7 1.5 add_convert_fusion
  (25 shorter events, 0.2 us)
Async XLA Ops:
  1.1 14.6 %collective-permute-start.2 = (bf16[352,512]{1,0:T(8,128)(2,1)S(1)}, bf16[352,512]{1,0:T(8,128)(2,1)S(1)}, u32[]{:S(2)}, u32[]{:S(2)}) collective-permute-start(bf16[352,512]{1,0:T(8,128)(2,1)S(1)} %get-tuple-element.9.refs_1_.refs_10_), channel_id=1, source_target_pairs={{0,4},{4,8},{8,12},{12,16},{16,20},{20,24},{24,28},{28,0},{1,5},{5... | collective-permute-start | bytes 1081352 | tf_op jit(solution)/shard_map/ppermute | solution.py:203
  5.1 16.3 %collective-permute-start.11 = (bf16[512,512]{1,0:T(8,128)(2,1)S(1)}, bf16[512,512]{1,0:T(8,128)(2,1)S(1)}, u32[]{:S(2)}, u32[]{:S(2)}) collective-permute-start(bf16[512,512]{1,0:T(8,128)(2,1)S(1)} %get-tuple-element.7), channel_id=1, source_target_pairs={{0,35},{1,34},{2,33},{3,32},{32,3},{33,2},{34,1},{35,0},{4,39},{5,... | collective-permute-start | bytes 1572872 | tf_op jit(solution)/shard_map/ppermute | solution.py:241
  8.5 11.6 %collective-permute-start.1 = (bf16[352,512]{1,0:T(8,128)(2,1)S(1)}, bf16[352,512]{1,0:T(8,128)(2,1)S(1)}, u32[]{:S(2)}, u32[]{:S(2)}) collective-permute-start(bf16[352,512]{1,0:T(8,128)(2,1)S(1)} %get-tuple-element.9.refs_1_.refs_10_), channel_id=1, source_target_pairs={{0,28},{4,0},{8,4},{12,8},{16,12},{20,16},{24,20},{28,24},{1,29},{... | collective-permute-start | bytes 1081352 | tf_op jit(solution)/shard_map/ppermute | solution.py:206
  12.2 15.4 %collective-permute-start.18 = (bf16[512,512]{1,0:T(8,128)(2,1)S(1)}, bf16[512,512]{1,0:T(8,128)(2,1)S(1)}, u32[]{:S(2)}, u32[]{:S(2)}) collective-permute-start(bf16[512,512]{1,0:T(8,128)(2,1)S(1)} %get-tuple-element.5), channel_id=1, source_target_pairs={{0,66},{2,64},{64,130},{66,128},{128,194},{130,192},{192,2},{194,0... | collective-permute-start | bytes 1572872 | tf_op jit(solution)/shard_map/ppermute | solution.py:212
  13.6 14.5 %collective-permute-start.17 = (bf16[512,512]{1,0:T(8,128)(2,1)S(1)}, bf16[512,512]{1,0:T(8,128)(2,1)S(1)}, u32[]{:S(2)}, u32[]{:S(2)}) collective-permute-start(bf16[512,512]{1,0:T(8,128)(2,1)S(1)} %get-tuple-element.5), channel_id=1, source_target_pairs={{0,194},{2,192},{64,2},{66,0},{128,66},{130,64},{192,130},{194,128... | collective-permute-start | bytes 1572872 | tf_op jit(solution)/shard_map/ppermute | solution.py:212
  15.7 13.5 %collective-permute-start.16 = (bf16[512,512]{1,0:T(8,128)(2,1)S(1)}, bf16[512,512]{1,0:T(8,128)(2,1)S(1)}, u32[]{:S(2)}, u32[]{:S(2)}) collective-permute-start(bf16[512,512]{1,0:T(8,128)(2,1)S(1)} %get-tuple-element.5), channel_id=1, source_target_pairs={{0,2},{2,0},{1,3},{3,1},{4,6},{6,4},{5,7},{7,5},{8,10},{10,8},{9,1... | collective-permute-start | bytes 1572872 | tf_op jit(solution)/shard_map/ppermute | solution.py:242
  20.2 18.0 %collective-permute-start.14 = (bf16[512,512]{1,0:T(8,128)(2,1)S(1)}, bf16[512,512]{1,0:T(8,128)(2,1)S(1)}, u32[]{:S(2)}, u32[]{:S(2)}) collective-permute-start(bf16[512,512]{1,0:T(8,128)(2,1)S(1)} %get-tuple-element.6.refs_15_.refs_24_), channel_id=1, source_target_pairs={{0,64},{64,128},{128,192},{192,0},{1,65},{65,129},{129,193},{193,1... | collective-permute-start | bytes 1572872 | tf_op jit(solution)/shard_map/ppermute | solution.py:203
  21.5 18.4 %collective-permute-start.12 = (bf16[512,512]{1,0:T(8,128)(2,1)S(1)}, bf16[512,512]{1,0:T(8,128)(2,1)S(1)}, u32[]{:S(2)}, u32[]{:S(2)}) collective-permute-start(bf16[512,512]{1,0:T(8,128)(2,1)S(1)} %get-tuple-element.6.refs_15_.refs_24_), channel_id=1, source_target_pairs={{0,192},{64,0},{128,64},{192,128},{1,193},{65,1},{129,65},{193,129... | collective-permute-start | bytes 1572872 | tf_op jit(solution)/shard_map/ppermute | solution.py:206
  27.7 13.8 %collective-permute-start.10 = (bf16[512,512]{1,0:T(8,128)(2,1)S(1)}, bf16[512,512]{1,0:T(8,128)(2,1)S(1)}, u32[]{:S(2)}, u32[]{:S(2)}) collective-permute-start(bf16[512,512]{1,0:T(8,128)(2,1)S(1)} %get-tuple-element.6.refs_15_.refs_24_), channel_id=1, source_target_pairs={{0,32},{32,0},{1,33},{33,1},{2,34},{34,2},{3,35},{35,3},{4,36},{36... | collective-permute-start | bytes 1572872 | tf_op jit(solution)/shard_map/ppermute | solution.py:240
  28.1 12.6 %collective-permute-start.6 = (bf16[352,512]{1,0:T(8,128)(2,1)S(1)}, bf16[352,512]{1,0:T(8,128)(2,1)S(1)}, u32[]{:S(2)}, u32[]{:S(2)}) collective-permute-start(bf16[352,512]{1,0:T(8,128)(2,1)S(1)} %collective-permute-done.2.refs_10_.refs_19_), channel_id=1, source_target_pairs={{0,4},{4,8},{8,12},{12,16},{16,20},{20,24},{24,28},{28,0},{1,5},{5... | collective-permute-start | bytes 1081352 | tf_op jit(solution)/shard_map/ppermute | solution.py:203
  29.2 22.9 %collective-permute-start.8 = (bf16[576,512]{1,0:T(8,128)(2,1)S(1)}, bf16[576,512]{1,0:T(8,128)(2,1)S(1)}, u32[]{:S(2)}, u32[]{:S(2)}) collective-permute-start(bf16[576,512]{1,0:T(8,128)(2,1)S(1)} %slice.3.refs_0_.refs_9_), channel_id=1, source_target_pairs={{0,4},{4,8},{8,12},{12,16},{16,20},{20,24},{24,28},{28,0},{1,5},{5... | collective-permute-start | bytes 1769480 | tf_op jit(solution)/shard_map/ppermute | solution.py:203
  38.2 16.1 %collective-permute-start = (bf16[576,512]{1,0:T(8,128)(2,1)S(1)}, bf16[576,512]{1,0:T(8,128)(2,1)S(1)}, u32[]{:S(2)}, u32[]{:S(2)}) collective-permute-start(bf16[576,512]{1,0:T(8,128)(2,1)S(1)} %slice.3.refs_0_.refs_9_), channel_id=1, source_target_pairs={{0,28},{4,0},{8,4},{12,8},{16,12},{20,16},{24,20},{28,24},{1,29},{... | collective-permute-start | bytes 1769480 | tf_op jit(solution)/shard_map/ppermute | solution.py:206
  39.9 20.0 %collective-permute-start.5 = (bf16[352,512]{1,0:T(8,128)(2,1)S(1)}, bf16[352,512]{1,0:T(8,128)(2,1)S(1)}, u32[]{:S(2)}, u32[]{:S(2)}) collective-permute-start(bf16[352,512]{1,0:T(8,128)(2,1)S(1)} %collective-permute-done.1.refs_4_.refs_13_), channel_id=1, source_target_pairs={{0,28},{4,0},{8,4},{12,8},{16,12},{20,16},{24,20},{28,24},{1,29},{... | collective-permute-start | bytes 1081352 | tf_op jit(solution)/shard_map/ppermute | solution.py:206
  40.6 22.2 %collective-permute-start.21 = (bf16[352,512]{1,0:T(8,128)(2,1)S(1)}, bf16[352,512]{1,0:T(8,128)(2,1)S(1)}, u32[]{:S(2)}, u32[]{:S(2)}) collective-permute-start(bf16[352,512]{1,0:T(8,128)(2,1)S(1)} %collective-permute-done.6.refs_13_.refs_22_), channel_id=1, source_target_pairs={{0,4},{4,8},{8,12},{12,16},{16,20},{20,24},{24,28},{28,0},{1,5},{5... | collective-permute-start | bytes 1081352 | tf_op jit(solution)/shard_map/ppermute | solution.py:203
  41.5 40.0 %collective-permute-start.3 = (bf16[704,512]{1,0:T(8,128)(2,1)S(1)}, bf16[704,512]{1,0:T(8,128)(2,1)S(1)}, u32[]{:S(2)}, u32[]{:S(2)}) collective-permute-start(bf16[704,512]{1,0:T(8,128)(2,1)S(1)} %pad_maximum_fusion.1), channel_id=1, source_target_pairs={{0,1},{1,0},{2,3},{3,2},{4,5},{5,4},{6,7},{7,6},{8,9},{9,8},{10,11... | collective-permute-start | bytes 2162696 | tf_op jit(solution)/shard_map/ppermute | solution.py:233
  52.1 37.9 %collective-permute-start.13 = (bf16[512,1024]{1,0:T(8,128)(2,1)S(1)}, bf16[512,1024]{1,0:T(8,128)(2,1)S(1)}, u32[]{:S(2)}, u32[]{:S(2)}) collective-permute-start(bf16[512,1024]{1,0:T(8,128)(2,1)S(1)} %constant_dynamic-update-slice_fusion.refs_16_.refs_22_.refs_25_), channel_id=1, source_target_pairs={{0,192},{64,0},{128,64},{192,128},{1,193},{65,1},{129,65},{193,129... | collective-permute-start | bytes 3145736 | tf_op jit(solution)/shard_map/ppermute | solution.py:206
  54.2 30.7 %collective-permute-start.9 = (bf16[576,512]{1,0:T(8,128)(2,1)S(1)}, bf16[576,512]{1,0:T(8,128)(2,1)S(1)}, u32[]{:S(2)}, u32[]{:S(2)}) collective-permute-start(bf16[576,512]{1,0:T(8,128)(2,1)S(1)} %collective-permute-done.8.refs_9_.refs_18_), channel_id=1, source_target_pairs={{0,4},{4,8},{8,12},{12,16},{16,20},{20,24},{24,28},{28,0},{1,5},{5... | collective-permute-start | bytes 1769480 | tf_op jit(solution)/shard_map/ppermute | solution.py:203
  59.9 26.0 %collective-permute-start.4 = (bf16[576,512]{1,0:T(8,128)(2,1)S(1)}, bf16[576,512]{1,0:T(8,128)(2,1)S(1)}, u32[]{:S(2)}, u32[]{:S(2)}) collective-permute-start(bf16[576,512]{1,0:T(8,128)(2,1)S(1)} %collective-permute-done.refs_3_.refs_12_), channel_id=1, source_target_pairs={{0,28},{4,0},{8,4},{12,8},{16,12},{20,16},{24,20},{28,24},{1,29},{... | collective-permute-start | bytes 1769480 | tf_op jit(solution)/shard_map/ppermute | solution.py:206
  62.8 18.6 %collective-permute-start.20 = (bf16[352,512]{1,0:T(8,128)(2,1)S(1)}, bf16[352,512]{1,0:T(8,128)(2,1)S(1)}, u32[]{:S(2)}, u32[]{:S(2)}) collective-permute-start(bf16[352,512]{1,0:T(8,128)(2,1)S(1)} %collective-permute-done.5.refs_7_.refs_16_), channel_id=1, source_target_pairs={{0,28},{4,0},{8,4},{12,8},{16,12},{20,16},{24,20},{28,24},{1,29},{... | collective-permute-start | bytes 1081352 | tf_op jit(solution)/shard_map/ppermute | solution.py:206
  81.4 23.3 %collective-permute-start.27 = (bf16[512,1024]{1,0:T(8,128)(2,1)S(1)}, bf16[512,1024]{1,0:T(8,128)(2,1)S(1)}, u32[]{:S(2)}, u32[]{:S(2)}) collective-permute-start(bf16[512,1024]{1,0:T(8,128)(2,1)S(1)} %pad_maximum_fusion), channel_id=1, source_target_pairs={{0,64},{64,128},{128,192},{192,0},{1,65},{65,129},{129,193},{193,1... | collective-permute-start | bytes 3145736 | tf_op jit(solution)/shard_map/ppermute | solution.py:203
  81.5 8.6 %collective-permute-start.25 = (bf16[352,512]{1,0:T(8,128)(2,1)S(1)}, bf16[352,512]{1,0:T(8,128)(2,1)S(1)}, u32[]{:S(2)}, u32[]{:S(2)}) collective-permute-start(bf16[352,512]{1,0:T(8,128)(2,1)S(1)} %collective-permute-done.20.refs_1_), channel_id=1, source_target_pairs={{0,28},{4,0},{8,4},{12,8},{16,12},{20,16},{24,20},{28,24},{1,29},{... | collective-permute-start | bytes 1081352 | tf_op jit(solution)/shard_map/ppermute | solution.py:206
  84.9 16.4 %collective-permute-start.7 = (bf16[704,512]{1,0:T(8,128)(2,1)S(1)}, bf16[704,512]{1,0:T(8,128)(2,1)S(1)}, u32[]{:S(2)}, u32[]{:S(2)}) collective-permute-start(bf16[704,512]{1,0:T(8,128)(2,1)S(1)} %pad_maximum_fusion.2), channel_id=1, source_target_pairs={{0,1},{1,0},{2,3},{3,2},{4,5},{5,4},{6,7},{7,6},{8,9},{9,8},{10,11... | collective-permute-start | bytes 2162696 | tf_op jit(solution)/shard_map/ppermute | solution.py:233
  85.8 41.4 %collective-permute-start.15 = (bf16[512,1024]{1,0:T(8,128)(2,1)S(1)}, bf16[512,1024]{1,0:T(8,128)(2,1)S(1)}, u32[]{:S(2)}, u32[]{:S(2)}) collective-permute-start(bf16[512,1024]{1,0:T(8,128)(2,1)S(1)} %constant_dynamic-update-slice_fusion.refs_16_.refs_22_.refs_25_), channel_id=1, source_target_pairs={{0,64},{64,128},{128,192},{192,0},{1,65},{65,129},{129,193},{193,1... | collective-permute-start | bytes 3145736 | tf_op jit(solution)/shard_map/ppermute | solution.py:203
  90.0 18.2 %collective-permute-start.23 = (bf16[576,512]{1,0:T(8,128)(2,1)S(1)}, bf16[576,512]{1,0:T(8,128)(2,1)S(1)}, u32[]{:S(2)}, u32[]{:S(2)}) collective-permute-start(bf16[576,512]{1,0:T(8,128)(2,1)S(1)} %collective-permute-done.9.refs_12_.refs_21_), channel_id=1, source_target_pairs={{0,4},{4,8},{8,12},{12,16},{16,20},{20,24},{24,28},{28,0},{1,5},{5... | collective-permute-start | bytes 1769480 | tf_op jit(solution)/shard_map/ppermute | solution.py:203
  90.0 48.1 %collective-permute-start.28 = (bf16[512,1024]{1,0:T(8,128)(2,1)S(1)}, bf16[512,1024]{1,0:T(8,128)(2,1)S(1)}, u32[]{:S(2)}, u32[]{:S(2)}) collective-permute-start(bf16[512,1024]{1,0:T(8,128)(2,1)S(1)} %collective-permute-done.13.refs_18_.refs_24_.refs_27_), channel_id=1, source_target_pairs={{0,192},{64,0},{128,64},{192,128},{1,193},{65,1},{129,65},{193,129... | collective-permute-start | bytes 3145736 | tf_op jit(solution)/shard_map/ppermute | solution.py:206
  101.3 36.8 %collective-permute-start.22 = (bf16[704,512]{1,0:T(8,128)(2,1)S(1)}, bf16[704,512]{1,0:T(8,128)(2,1)S(1)}, u32[]{:S(2)}, u32[]{:S(2)}) collective-permute-start(bf16[704,512]{1,0:T(8,128)(2,1)S(1)} %pad_maximum_fusion.3), channel_id=1, source_target_pairs={{0,1},{1,0},{2,3},{3,2},{4,5},{5,4},{6,7},{7,6},{8,9},{9,8},{10,11... | collective-permute-start | bytes 2162696 | tf_op jit(solution)/shard_map/ppermute | solution.py:233
  104.8 33.4 %collective-permute-start.19 = (bf16[576,512]{1,0:T(8,128)(2,1)S(1)}, bf16[576,512]{1,0:T(8,128)(2,1)S(1)}, u32[]{:S(2)}, u32[]{:S(2)}) collective-permute-start(bf16[576,512]{1,0:T(8,128)(2,1)S(1)} %collective-permute-done.4.refs_6_.refs_15_), channel_id=1, source_target_pairs={{0,28},{4,0},{8,4},{12,8},{16,12},{20,16},{24,20},{28,24},{1,29},{... | collective-permute-start | bytes 1769480 | tf_op jit(solution)/shard_map/ppermute | solution.py:206
  108.2 30.0 %collective-permute-start.24 = (bf16[576,512]{1,0:T(8,128)(2,1)S(1)}, bf16[576,512]{1,0:T(8,128)(2,1)S(1)}, u32[]{:S(2)}, u32[]{:S(2)}) collective-permute-start(bf16[576,512]{1,0:T(8,128)(2,1)S(1)} %collective-permute-done.23.refs_3_), channel_id=1, source_target_pairs={{0,4},{4,8},{8,12},{12,16},{16,20},{20,24},{24,28},{28,0},{1,5},{5... | collective-permute-start | bytes 1769480 | tf_op jit(solution)/shard_map/ppermute | solution.py:203
  127.2 10.9 %collective-permute-start.26 = (bf16[352,512]{1,0:T(8,128)(2,1)S(1)}, bf16[352,512]{1,0:T(8,128)(2,1)S(1)}, u32[]{:S(2)}, u32[]{:S(2)}) collective-permute-start(bf16[352,512]{1,0:T(8,128)(2,1)S(1)} %collective-permute-done.25.refs_7_), channel_id=1, source_target_pairs={{0,1},{1,0},{2,3},{3,2},{4,5},{5,4},{6,7},{7,6},{8,9},{9,8},{10,11... | collective-permute-start | bytes 1081352 | tf_op jit(solution)/shard_map/ppermute | solution.py:235
  141.4 8.3 %collective-permute-start.29 = (f32[1280,512]{1,0:T(8,128)S(1)}, f32[1280,512]{1,0:T(8,128)S(1)}, u32[]{:S(2)}, u32[]{:S(2)}) collective-permute-start(f32[1280,512]{1,0:T(8,128)S(1)} %shard_map.30), channel_id=1, source_target_pairs={{0,2},{2,0},{1,3},{3,1},{4,6},{6,4},{5,7},{7,5},{8,10},{10,8},{9,1... | collective-permute-start | bytes 7864328 | tf_op jit(solution)/shard_map/ppermute | solution.py:269
where the time goes:
time: 151 us
  waiting for transfers between devices  85.6 us (57%)
  starting transfers between devices  43.2 us (29%)
  Pallas kernels  16.6 us (11%)
  local copies, waits for them, and re-layouts  3.84 us (3%)
  other arithmetic  1.78 us (1%)
    ppermute x10, waiting for transfers between devices, up(): return lax.ppermute(a, axis, ring(lax.axis_size(axis), 1))  41.2 us
    ppermute x10, waiting for transfers between devices, down(): return lax.ppermute(a, axis, ring(lax.axis_size(axis), -1))  30.2 us
    ppermute x10, starting transfers between devices, down(): return lax.ppermute(a, axis, ring(lax.axis_size(axis), -1))  22.9 us
    pallas_call x3, Pallas kernels, call(): pl.pallas_call(kernel, out_shape=jax.ShapeDtypeStruct(out_shape, jnp.floa...  16.6 us
    ppermute x3, waiting for transfers between devices, per_device(): pair = lax.ppermute(jnp.concatenate([b[-d], b[d]], 0), 'xh', ring(2, 1))  8.85 us
    ppermute x10, starting transfers between devices, up(): return lax.ppermute(a, axis, ring(lax.axis_size(axis), 1))  5.96 us
    ppermute x2, waiting for transfers between devices, crossed(): return lax.ppermute(a, ('y', 'core'), pairs)  4.11 us
    ppermute x1, starting transfers between devices, per_device(): swapped = lax.ppermute(rest[1](), 'core', ring(2, 1))  3.79 us
  transfers between devices with their start and end apart: 30, of which 14 were waited for; matrix products, arithmetic and copies ran while one was open for 2% of the time, Pallas kernels for 9%

commit v1 on v0

--- a/solution.py
+++ b/solution.py
@@ -11,7 +11,8 @@
 
 AXES = ("y", "xl", "z", "core", "xh")
 NEAR = (0, 1, 2, -1, -2)
-LATE = (3, -3, 4)
+MIDDLE = (3, -3)
+LATE = (4,)
 
 
 def ring(size, shift):
@@ -38,7 +39,7 @@
     )
 
 
-def call(kernel, out_shape, blocks, tokens, weights, extra, scratch):
+def call(kernel, out_shape, blocks, tokens, weights, extra, scratch, aliases):
     rows, width = out_shape[-2:]
     depth = weights[0].shape[0]
     parts = [part for block in tokens for part, _ in block]
@@ -47,6 +48,7 @@
         out_shape=jax.ShapeDtypeStruct(out_shape, jnp.float32),
         in_specs=[VMEM] * (len(extra) + len(parts)) + [ANYWHERE] * len(weights),
         out_specs=VMEM,
+        input_output_aliases=aliases,
         scratch_shapes=[pltpu.VMEM((2, depth, width), jnp.bfloat16), pltpu.SemaphoreType.DMA((2,))]
         + scratch,
         compiler_params=pltpu.CompilerParams(vmem_limit_bytes=8 * 1024 * 1024),
@@ -58,14 +60,15 @@
     )(*extra, *parts, *weights)
 
 
-def early_product(tokens, near_weights, rows, nb, zn, yn):
+def early_product(order, total, tokens, near_weights, rows, nb, zn, yn):
     width = near_weights[0][0][0].shape[1]
     arrays = [w for half in near_weights for w, _ in half]
     known = (0, 1, 2, 3, 2 * yn - 2, 2 * yn - 1)
+    totals = [] if total is None else [total]
 
     def kernel(*refs):
-        parts, w_refs = refs[: 3 * len(NEAR)], refs[3 * len(NEAR) : -3]
-        out_ref, w_buf, sem = refs[-3:]
+        refs, (out_ref, w_buf, sem) = refs[len(totals) : -3], refs[-3:]
+        parts, w_refs = refs[: 3 * len(order)], refs[3 * len(order) :]
         at = places(rows, nb)
 
         def copy(half, i, slot):
@@ -84,12 +87,13 @@
                         copy(half, i, slot).start()
 
         def both(turn, carry):
-            out_ref[turn] = jnp.zeros((rows, width), jnp.float32)
-            start(turn, NEAR[0], 0)
-            for j, d in enumerate(NEAR):
+            if total is None:
+                out_ref[turn] = jnp.zeros((rows, width), jnp.float32)
+            start(turn, order[0], 0)
+            for j, d in enumerate(order):
                 slot = j % 2
-                if j + 1 < len(NEAR):
-                    start(turn, NEAR[j + 1], 1 - slot)
+                if j + 1 < len(order):
+                    start(turn, order[j + 1], 1 - slot)
 
                 @pl.when(meets(d, zn, yn)[0] != yn // 2)
                 def _():
@@ -105,7 +109,9 @@
 
         lax.fori_loop(0, 2, both, 0)
 
-    return call(kernel, (2, rows, width), 6, tokens, arrays, [], [])
+    blocks = 2 * len(order)
+    aliases = {i: 0 for i in range(len(totals))}
+    return call(kernel, (2, rows, width), blocks, tokens, arrays, totals, [], aliases)
 
 
 def final_product(half, total, late_tokens, near_tokens, weights, rows, nb, zn, yn):
@@ -141,7 +147,7 @@
 
         start_weight(meets(LATE[0], zn, yn)[1], 0, True)
         found, side = jnp.int32(0), [jnp.int32(0)] * 2
-        for j, d in enumerate(NEAR):
+        for j, d in enumerate(NEAR + MIDDLE):
             across, index = meets(d, zn, yn)
             for slot in range(2):
                 here = jnp.logical_and(across == yn // 2, found == slot)
@@ -189,14 +195,14 @@
 
     scratch = [pltpu.VMEM((2, rows, depth), jnp.bfloat16), pltpu.SemaphoreType.DMA((2, 3))]
     arrays = [w for w, _ in weights]
-    return call(kernel, (rows, width), 4, tokens, arrays, [total], scratch)
+    return call(kernel, (rows, width), 3, tokens, arrays, [total], scratch, {})
 
 
 def per_device(tokens, up_weight):
     _, _, _, core, xh = (lax.axis_index(axis) for axis in AXES)
     zn, yn = lax.axis_size("z"), lax.axis_size("y")
     rows, depth = tokens.shape
-    nb = 11 * rows // 40
+    nb = rows // 4
     width = up_weight.shape[1] // 2
 
     def up(axis, a):
@@ -249,7 +255,7 @@
     def block(d):
         return [(a[d], 0), (b[d], 0), c[d]]
 
-    near, late = [block(d) for d in NEAR], [block(d) for d in LATE]
+    near, middle, late = ([block(d) for d in order] for order in (NEAR, MIDDLE, LATE))
 
     def weights(half, distances):
         listed = []
@@ -259,10 +265,12 @@
         return listed
 
     sizes = (rows, nb, zn, yn)
-    total = early_product(near, [weights(half, (0, 1, -1)) for half in range(2)], *sizes)
+    near_weights = [weights(half, (0, 1, -1)) for half in range(2)]
+    total = early_product(NEAR, None, near, near_weights, *sizes)
+    total = early_product(MIDDLE, total, middle, near_weights, *sizes)
     rest = [
         functools.partial(
-            final_product, half, total, late, near, weights(half, (0, 1, 2, -1)), *sizes
+            final_product, half, total, late, near + middle, weights(half, (0, 1, 2, -1)), *sizes
         )
         for half in range(2)
     ]

time: 151 us -> 139 us (0.921)
  waiting for transfers between devices: 85.6 us -> 69.2 us
  starting transfers between devices: 43.2 us -> 46.9 us
    ppermute x10, waiting for transfers between devices: 30.2 us -> 16.3 us  [down(): return lax.ppermute(a, axis, ring(lax.axis_size(axis), -1))]
    ppermute x3, waiting for transfers between devices: 8.85 us -> 0.01 us  [per_device(): pair = lax.ppermute(jnp.concatenate([b[-d], b[d]], 0), 'xh', ring(2, 1))]
    ppermute x2, waiting for transfers between devices: 4.11 us -> 7.86 us  [crossed(): return lax.ppermute(a, ('y', 'core'), pairs)]
    ppermute x2, starting transfers between devices: 2.96 us -> 5.97 us  [crossed(): return lax.ppermute(a, ('y', 'core'), pairs)]
    ppermute x10, starting transfers between devices: 22.9 us -> 25.8 us  [down(): return lax.ppermute(a, axis, ring(lax.axis_size(axis), -1))]
    ppermute x10, waiting for transfers between devices: 41.2 us -> 43.1 us  [up(): return lax.ppermute(a, axis, ring(lax.axis_size(axis), 1))]
    pallas_call x3 -> x4, Pallas kernels: 16.6 us -> 17.6 us  [call(): pl.pallas_call(kernel, out_shape=jax.ShapeDtypeStruct(out_shape, jnp.floa...]
  transfers between devices with their start and end apart: 30 -> 30, of which waited for: 14 -> 12; matrix products, arithmetic and copies ran while one was open for 2% -> 1% of each run, Pallas kernels for 9% -> 11%
where the time goes in v1:
time: 139 us; the launch traced here: 138 us
  waiting for transfers between devices  69.2 us (50%)
  starting transfers between devices  46.9 us (34%)
  Pallas kernels  17.6 us (13%)
  local copies, waits for them, and re-layouts  2.85 us (2%)
  other arithmetic  1.74 us (1%)
    ppermute x10, waiting for transfers between devices, up(): return lax.ppermute(a, axis, ring(lax.axis_size(axis), 1))  43.1 us
    ppermute x10, starting transfers between devices, down(): return lax.ppermute(a, axis, ring(lax.axis_size(axis), -1))  25.8 us
    pallas_call x4, Pallas kernels, call(): pl.pallas_call(kernel, out_shape=jax.ShapeDtypeStruct(out_shape, jnp.floa...  17.6 us
    ppermute x10, waiting for transfers between devices, down(): return lax.ppermute(a, axis, ring(lax.axis_size(axis), -1))  16.3 us
    ppermute x2, waiting for transfers between devices, crossed(): return lax.ppermute(a, ('y', 'core'), pairs)  7.86 us
    ppermute x2, starting transfers between devices, crossed(): return lax.ppermute(a, ('y', 'core'), pairs)  5.97 us
    ppermute x10, starting transfers between devices, up(): return lax.ppermute(a, axis, ring(lax.axis_size(axis), 1))  5.62 us
    ppermute x1, starting transfers between devices, per_device(): lax.ppermute(far, ('xl', 'core', 'xh'), [(i, 7 - i) for i in range(8)])  2.93 us
  transfers between devices with their start and end apart: 30, of which 12 were waited for; matrix products, arithmetic and copies ran while one was open for 1% of the time, Pallas kernels for 11%

profile of v1, /device:TPU:1, one launch (start us, length us, event | category | flops | bytes accessed | tf_op | source)
XLA Modules:
  0.0 138.5 jit_solution(14369837862279366116)
XLA Ops:
  0.0 1.2 constant_dynamic-slice_fusion
  1.2 6.5 %collective-permute-start.1 = (bf16[320,512]{1,0:T(8,128)(2,1)S(1)}, bf16[320,512]{1,0:T(8,128)(2,1)S(1)}, u32[]{:S(2)}, u32[]{:S(2)}) collective-permute-start(bf16[320,512]{1,0:T(8,128)(2,1)S(1)} %get-tuple-element.9.refs_1_.refs_4_), channel_id=1, source_target_pairs={{0,28},{4,0},{8,4},{12,8},{16,12},{20,16},{24,20},{28,24},{1,29},{... | collective-permute-start | bytes 983048 | tf_op jit(solution)/shard_map/ppermute | solution.py:212
  7.7 1.5 %fusion = (bf16[512,512]{1,0:T(8,128)(2,1)S(1)}, bf16[512,512]{1,0:T(8,128)(2,1)S(1)}, bf16[512,512]{1,0:T(8,128)(2,1)S(1)}) fusion(bf16[1024,1024]{1,0:T(8,128)(2,1)} %param.3, s32[]{:T(128)S(6)} %select_n.24, s32[]{:T(128)S(6)} %select_n.23, s32[]{:T(128)S(6)} %select_n.22, s32[]{:T(128)S(6)} %select_n.25), kind=kLoop, calls=%fused_computation.9 | loop fusion | bytes 3145744 | tf_op jit(solution)/shard_map/dynamic_slice | solution.py:221
  9.2 1.3 collective-permute-start.10
  10.5 0.0 collective-permute-start.2
  10.5 2.9 %collective-permute-start.11 = (bf16[512,512]{1,0:T(8,128)(2,1)S(1)}, bf16[512,512]{1,0:T(8,128)(2,1)S(1)}, u32[]{:S(2)}, u32[]{:S(2)}) collective-permute-start(bf16[512,512]{1,0:T(8,128)(2,1)S(1)} %get-tuple-element.7), channel_id=1, source_target_pairs={{0,35},{1,34},{2,33},{3,32},{32,3},{33,2},{34,1},{35,0},{4,39},{5,... | collective-permute-start | bytes 1572872 | tf_op jit(solution)/shard_map/ppermute | solution.py:247
  13.4 2.7 %collective-permute-start.12 = (bf16[512,512]{1,0:T(8,128)(2,1)S(1)}, bf16[512,512]{1,0:T(8,128)(2,1)S(1)}, u32[]{:S(2)}, u32[]{:S(2)}) collective-permute-start(bf16[512,512]{1,0:T(8,128)(2,1)S(1)} %get-tuple-element.6.refs_15_.refs_7_.refs_24_), channel_id=1, source_target_pairs={{0,192},{64,0},{128,64},{192,128},{1,193},{65,1},{129,65},{193,129... | collective-permute-start | bytes 1572872 | tf_op jit(solution)/shard_map/ppermute | solution.py:212
  16.1 0.0 collective-permute-start.14
  16.1 3.6 %collective-permute-done.2.refs_10_.refs_13_ = bf16[320,512]{1,0:T(8,128)(2,1)S(1)} collective-permute-done((bf16[320,512]{1,0:T(8,128)(2,1)S(1)}, bf16[320,512]{1,0:T(8,128)(2,1)S(1)}, u32[]{:S(2)}, u32[]{:S(2)}) %collective-permute-start.2) | collective-permute-done | bytes 327712 | tf_op jit(solution)/shard_map/ppermute | solution.py:209
  19.7 2.1 %collective-permute-start.16 = (bf16[512,512]{1,0:T(8,128)(2,1)S(1)}, bf16[512,512]{1,0:T(8,128)(2,1)S(1)}, u32[]{:S(2)}, u32[]{:S(2)}) collective-permute-start(bf16[512,512]{1,0:T(8,128)(2,1)S(1)} %get-tuple-element.5), channel_id=1, source_target_pairs={{0,2},{2,0},{1,3},{3,1},{4,6},{6,4},{5,7},{7,5},{8,10},{10,8},{9,1... | collective-permute-start | bytes 1572872 | tf_op jit(solution)/shard_map/ppermute | solution.py:248
  21.8 4.4 %collective-permute-start.17 = (bf16[512,512]{1,0:T(8,128)(2,1)S(1)}, bf16[512,512]{1,0:T(8,128)(2,1)S(1)}, u32[]{:S(2)}, u32[]{:S(2)}) collective-permute-start(bf16[512,512]{1,0:T(8,128)(2,1)S(1)} %get-tuple-element.5), channel_id=1, source_target_pairs={{0,194},{2,192},{64,2},{66,0},{128,66},{130,64},{192,130},{194,128... | collective-permute-start | bytes 1572872 | tf_op jit(solution)/shard_map/ppermute | solution.py:218
  26.2 1.6 %collective-permute-start.18 = (bf16[512,512]{1,0:T(8,128)(2,1)S(1)}, bf16[512,512]{1,0:T(8,128)(2,1)S(1)}, u32[]{:S(2)}, u32[]{:S(2)}) collective-permute-start(bf16[512,512]{1,0:T(8,128)(2,1)S(1)} %get-tuple-element.5), channel_id=1, source_target_pairs={{0,66},{2,64},{64,130},{66,128},{128,194},{130,192},{192,2},{194,0... | collective-permute-start | bytes 1572872 | tf_op jit(solution)/shard_map/ppermute | solution.py:218
  27.8 0.0 collective-permute-done.12.refs_17_.refs_9_.refs_26_
  27.9 3.0 %collective-permute-start = (bf16[640,512]{1,0:T(8,128)(2,1)S(1)}, bf16[640,512]{1,0:T(8,128)(2,1)S(1)}, u32[]{:S(2)}, u32[]{:S(2)}) collective-permute-start(bf16[640,512]{1,0:T(8,128)(2,1)S(1)} %slice.3.refs_0_.refs_3_), channel_id=1, source_target_pairs={{0,28},{4,0},{8,4},{12,8},{16,12},{20,16},{24,20},{28,24},{1,29},{... | collective-permute-start | bytes 1966088 | tf_op jit(solution)/shard_map/ppermute | solution.py:212
  30.8 0.4 collective-permute-done.14.refs_19_.refs_11_.refs_30_
  31.3 0.0 collective-permute-done.16.refs_21_.refs_13_.refs_24_
  31.3 0.7 collective-permute-start.3
  32.0 6.9 %collective-permute-done.17.refs_23_.refs_15_.refs_26_ = bf16[512,512]{1,0:T(8,128)(2,1)S(1)} collective-permute-done((bf16[512,512]{1,0:T(8,128)(2,1)S(1)}, bf16[512,512]{1,0:T(8,128)(2,1)S(1)}, u32[]{:S(2)}, u32[]{:S(2)}) %collective-permute-start.17) | collective-permute-done | bytes 524320 | tf_op jit(solution)/shard_map/ppermute | solution.py:218
  38.9 2.7 %collective-permute-start.5 = (bf16[320,512]{1,0:T(8,128)(2,1)S(1)}, bf16[320,512]{1,0:T(8,128)(2,1)S(1)}, u32[]{:S(2)}, u32[]{:S(2)}) collective-permute-start(bf16[320,512]{1,0:T(8,128)(2,1)S(1)} %collective-permute-done.1.refs_4_.refs_7_), channel_id=1, source_target_pairs={{0,28},{4,0},{8,4},{12,8},{16,12},{20,16},{24,20},{28,24},{1,29},{... | collective-permute-start | bytes 983048 | tf_op jit(solution)/shard_map/ppermute | solution.py:212
  41.5 1.0 collective-permute-done.18.refs_25_.refs_17_.refs_30_
  42.5 9.9 %collective-permute-done.5.refs_7_.refs_10_ = bf16[320,512]{1,0:T(8,128)(2,1)S(1)} collective-permute-done((bf16[320,512]{1,0:T(8,128)(2,1)S(1)}, bf16[320,512]{1,0:T(8,128)(2,1)S(1)}, u32[]{:S(2)}, u32[]{:S(2)}) %collective-permute-start.5) | collective-permute-done | bytes 327712 | tf_op jit(solution)/shard_map/ppermute | solution.py:212
  52.4 3.4 %collective-permute-start.20 = (bf16[320,512]{1,0:T(8,128)(2,1)S(1)}, bf16[320,512]{1,0:T(8,128)(2,1)S(1)}, u32[]{:S(2)}, u32[]{:S(2)}) collective-permute-start(bf16[320,512]{1,0:T(8,128)(2,1)S(1)} %collective-permute-done.5.refs_7_.refs_10_), channel_id=1, source_target_pairs={{0,28},{4,0},{8,4},{12,8},{16,12},{20,16},{24,20},{28,24},{1,29},{... | collective-permute-start | bytes 983048 | tf_op jit(solution)/shard_map/ppermute | solution.py:212
  55.8 0.1 constant_dynamic-update-slice_fusion.1
  55.9 0.1 collective-permute-start.4
  56.0 1.4 %collective-permute-start.9 = (bf16[640,512]{1,0:T(8,128)(2,1)S(1)}, bf16[640,512]{1,0:T(8,128)(2,1)S(1)}, u32[]{:S(2)}, u32[]{:S(2)}) collective-permute-start(bf16[640,512]{1,0:T(8,128)(2,1)S(1)} %collective-permute-done.8.refs_9_.refs_12_), channel_id=1, source_target_pairs={{0,4},{4,8},{8,12},{12,16},{16,20},{20,24},{24,28},{28,0},{1,5},{5... | collective-permute-start | bytes 1966088 | tf_op jit(solution)/shard_map/ppermute | solution.py:209
  57.4 0.1 collective-permute-start.21
  57.5 0.1 constant_dynamic-update-slice_fusion.refs_16_.refs_22_.refs_8_.refs_14_.refs_25_
  57.6 3.1 %collective-permute-start.13 = (bf16[512,1024]{1,0:T(8,128)(2,1)S(1)}, bf16[512,1024]{1,0:T(8,128)(2,1)S(1)}, u32[]{:S(2)}, u32[]{:S(2)}) collective-permute-start(bf16[512,1024]{1,0:T(8,128)(2,1)S(1)} %constant_dynamic-update-slice_fusion.refs_16_.refs_22_.refs_8_.refs_14_.refs_25_), channel_id=1, source_target_pairs={{0,192},{64,0},{128,64},{192,128},{1,193},{65,1},{129,65},{193,129... | collective-permute-start | bytes 3145736 | tf_op jit(solution)/shard_map/ppermute | solution.py:212
  60.8 1.7 %collective-permute-done.20.refs_2_.refs_19_ = bf16[320,512]{1,0:T(8,128)(2,1)S(1)} collective-permute-done((bf16[320,512]{1,0:T(8,128)(2,1)S(1)}, bf16[320,512]{1,0:T(8,128)(2,1)S(1)}, u32[]{:S(2)}, u32[]{:S(2)}) %collective-permute-start.20) | collective-permute-done | bytes 327712 | tf_op jit(solution)/shard_map/ppermute | solution.py:212
  62.5 17.6 %collective-permute-done.21.refs_5_.refs_22_ = bf16[320,512]{1,0:T(8,128)(2,1)S(1)} collective-permute-done((bf16[320,512]{1,0:T(8,128)(2,1)S(1)}, bf16[320,512]{1,0:T(8,128)(2,1)S(1)}, u32[]{:S(2)}, u32[]{:S(2)}) %collective-permute-start.21) | collective-permute-done | bytes 327712 | tf_op jit(solution)/shard_map/ppermute | solution.py:209
  80.1 1.3 collective-permute-start.15
  81.4 0.3 collective-permute-start.22
  81.8 2.7 %collective-permute-start.25 = (bf16[320,512]{1,0:T(8,128)(2,1)S(1)}, bf16[320,512]{1,0:T(8,128)(2,1)S(1)}, u32[]{:S(2)}, u32[]{:S(2)}) collective-permute-start(bf16[320,512]{1,0:T(8,128)(2,1)S(1)} %collective-permute-done.20.refs_2_.refs_19_), channel_id=1, source_target_pairs={{0,28},{4,0},{8,4},{12,8},{16,12},{20,16},{24,20},{28,24},{1,29},{... | collective-permute-start | bytes 983048 | tf_op jit(solution)/shard_map/ppermute | solution.py:212
  84.4 0.1 pad_maximum_fusion
  84.6 4.2 %collective-permute-done.25.refs_1_ = bf16[320,512]{1,0:T(8,128)(2,1)S(1)} collective-permute-done((bf16[320,512]{1,0:T(8,128)(2,1)S(1)}, bf16[320,512]{1,0:T(8,128)(2,1)S(1)}, u32[]{:S(2)}, u32[]{:S(2)}) %collective-permute-start.25) | collective-permute-done | bytes 327712 | tf_op jit(solution)/shard_map/ppermute | solution.py:212
  88.7 1.0 collective-permute-start.27
  89.8 1.6 %collective-permute-start.28 = (bf16[512,1024]{1,0:T(8,128)(2,1)S(1)}, bf16[512,1024]{1,0:T(8,128)(2,1)S(1)}, u32[]{:S(2)}, u32[]{:S(2)}) collective-permute-start(bf16[512,1024]{1,0:T(8,128)(2,1)S(1)} %collective-permute-done.13.refs_18_.refs_24_.refs_10_.refs_16_.refs_27_), channel_id=1, source_target_pairs={{0,192},{64,0},{128,64},{192,128},{1,193},{65,1},{129,65},{193,129... | collective-permute-start | bytes 3145736 | tf_op jit(solution)/shard_map/ppermute | solution.py:212
  91.4 13.5 %collective-permute-done.15.refs_20_.refs_26_.refs_12_.refs_18_.refs_31_ = bf16[512,1024]{1,0:T(8,128)(2,1)S(1)} collective-permute-done((bf16[512,1024]{1,0:T(8,128)(2,1)S(1)}, bf16[512,1024]{1,0:T(8,128)(2,1)S(1)}, u32[]{:S(2)}, u32[]{:S(2)}) %collective-permute-start.15) | collective-permute-done | bytes 1048608 | tf_op jit(solution)/shard_map/ppermute | solution.py:209
  105.0 1.7 %collective-permute-start.24 = (bf16[640,512]{1,0:T(8,128)(2,1)S(1)}, bf16[640,512]{1,0:T(8,128)(2,1)S(1)}, u32[]{:S(2)}, u32[]{:S(2)}) collective-permute-start(bf16[640,512]{1,0:T(8,128)(2,1)S(1)} %collective-permute-done.23.refs_4_.refs_21_), channel_id=1, source_target_pairs={{0,4},{4,8},{8,12},{12,16},{16,20},{20,24},{24,28},{28,0},{1,5},{5... | collective-permute-start | bytes 1966088 | tf_op jit(solution)/shard_map/ppermute | solution.py:209
  106.7 10.1 %shard_map.28.refs_0_ = f32[2,1280,512]{2,1,0:T(8,128)S(1)} custom-call(bf16[640,512]{1,0:T(8,128)(2,1)S(1)} %slice.3.refs_0_.refs_3_, bf16[320,512]{1,0:T(8,128)(2,1)S(1)} %get-tuple-element.9.refs_1_.refs_4_, bf16[320,512]{1,0:T(8,128)(2,1)S(1)} %get-tuple-element.8.refs_2_.refs_5_, bf16[640,512]{1,0:T(8,128)(2,1)S(1)} %collective-permute-done.refs_3_.refs_6_, ...), custom_call_target="tpu_custom_call" | custom-call | flops 6710886400 | bytes 20971520 | tf_op jit(solution)/shard_map/pallas_call | solution.py:46
  116.8 0.4 collective-permute-done.19.refs_1_.refs_18_
  117.2 2.2 %shard_map.29.total_ref = f32[2,1280,512]{2,1,0:T(8,128)S(1)} custom-call(f32[2,1280,512]{2,1,0:T(8,128)S(1)} %shard_map.28.refs_0_, bf16[640,512]{1,0:T(8,128)(2,1)S(1)} %collective-permute-done.19.refs_1_.refs_18_, bf16[320,512]{1,0:T(8,128)(2,1)S(1)} %collective-permute-done.20.refs_2_.refs_19_, ...), custom_call_target="tpu_custom_call", output_to_operand_aliasing={{}: (0, {})} | custom-call | flops 2684354560 | bytes 9961472 | tf_op jit(solution)/shard_map/pallas_call | solution.py:46
  119.4 8.0 %collective-permute-done.27.refs_28_ = bf16[512,1024]{1,0:T(8,128)(2,1)S(1)} collective-permute-done((bf16[512,1024]{1,0:T(8,128)(2,1)S(1)}, bf16[512,1024]{1,0:T(8,128)(2,1)S(1)}, u32[]{:S(2)}, u32[]{:S(2)}) %collective-permute-start.27) | collective-permute-done | bytes 1048608 | tf_op jit(solution)/shard_map/ppermute | solution.py:209
  127.4 2.7 %shard_map.31 = f32[1280,512]{1,0:T(8,128)S(1)} custom-call(f32[2,1280,512]{2,1,0:T(8,128)S(1)} %shard_map.29.total_ref, bf16[640,512]{1,0:T(8,128)(2,1)S(1)} %collective-permute-done.24.refs_0_, bf16[320,512]{1,0:T(8,128)(2,1)S(1)} %collective-permute-done.25.refs_1_, bf16[320,512]{1,0:T(8,128)(2,1)S(1)} %collective-permute-done.26.refs_2_, ...), custom_call_target="tpu_custom_call" | custom-call | flops 2013265920 | bytes 8126464 | tf_op jit(solution)/shard_map/pallas_call | solution.py:46
  130.1 2.3 %collective-permute-start.29 = (f32[1280,512]{1,0:T(8,128)S(1)}, f32[1280,512]{1,0:T(8,128)S(1)}, u32[]{:S(2)}, u32[]{:S(2)}) collective-permute-start(f32[1280,512]{1,0:T(8,128)S(1)} %shard_map.31), channel_id=1, source_target_pairs={{0,2},{2,0},{1,3},{3,1},{4,6},{6,4},{5,7},{7,5},{8,10},{10,8},{9,1... | collective-permute-start | bytes 7864328 | tf_op jit(solution)/shard_map/ppermute | solution.py:277
  132.4 2.6 %shard_map.30 = f32[1280,512]{1,0:T(8,128)S(1)} custom-call(f32[2,1280,512]{2,1,0:T(8,128)S(1)} %shard_map.29.total_ref, bf16[640,512]{1,0:T(8,128)(2,1)S(1)} %collective-permute-done.24.refs_0_, bf16[320,512]{1,0:T(8,128)(2,1)S(1)} %collective-permute-done.25.refs_1_, bf16[320,512]{1,0:T(8,128)(2,1)S(1)} %collective-permute-done.26.refs_2_, ...), custom_call_target="tpu_custom_call" | custom-call | flops 2013265920 | bytes 8126464 | tf_op jit(solution)/shard_map/pallas_call | solution.py:46
  135.1 1.9 %collective-permute-done.29 = f32[1280,512]{1,0:T(8,128)S(1)} collective-permute-done((f32[1280,512]{1,0:T(8,128)S(1)}, f32[1280,512]{1,0:T(8,128)S(1)}, u32[]{:S(2)}, u32[]{:S(2)}) %collective-permute-start.29) | collective-permute-done | bytes 2621472 | tf_op jit(solution)/shard_map/ppermute | solution.py:277
  137.0 1.5 %add_convert_fusion = bf16[1280,512]{1,0:T(8,128)(2,1)} fusion(f32[1280,512]{1,0:T(8,128)S(1)} %shard_map.30, f32[1280,512]{1,0:T(8,128)S(1)} %collective-permute-done.29), kind=kLoop, calls=%fused_computation | loop fusion | flops 1310720 | bytes 6553600 | tf_op jit(solution)/shard_map/convert_element_type | solution.py:278
  (28 shorter events, 0.2 us)
Async XLA Ops:
  0.0 27.8 %copy-start = (bf16[1280,512]{1,0:T(8,128)(2,1)S(1)}, bf16[1280,512]{1,0:T(8,128)(2,1)}, u32[]{:S(2)}) copy-start(bf16[1280,512]{1,0:T(8,128)(2,1)} %param.2) | copy-start | bytes 3932164
  1.2 14.9 %collective-permute-start.1 = (bf16[320,512]{1,0:T(8,128)(2,1)S(1)}, bf16[320,512]{1,0:T(8,128)(2,1)S(1)}, u32[]{:S(2)}, u32[]{:S(2)}) collective-permute-start(bf16[320,512]{1,0:T(8,128)(2,1)S(1)} %get-tuple-element.9.refs_1_.refs_4_), channel_id=1, source_target_pairs={{0,28},{4,0},{8,4},{12,8},{16,12},{20,16},{24,20},{28,24},{1,29},{... | collective-permute-start | bytes 983048 | tf_op jit(solution)/shard_map/ppermute | solution.py:212
  9.2 12.6 %collective-permute-start.10 = (bf16[512,512]{1,0:T(8,128)(2,1)S(1)}, bf16[512,512]{1,0:T(8,128)(2,1)S(1)}, u32[]{:S(2)}, u32[]{:S(2)}) collective-permute-start(bf16[512,512]{1,0:T(8,128)(2,1)S(1)} %get-tuple-element.6.refs_15_.refs_7_.refs_24_), channel_id=1, source_target_pairs={{0,32},{32,0},{1,33},{33,1},{2,34},{34,2},{3,35},{35,3},{4,36},{36... | collective-permute-start | bytes 1572872 | tf_op jit(solution)/shard_map/ppermute | solution.py:246
  10.5 9.3 %collective-permute-start.2 = (bf16[320,512]{1,0:T(8,128)(2,1)S(1)}, bf16[320,512]{1,0:T(8,128)(2,1)S(1)}, u32[]{:S(2)}, u32[]{:S(2)}) collective-permute-start(bf16[320,512]{1,0:T(8,128)(2,1)S(1)} %get-tuple-element.9.refs_1_.refs_4_), channel_id=1, source_target_pairs={{0,4},{4,8},{8,12},{12,16},{16,20},{20,24},{24,28},{28,0},{1,5},{5... | collective-permute-start | bytes 983048 | tf_op jit(solution)/shard_map/ppermute | solution.py:209
  10.5 15.7 %collective-permute-start.11 = (bf16[512,512]{1,0:T(8,128)(2,1)S(1)}, bf16[512,512]{1,0:T(8,128)(2,1)S(1)}, u32[]{:S(2)}, u32[]{:S(2)}) collective-permute-start(bf16[512,512]{1,0:T(8,128)(2,1)S(1)} %get-tuple-element.7), channel_id=1, source_target_pairs={{0,35},{1,34},{2,33},{3,32},{32,3},{33,2},{34,1},{35,0},{4,39},{5,... | collective-permute-start | bytes 1572872 | tf_op jit(solution)/shard_map/ppermute | solution.py:247
  13.4 14.5 %collective-permute-start.12 = (bf16[512,512]{1,0:T(8,128)(2,1)S(1)}, bf16[512,512]{1,0:T(8,128)(2,1)S(1)}, u32[]{:S(2)}, u32[]{:S(2)}) collective-permute-start(bf16[512,512]{1,0:T(8,128)(2,1)S(1)} %get-tuple-element.6.refs_15_.refs_7_.refs_24_), channel_id=1, source_target_pairs={{0,192},{64,0},{128,64},{192,128},{1,193},{65,1},{129,65},{193,129... | collective-permute-start | bytes 1572872 | tf_op jit(solution)/shard_map/ppermute | solution.py:212
  16.1 15.1 %collective-permute-start.14 = (bf16[512,512]{1,0:T(8,128)(2,1)S(1)}, bf16[512,512]{1,0:T(8,128)(2,1)S(1)}, u32[]{:S(2)}, u32[]{:S(2)}) collective-permute-start(bf16[512,512]{1,0:T(8,128)(2,1)S(1)} %get-tuple-element.6.refs_15_.refs_7_.refs_24_), channel_id=1, source_target_pairs={{0,64},{64,128},{128,192},{192,0},{1,65},{65,129},{129,193},{193,1... | collective-permute-start | bytes 1572872 | tf_op jit(solution)/shard_map/ppermute | solution.py:209
  19.7 11.6 %collective-permute-start.16 = (bf16[512,512]{1,0:T(8,128)(2,1)S(1)}, bf16[512,512]{1,0:T(8,128)(2,1)S(1)}, u32[]{:S(2)}, u32[]{:S(2)}) collective-permute-start(bf16[512,512]{1,0:T(8,128)(2,1)S(1)} %get-tuple-element.5), channel_id=1, source_target_pairs={{0,2},{2,0},{1,3},{3,1},{4,6},{6,4},{5,7},{7,5},{8,10},{10,8},{9,1... | collective-permute-start | bytes 1572872 | tf_op jit(solution)/shard_map/ppermute | solution.py:248
  21.8 17.1 %collective-permute-start.17 = (bf16[512,512]{1,0:T(8,128)(2,1)S(1)}, bf16[512,512]{1,0:T(8,128)(2,1)S(1)}, u32[]{:S(2)}, u32[]{:S(2)}) collective-permute-start(bf16[512,512]{1,0:T(8,128)(2,1)S(1)} %get-tuple-element.5), channel_id=1, source_target_pairs={{0,194},{2,192},{64,2},{66,0},{128,66},{130,64},{192,130},{194,128... | collective-permute-start | bytes 1572872 | tf_op jit(solution)/shard_map/ppermute | solution.py:218
  26.2 16.3 %collective-permute-start.18 = (bf16[512,512]{1,0:T(8,128)(2,1)S(1)}, bf16[512,512]{1,0:T(8,128)(2,1)S(1)}, u32[]{:S(2)}, u32[]{:S(2)}) collective-permute-start(bf16[512,512]{1,0:T(8,128)(2,1)S(1)} %get-tuple-element.5), channel_id=1, source_target_pairs={{0,66},{2,64},{64,130},{66,128},{128,194},{130,192},{192,2},{194,0... | collective-permute-start | bytes 1572872 | tf_op jit(solution)/shard_map/ppermute | solution.py:218
  27.9 28.0 %collective-permute-start = (bf16[640,512]{1,0:T(8,128)(2,1)S(1)}, bf16[640,512]{1,0:T(8,128)(2,1)S(1)}, u32[]{:S(2)}, u32[]{:S(2)}) collective-permute-start(bf16[640,512]{1,0:T(8,128)(2,1)S(1)} %slice.3.refs_0_.refs_3_), channel_id=1, source_target_pairs={{0,28},{4,0},{8,4},{12,8},{16,12},{20,16},{24,20},{28,24},{1,29},{... | collective-permute-start | bytes 1966088 | tf_op jit(solution)/shard_map/ppermute | solution.py:212
  31.3 24.7 %collective-permute-start.8 = (bf16[640,512]{1,0:T(8,128)(2,1)S(1)}, bf16[640,512]{1,0:T(8,128)(2,1)S(1)}, u32[]{:S(2)}, u32[]{:S(2)}) collective-permute-start(bf16[640,512]{1,0:T(8,128)(2,1)S(1)} %slice.3.refs_0_.refs_3_), channel_id=1, source_target_pairs={{0,4},{4,8},{8,12},{12,16},{16,20},{20,24},{24,28},{28,0},{1,5},{5... | collective-permute-start | bytes 1966088 | tf_op jit(solution)/shard_map/ppermute | solution.py:209
  31.3 26.3 %collective-permute-start.3 = (bf16[640,512]{1,0:T(8,128)(2,1)S(1)}, bf16[640,512]{1,0:T(8,128)(2,1)S(1)}, u32[]{:S(2)}, u32[]{:S(2)}) collective-permute-start(bf16[640,512]{1,0:T(8,128)(2,1)S(1)} %pad_maximum_fusion.1), channel_id=1, source_target_pairs={{0,1},{1,0},{2,3},{3,2},{4,5},{5,4},{6,7},{7,6},{8,9},{9,8},{10,11... | collective-permute-start | bytes 1966088 | tf_op jit(solution)/shard_map/ppermute | solution.py:239
  38.9 13.5 %collective-permute-start.5 = (bf16[320,512]{1,0:T(8,128)(2,1)S(1)}, bf16[320,512]{1,0:T(8,128)(2,1)S(1)}, u32[]{:S(2)}, u32[]{:S(2)}) collective-permute-start(bf16[320,512]{1,0:T(8,128)(2,1)S(1)} %collective-permute-done.1.refs_4_.refs_7_), channel_id=1, source_target_pairs={{0,28},{4,0},{8,4},{12,8},{16,12},{20,16},{24,20},{28,24},{1,29},{... | collective-permute-start | bytes 983048 | tf_op jit(solution)/shard_map/ppermute | solution.py:212
  42.5 14.9 %collective-permute-start.6 = (bf16[320,512]{1,0:T(8,128)(2,1)S(1)}, bf16[320,512]{1,0:T(8,128)(2,1)S(1)}, u32[]{:S(2)}, u32[]{:S(2)}) collective-permute-start(bf16[320,512]{1,0:T(8,128)(2,1)S(1)} %collective-permute-done.2.refs_10_.refs_13_), channel_id=1, source_target_pairs={{0,4},{4,8},{8,12},{12,16},{16,20},{20,24},{24,28},{28,0},{1,5},{5... | collective-permute-start | bytes 983048 | tf_op jit(solution)/shard_map/ppermute | solution.py:209
  52.4 10.1 %collective-permute-start.20 = (bf16[320,512]{1,0:T(8,128)(2,1)S(1)}, bf16[320,512]{1,0:T(8,128)(2,1)S(1)}, u32[]{:S(2)}, u32[]{:S(2)}) collective-permute-start(bf16[320,512]{1,0:T(8,128)(2,1)S(1)} %collective-permute-done.5.refs_7_.refs_10_), channel_id=1, source_target_pairs={{0,28},{4,0},{8,4},{12,8},{16,12},{20,16},{24,20},{28,24},{1,29},{... | collective-permute-start | bytes 983048 | tf_op jit(solution)/shard_map/ppermute | solution.py:212
  55.9 25.5 %collective-permute-start.4 = (bf16[640,512]{1,0:T(8,128)(2,1)S(1)}, bf16[640,512]{1,0:T(8,128)(2,1)S(1)}, u32[]{:S(2)}, u32[]{:S(2)}) collective-permute-start(bf16[640,512]{1,0:T(8,128)(2,1)S(1)} %collective-permute-done.refs_3_.refs_6_), channel_id=1, source_target_pairs={{0,28},{4,0},{8,4},{12,8},{16,12},{20,16},{24,20},{28,24},{1,29},{... | collective-permute-start | bytes 1966088 | tf_op jit(solution)/shard_map/ppermute | solution.py:212
  56.0 25.8 %collective-permute-start.9 = (bf16[640,512]{1,0:T(8,128)(2,1)S(1)}, bf16[640,512]{1,0:T(8,128)(2,1)S(1)}, u32[]{:S(2)}, u32[]{:S(2)}) collective-permute-start(bf16[640,512]{1,0:T(8,128)(2,1)S(1)} %collective-permute-done.8.refs_9_.refs_12_), channel_id=1, source_target_pairs={{0,4},{4,8},{8,12},{12,16},{16,20},{20,24},{24,28},{28,0},{1,5},{5... | collective-permute-start | bytes 1966088 | tf_op jit(solution)/shard_map/ppermute | solution.py:209
  57.4 22.6 %collective-permute-start.21 = (bf16[320,512]{1,0:T(8,128)(2,1)S(1)}, bf16[320,512]{1,0:T(8,128)(2,1)S(1)}, u32[]{:S(2)}, u32[]{:S(2)}) collective-permute-start(bf16[320,512]{1,0:T(8,128)(2,1)S(1)} %collective-permute-done.6.refs_13_.refs_16_), channel_id=1, source_target_pairs={{0,4},{4,8},{8,12},{12,16},{16,20},{20,24},{24,28},{28,0},{1,5},{5... | collective-permute-start | bytes 983048 | tf_op jit(solution)/shard_map/ppermute | solution.py:209
  57.6 32.2 %collective-permute-start.13 = (bf16[512,1024]{1,0:T(8,128)(2,1)S(1)}, bf16[512,1024]{1,0:T(8,128)(2,1)S(1)}, u32[]{:S(2)}, u32[]{:S(2)}) collective-permute-start(bf16[512,1024]{1,0:T(8,128)(2,1)S(1)} %constant_dynamic-update-slice_fusion.refs_16_.refs_22_.refs_8_.refs_14_.refs_25_), channel_id=1, source_target_pairs={{0,192},{64,0},{128,64},{192,128},{1,193},{65,1},{129,65},{193,129... | collective-permute-start | bytes 3145736 | tf_op jit(solution)/shard_map/ppermute | solution.py:212
  62.5 19.3 %collective-permute-start.7 = (bf16[640,512]{1,0:T(8,128)(2,1)S(1)}, bf16[640,512]{1,0:T(8,128)(2,1)S(1)}, u32[]{:S(2)}, u32[]{:S(2)}) collective-permute-start(bf16[640,512]{1,0:T(8,128)(2,1)S(1)} %pad_maximum_fusion.2), channel_id=1, source_target_pairs={{0,1},{1,0},{2,3},{3,2},{4,5},{5,4},{6,7},{7,6},{8,9},{9,8},{10,11... | collective-permute-start | bytes 1966088 | tf_op jit(solution)/shard_map/ppermute | solution.py:239
  80.1 24.9 %collective-permute-start.15 = (bf16[512,1024]{1,0:T(8,128)(2,1)S(1)}, bf16[512,1024]{1,0:T(8,128)(2,1)S(1)}, u32[]{:S(2)}, u32[]{:S(2)}) collective-permute-start(bf16[512,1024]{1,0:T(8,128)(2,1)S(1)} %constant_dynamic-update-slice_fusion.refs_16_.refs_22_.refs_8_.refs_14_.refs_25_), channel_id=1, source_target_pairs={{0,64},{64,128},{128,192},{192,0},{1,65},{65,129},{129,193},{193,1... | collective-permute-start | bytes 3145736 | tf_op jit(solution)/shard_map/ppermute | solution.py:209
  81.4 23.5 %collective-permute-start.22 = (bf16[640,512]{1,0:T(8,128)(2,1)S(1)}, bf16[640,512]{1,0:T(8,128)(2,1)S(1)}, u32[]{:S(2)}, u32[]{:S(2)}) collective-permute-start(bf16[640,512]{1,0:T(8,128)(2,1)S(1)} %pad_maximum_fusion.3), channel_id=1, source_target_pairs={{0,1},{1,0},{2,3},{3,2},{4,5},{5,4},{6,7},{7,6},{8,9},{9,8},{10,11... | collective-permute-start | bytes 1966088 | tf_op jit(solution)/shard_map/ppermute | solution.py:239
  81.8 23.2 %collective-permute-start.23 = (bf16[640,512]{1,0:T(8,128)(2,1)S(1)}, bf16[640,512]{1,0:T(8,128)(2,1)S(1)}, u32[]{:S(2)}, u32[]{:S(2)}) collective-permute-start(bf16[640,512]{1,0:T(8,128)(2,1)S(1)} %collective-permute-done.9.refs_12_.refs_15_), channel_id=1, source_target_pairs={{0,4},{4,8},{8,12},{12,16},{16,20},{20,24},{24,28},{28,0},{1,5},{5... | collective-permute-start | bytes 1966088 | tf_op jit(solution)/shard_map/ppermute | solution.py:209
  81.8 7.0 %collective-permute-start.25 = (bf16[320,512]{1,0:T(8,128)(2,1)S(1)}, bf16[320,512]{1,0:T(8,128)(2,1)S(1)}, u32[]{:S(2)}, u32[]{:S(2)}) collective-permute-start(bf16[320,512]{1,0:T(8,128)(2,1)S(1)} %collective-permute-done.20.refs_2_.refs_19_), channel_id=1, source_target_pairs={{0,28},{4,0},{8,4},{12,8},{16,12},{20,16},{24,20},{28,24},{1,29},{... | collective-permute-start | bytes 983048 | tf_op jit(solution)/shard_map/ppermute | solution.py:212
  88.7 38.7 %collective-permute-start.27 = (bf16[512,1024]{1,0:T(8,128)(2,1)S(1)}, bf16[512,1024]{1,0:T(8,128)(2,1)S(1)}, u32[]{:S(2)}, u32[]{:S(2)}) collective-permute-start(bf16[512,1024]{1,0:T(8,128)(2,1)S(1)} %pad_maximum_fusion), channel_id=1, source_target_pairs={{0,64},{64,128},{128,192},{192,0},{1,65},{65,129},{129,193},{193,1... | collective-permute-start | bytes 3145736 | tf_op jit(solution)/shard_map/ppermute | solution.py:209
  89.8 37.6 %collective-permute-start.28 = (bf16[512,1024]{1,0:T(8,128)(2,1)S(1)}, bf16[512,1024]{1,0:T(8,128)(2,1)S(1)}, u32[]{:S(2)}, u32[]{:S(2)}) collective-permute-start(bf16[512,1024]{1,0:T(8,128)(2,1)S(1)} %collective-permute-done.13.refs_18_.refs_24_.refs_10_.refs_16_.refs_27_), channel_id=1, source_target_pairs={{0,192},{64,0},{128,64},{192,128},{1,193},{65,1},{129,65},{193,129... | collective-permute-start | bytes 3145736 | tf_op jit(solution)/shard_map/ppermute | solution.py:212
  104.9 12.3 %collective-permute-start.19 = (bf16[640,512]{1,0:T(8,128)(2,1)S(1)}, bf16[640,512]{1,0:T(8,128)(2,1)S(1)}, u32[]{:S(2)}, u32[]{:S(2)}) collective-permute-start(bf16[640,512]{1,0:T(8,128)(2,1)S(1)} %collective-permute-done.4.refs_6_.refs_9_), channel_id=1, source_target_pairs={{0,28},{4,0},{8,4},{12,8},{16,12},{20,16},{24,20},{28,24},{1,29},{... | collective-permute-start | bytes 1966088 | tf_op jit(solution)/shard_map/ppermute | solution.py:212
  105.0 22.5 %collective-permute-start.26 = (bf16[320,512]{1,0:T(8,128)(2,1)S(1)}, bf16[320,512]{1,0:T(8,128)(2,1)S(1)}, u32[]{:S(2)}, u32[]{:S(2)}) collective-permute-start(bf16[320,512]{1,0:T(8,128)(2,1)S(1)} %collective-permute-done.25.refs_1_), channel_id=1, source_target_pairs={{0,1},{1,0},{2,3},{3,2},{4,5},{5,4},{6,7},{7,6},{8,9},{9,8},{10,11... | collective-permute-start | bytes 983048 | tf_op jit(solution)/shard_map/ppermute | solution.py:241
  105.0 22.4 %collective-permute-start.24 = (bf16[640,512]{1,0:T(8,128)(2,1)S(1)}, bf16[640,512]{1,0:T(8,128)(2,1)S(1)}, u32[]{:S(2)}, u32[]{:S(2)}) collective-permute-start(bf16[640,512]{1,0:T(8,128)(2,1)S(1)} %collective-permute-done.23.refs_4_.refs_21_), channel_id=1, source_target_pairs={{0,4},{4,8},{8,12},{12,16},{16,20},{20,24},{24,28},{28,0},{1,5},{5... | collective-permute-start | bytes 1966088 | tf_op jit(solution)/shard_map/ppermute | solution.py:209
  130.1 6.8 %collective-permute-start.29 = (f32[1280,512]{1,0:T(8,128)S(1)}, f32[1280,512]{1,0:T(8,128)S(1)}, u32[]{:S(2)}, u32[]{:S(2)}) collective-permute-start(f32[1280,512]{1,0:T(8,128)S(1)} %shard_map.31), channel_id=1, source_target_pairs={{0,2},{2,0},{1,3},{3,1},{4,6},{6,4},{5,7},{7,5},{8,10},{10,8},{9,1... | collective-permute-start | bytes 7864328 | tf_op jit(solution)/shard_map/ppermute | solution.py:277

commit v2 on v1

--- a/solution.py
+++ b/solution.py
@@ -1,5 +1,3 @@
-import functools
-
 import jax
 import jax.numpy as jnp
 from jax import lax
@@ -10,8 +8,9 @@
 
 
 AXES = ("y", "xl", "z", "core", "xh")
-NEAR = (0, 1, 2, -1, -2)
-MIDDLE = (3, -3)
+FIRST = (0, 1, -1)
+SECOND = (2, -2)
+THIRD = (3, -3)
 LATE = (4,)
 
 
@@ -114,15 +113,18 @@
     return call(kernel, (2, rows, width), blocks, tokens, arrays, totals, [], aliases)
 
 
-def final_product(half, total, late_tokens, near_tokens, weights, rows, nb, zn, yn):
+def final_product(half, used, total, late_tokens, near_tokens, weights, rows, nb, zn, yn):
     depth, width = weights[0][0].shape[0], total.shape[2]
-    tokens = late_tokens + near_tokens
-    late = len(LATE)
+    tokens = [[block[part] for part in used] for block in late_tokens + near_tokens]
+    late, n = len(LATE), len(used)
+    base = 2 * nb if used == (0,) else 0
+    wanted_rows = sum((rows - 2 * nb, nb, nb)[part] for part in used)
 
     def kernel(total_ref, *refs):
-        parts, w_refs = refs[: 3 * len(tokens)], refs[3 * len(tokens) : -5]
+        parts, w_refs = refs[: n * len(tokens)], refs[n * len(tokens) : -5]
         out_ref, w_buf, w_sem, t_buf, t_sem = refs[-5:]
-        at = places(rows, nb)
+        from_total = [places(rows, nb)[part] for part in used]
+        at = [pl.ds(0, where.size) if base else where for where in from_total]
 
         def weight_copy(i, slot):
             return pltpu.make_async_copy(
@@ -141,13 +143,13 @@
                     ref.at[pl.ds(first, where.size)], t_buf.at[slot, where], t_sem.at[slot, k]
                 )
                 for k, (ref, (_, first), where) in enumerate(
-                    zip(parts[3 * j : 3 * j + 3], tokens[j], at)
+                    zip(parts[n * j : n * j + n], tokens[j], at)
                 )
             ]
 
         start_weight(meets(LATE[0], zn, yn)[1], 0, True)
         found, side = jnp.int32(0), [jnp.int32(0)] * 2
-        for j, d in enumerate(NEAR + MIDDLE):
+        for j, d in enumerate(FIRST + SECOND + THIRD):
             across, index = meets(d, zn, yn)
             for slot in range(2):
                 here = jnp.logical_and(across == yn // 2, found == slot)
@@ -166,8 +168,10 @@
             else:
                 start_weight(side[0], 1 - slot, found > 0)
             weight_copy(0, slot).wait()
-            for ref, (_, first), where in zip(parts[3 * j : 3 * j + 3], tokens[j], at):
-                before = total_ref[half, where, :] if j == 0 else out_ref[where, :]
+            for ref, (_, first), where, source in zip(
+                parts[n * j : n * j + n], tokens[j], at, from_total
+            ):
+                before = total_ref[half, source, :] if j == 0 else out_ref[where, :]
                 out_ref[where, :] = before + jnp.dot(
                     ref[first : first + where.size, :],
                     w_buf[slot],
@@ -184,18 +188,61 @@
             weight_copy(0, slot).wait()
             for copy in token_copies(late, k):
                 copy.wait()
-            for first in range(0, rows, rows // 2):
-                where = slice(first, first + rows // 2)
+
+            def rows_of(i, carry):
+                where = pl.ds(pl.multiple_of(i * (rows // 2), rows // 2), rows // 2)
                 out_ref[where, :] += jnp.dot(
                     t_buf[k, where, :], w_buf[slot], preferred_element_type=jnp.float32
                 )
-            return carry
+                return carry
+
+            return lax.fori_loop(0, wanted_rows // (rows // 2), rows_of, carry)
 
         lax.fori_loop(0, found, rest, 0)
 
-    scratch = [pltpu.VMEM((2, rows, depth), jnp.bfloat16), pltpu.SemaphoreType.DMA((2, 3))]
+    scratch = [
+        pltpu.VMEM((2, wanted_rows, depth), jnp.bfloat16),
+        pltpu.SemaphoreType.DMA((2, n)),
+    ]
     arrays = [w for w, _ in weights]
-    return call(kernel, (rows, width), 3, tokens, arrays, [total], scratch, {})
+    shape = (wanted_rows, width)
+    return call(kernel, shape, 3, tokens, arrays, [total], scratch, {})
+
+
+def finish(own, lower, upper):
+    rows, width = own.shape
+    chunk = rows // 4
+
+    def kernel(own_ref, lower_ref, upper_ref, out_ref, buf, sem):
+        def store(i):
+            return pltpu.make_async_copy(
+                buf.at[i], out_ref.at[pl.ds(i * chunk, chunk)], sem.at[i]
+            )
+
+        for i in range(4):
+            source = lower_ref if i < 2 else upper_ref
+            first = (i % 2) * chunk
+            buf[i] = (
+                own_ref[i * chunk : (i + 1) * chunk, :] + source[first : first + chunk, :]
+            ).astype(jnp.bfloat16)
+            if i:
+                store(i - 1).start()
+        store(3).start()
+        for i in range(4):
+            store(i).wait()
+
+    return pl.pallas_call(
+        kernel,
+        name="finish",
+        out_shape=jax.ShapeDtypeStruct((rows, width), jnp.bfloat16),
+        in_specs=[VMEM] * 3,
+        out_specs=ANYWHERE,
+        scratch_shapes=[pltpu.VMEM((4, chunk, width), jnp.bfloat16), pltpu.SemaphoreType.DMA((4,))],
+        compiler_params=pltpu.CompilerParams(vmem_limit_bytes=4 * 1024 * 1024),
+        cost_estimate=pl.CostEstimate(
+            flops=rows * width, bytes_accessed=10 * rows * width, transcendentals=0
+        ),
+    )(own, lower, upper)
 
 
 def per_device(tokens, up_weight):
@@ -255,7 +302,9 @@
     def block(d):
         return [(a[d], 0), (b[d], 0), c[d]]
 
-    near, middle, late = ([block(d) for d in order] for order in (NEAR, MIDDLE, LATE))
+    first, second, third, late = (
+        [block(d) for d in order] for order in (FIRST, SECOND, THIRD, LATE)
+    )
 
     def weights(half, distances):
         listed = []
@@ -266,16 +315,19 @@
 
     sizes = (rows, nb, zn, yn)
     near_weights = [weights(half, (0, 1, -1)) for half in range(2)]
-    total = early_product(NEAR, None, near, near_weights, *sizes)
-    total = early_product(MIDDLE, total, middle, near_weights, *sizes)
-    rest = [
-        functools.partial(
-            final_product, half, total, late, near + middle, weights(half, (0, 1, 2, -1)), *sizes
-        )
-        for half in range(2)
-    ]
-    swapped = lax.ppermute(rest[1](), "core", ring(2, 1))
-    return (rest[0]() + swapped).astype(jnp.bfloat16)
+    total = early_product(FIRST, None, first, near_weights, *sizes)
+    total = early_product(SECOND, total, second, near_weights, *sizes)
+    total = early_product(THIRD, total, third, near_weights, *sizes)
+
+    def final(half, used):
+        others = first + second + third
+        far_weights = weights(half, (0, 1, 2, -1))
+        return final_product(half, used, total, late, others, far_weights, *sizes)
+
+    upper = lax.ppermute(final(1, (0,)), "core", ring(2, 1))
+    lower = lax.ppermute(final(1, (1, 2)), "core", ring(2, 1))
+    own = final(0, (0, 1, 2))
+    return finish(own, lower, upper)
 
 
 def solution(mesh):

time: 139 us -> 131 us (0.942)
  waiting for transfers between devices: 69.2 us -> 39.8 us
  starting transfers between devices: 46.9 us -> 68.4 us
  Pallas kernels: 17.6 us -> 19.6 us
  other arithmetic: 1.74 us -> 0.25 us
    ppermute x10, waiting for transfers between devices: 43.1 us -> 19.5 us  [up(): return lax.ppermute(a, axis, ring(lax.axis_size(axis), 1))]
    ppermute x1 -> x2, starting transfers between devices: 2.29 us -> 14.2 us  [the longest x1 14.1 us: per_device(): lower = lax.ppermute(final(1, (1, 2)), 'core', ring(2, 1))]
    ppermute x10, waiting for transfers between devices: 16.3 us -> 8.01 us  [down(): return lax.ppermute(a, axis, ring(lax.axis_size(axis), -1))]
    ppermute x10, starting transfers between devices: 25.8 us -> 32.5 us  [down(): return lax.ppermute(a, axis, ring(lax.axis_size(axis), -1))]
    ppermute x3, starting transfers between devices: 0.99 us -> 7.7 us  [per_device(): pair = lax.ppermute(jnp.concatenate([b[-d], b[d]], 0), 'xh', ring(2, 1))]
    ppermute x3, waiting for transfers between devices: 0.01 us -> 5.86 us  [per_device(): pair = lax.ppermute(jnp.concatenate([b[-d], b[d]], 0), 'xh', ring(2, 1))]
    ppermute x2, waiting for transfers between devices: 7.86 us -> 4.31 us  [crossed(): return lax.ppermute(a, ('y', 'core'), pairs)]
    ppermute x10, starting transfers between devices: 5.62 us -> 3.02 us  [up(): return lax.ppermute(a, axis, ring(lax.axis_size(axis), 1))]
  transfers between devices with their start and end apart: 30 -> 31, of which waited for: 12 -> 13; matrix products, arithmetic and copies ran while one was open for 1% -> 0% of each run, Pallas kernels for 11% -> 14%
where the time goes in v2:
time: 131 us; the launch traced here: 130 us
  starting transfers between devices  68.4 us (52%)
  waiting for transfers between devices  39.8 us (30%)
  Pallas kernels  19.6 us (15%)
  local copies, waits for them, and re-layouts  1.77 us (1%)
    ppermute x10, starting transfers between devices, down(): return lax.ppermute(a, axis, ring(lax.axis_size(axis), -1))  32.5 us
    ppermute x10, waiting for transfers between devices, up(): return lax.ppermute(a, axis, ring(lax.axis_size(axis), 1))  19.5 us
    pallas_call x6, Pallas kernels, call(): pl.pallas_call(kernel, out_shape=jax.ShapeDtypeStruct(out_shape, jnp.floa...  18.4 us
    ppermute x1, starting transfers between devices, per_device(): lower = lax.ppermute(final(1, (1, 2)), 'core', ring(2, 1))  14.1 us
    ppermute x10, waiting for transfers between devices, down(): return lax.ppermute(a, axis, ring(lax.axis_size(axis), -1))  8.01 us
    ppermute x3, starting transfers between devices, per_device(): pair = lax.ppermute(jnp.concatenate([b[-d], b[d]], 0), 'xh', ring(2, 1))  7.7 us
    ppermute x3, waiting for transfers between devices, per_device(): pair = lax.ppermute(jnp.concatenate([b[-d], b[d]], 0), 'xh', ring(2, 1))  5.86 us
    ppermute x2, waiting for transfers between devices, crossed(): return lax.ppermute(a, ('y', 'core'), pairs)  4.31 us
  transfers between devices with their start and end apart: 31, of which 13 were waited for; matrix products, arithmetic and copies ran while one was open for 0% of the time, Pallas kernels for 14%

profile of v2, /device:TPU:1, one launch (start us, length us, event | category | flops | bytes accessed | tf_op | source)
XLA Modules:
  0.0 130.2 jit_solution(12820293062701898119)
XLA Ops:
  0.0 1.6 %fusion = (bf16[512,512]{1,0:T(8,128)(2,1)S(1)}, bf16[512,512]{1,0:T(8,128)(2,1)S(1)}, bf16[512,512]{1,0:T(8,128)(2,1)S(1)}) fusion(bf16[1024,1024]{1,0:T(8,128)(2,1)} %param.3, s32[]{:T(128)S(6)} %select_n.24, s32[]{:T(128)S(6)} %select_n.23, s32[]{:T(128)S(6)} %select_n.22, s32[]{:T(128)S(6)} %select_n.25), kind=kLoop, calls=%fused_computation.8 | loop fusion | bytes 3145744 | tf_op jit(solution)/shard_map/dynamic_slice | solution.py:268
  1.6 2.1 %collective-permute-start.5 = (bf16[512,512]{1,0:T(8,128)(2,1)S(1)}, bf16[512,512]{1,0:T(8,128)(2,1)S(1)}, u32[]{:S(2)}, u32[]{:S(2)}) collective-permute-start(bf16[512,512]{1,0:T(8,128)(2,1)S(1)} %get-tuple-element.6.refs_9_.refs_7_.refs_24_), channel_id=1, source_target_pairs={{0,32},{32,0},{1,33},{33,1},{2,34},{34,2},{3,35},{35,3},{4,36},{36... | collective-permute-start | bytes 1572872 | tf_op jit(solution)/shard_map/ppermute | solution.py:293
  3.7 5.7 %collective-permute-start.1 = (bf16[320,512]{1,0:T(8,128)(2,1)S(1)}, bf16[320,512]{1,0:T(8,128)(2,1)S(1)}, u32[]{:S(2)}, u32[]{:S(2)}) collective-permute-start(bf16[320,512]{1,0:T(8,128)(2,1)S(1)} %get-tuple-element.9.refs_1_.refs_4_.refs_2_), channel_id=1, source_target_pairs={{0,28},{4,0},{8,4},{12,8},{16,12},{20,16},{24,20},{28,24},{1,29},{... | collective-permute-start | bytes 983048 | tf_op jit(solution)/shard_map/ppermute | solution.py:259
  9.4 2.9 %collective-permute-start.6 = (bf16[512,512]{1,0:T(8,128)(2,1)S(1)}, bf16[512,512]{1,0:T(8,128)(2,1)S(1)}, u32[]{:S(2)}, u32[]{:S(2)}) collective-permute-start(bf16[512,512]{1,0:T(8,128)(2,1)S(1)} %get-tuple-element.7), channel_id=1, source_target_pairs={{0,35},{1,34},{2,33},{3,32},{32,3},{33,2},{34,1},{35,0},{4,39},{5,... | collective-permute-start | bytes 1572872 | tf_op jit(solution)/shard_map/ppermute | solution.py:294
  12.3 2.7 %collective-permute-start.7 = (bf16[512,512]{1,0:T(8,128)(2,1)S(1)}, bf16[512,512]{1,0:T(8,128)(2,1)S(1)}, u32[]{:S(2)}, u32[]{:S(2)}) collective-permute-start(bf16[512,512]{1,0:T(8,128)(2,1)S(1)} %get-tuple-element.6.refs_9_.refs_7_.refs_24_), channel_id=1, source_target_pairs={{0,192},{64,0},{128,64},{192,128},{1,193},{65,1},{129,65},{193,129... | collective-permute-start | bytes 1572872 | tf_op jit(solution)/shard_map/ppermute | solution.py:259
  15.1 0.4 collective-permute-done.1.refs_4_.refs_7_
  15.5 1.3 collective-permute-start.9
  16.8 6.2 %collective-permute-done.2.refs_7_.refs_10_.refs_6_ = bf16[320,512]{1,0:T(8,128)(2,1)S(1)} collective-permute-done((bf16[320,512]{1,0:T(8,128)(2,1)S(1)}, bf16[320,512]{1,0:T(8,128)(2,1)S(1)}, u32[]{:S(2)}, u32[]{:S(2)}) %collective-permute-start.2) | collective-permute-done | bytes 327712 | tf_op jit(solution)/shard_map/ppermute | solution.py:256
  23.0 0.1 collective-permute-start.11
  23.1 3.0 %collective-permute-start.12 = (bf16[512,512]{1,0:T(8,128)(2,1)S(1)}, bf16[512,512]{1,0:T(8,128)(2,1)S(1)}, u32[]{:S(2)}, u32[]{:S(2)}) collective-permute-start(bf16[512,512]{1,0:T(8,128)(2,1)S(1)} %get-tuple-element.5), channel_id=1, source_target_pairs={{0,194},{2,192},{64,2},{66,0},{128,66},{130,64},{192,130},{194,128... | collective-permute-start | bytes 1572872 | tf_op jit(solution)/shard_map/ppermute | solution.py:265
  26.1 0.6 collective-permute-start.13
  26.8 0.1 collective-permute-start.4
  26.8 1.7 %collective-permute-done.9.refs_13_.refs_11_.refs_30_ = bf16[512,512]{1,0:T(8,128)(2,1)S(1)} collective-permute-done((bf16[512,512]{1,0:T(8,128)(2,1)S(1)}, bf16[512,512]{1,0:T(8,128)(2,1)S(1)}, u32[]{:S(2)}, u32[]{:S(2)}) %collective-permute-start.9) | collective-permute-done | bytes 524320 | tf_op jit(solution)/shard_map/ppermute | solution.py:256
  28.5 3.4 %collective-permute-start = (bf16[640,512]{1,0:T(8,128)(2,1)S(1)}, bf16[640,512]{1,0:T(8,128)(2,1)S(1)}, u32[]{:S(2)}, u32[]{:S(2)}) collective-permute-start(bf16[640,512]{1,0:T(8,128)(2,1)S(1)} %slice.3.refs_0_.refs_3_.refs_1_), channel_id=1, source_target_pairs={{0,28},{4,0},{8,4},{12,8},{16,12},{20,16},{24,20},{28,24},{1,29},{... | collective-permute-start | bytes 1966088 | tf_op jit(solution)/shard_map/ppermute | solution.py:259
  32.0 2.5 %collective-permute-start.3 = (bf16[640,512]{1,0:T(8,128)(2,1)S(1)}, bf16[640,512]{1,0:T(8,128)(2,1)S(1)}, u32[]{:S(2)}, u32[]{:S(2)}) collective-permute-start(bf16[640,512]{1,0:T(8,128)(2,1)S(1)} %pad_maximum_fusion.1), channel_id=1, source_target_pairs={{0,1},{1,0},{2,3},{3,2},{4,5},{5,4},{6,7},{7,6},{8,9},{9,8},{10,11... | collective-permute-start | bytes 1966088 | tf_op jit(solution)/shard_map/ppermute | solution.py:286
  34.5 3.1 %collective-permute-done.12.refs_17_.refs_15_.refs_18_.refs_10_ = bf16[512,512]{1,0:T(8,128)(2,1)S(1)} collective-permute-done((bf16[512,512]{1,0:T(8,128)(2,1)S(1)}, bf16[512,512]{1,0:T(8,128)(2,1)S(1)}, u32[]{:S(2)}, u32[]{:S(2)}) %collective-permute-start.12) | collective-permute-done | bytes 524320 | tf_op jit(solution)/shard_map/ppermute | solution.py:265
  37.6 3.1 %collective-permute-start.15 = (bf16[320,512]{1,0:T(8,128)(2,1)S(1)}, bf16[320,512]{1,0:T(8,128)(2,1)S(1)}, u32[]{:S(2)}, u32[]{:S(2)}) collective-permute-start(bf16[320,512]{1,0:T(8,128)(2,1)S(1)} %collective-permute-done.1.refs_4_.refs_7_), channel_id=1, source_target_pairs={{0,28},{4,0},{8,4},{12,8},{16,12},{20,16},{24,20},{28,24},{1,29},{... | collective-permute-start | bytes 983048 | tf_op jit(solution)/shard_map/ppermute | solution.py:259
  40.7 1.3 collective-permute-done.13.refs_19_.refs_17_.refs_22_.refs_14_
  42.0 6.6 %collective-permute-done.15.refs_2_.refs_13_.refs_8_ = bf16[320,512]{1,0:T(8,128)(2,1)S(1)} collective-permute-done((bf16[320,512]{1,0:T(8,128)(2,1)S(1)}, bf16[320,512]{1,0:T(8,128)(2,1)S(1)}, u32[]{:S(2)}, u32[]{:S(2)}) %collective-permute-start.15) | collective-permute-done | bytes 327712 | tf_op jit(solution)/shard_map/ppermute | solution.py:259
  48.6 3.1 %collective-permute-start.20 = (bf16[320,512]{1,0:T(8,128)(2,1)S(1)}, bf16[320,512]{1,0:T(8,128)(2,1)S(1)}, u32[]{:S(2)}, u32[]{:S(2)}) collective-permute-start(bf16[320,512]{1,0:T(8,128)(2,1)S(1)} %collective-permute-done.15.refs_2_.refs_13_.refs_8_), channel_id=1, source_target_pairs={{0,28},{4,0},{8,4},{12,8},{16,12},{20,16},{24,20},{28,24},{1,29},{... | collective-permute-start | bytes 983048 | tf_op jit(solution)/shard_map/ppermute | solution.py:259
  51.7 0.1 collective-permute-start.18
  51.8 1.0 collective-permute-done.16.refs_5_.refs_16_.refs_10_
  52.8 0.1 constant_dynamic-update-slice_fusion.refs_10_.refs_16_.refs_8_.refs_14_.refs_25_.refs_17_.refs_9_
  52.9 2.8 %collective-permute-start.8 = (bf16[512,1024]{1,0:T(8,128)(2,1)S(1)}, bf16[512,1024]{1,0:T(8,128)(2,1)S(1)}, u32[]{:S(2)}, u32[]{:S(2)}) collective-permute-start(bf16[512,1024]{1,0:T(8,128)(2,1)S(1)} %constant_dynamic-update-slice_fusion.refs_10_.refs_16_.refs_8_.refs_14_.refs_25_.refs_17_.refs_9_), channel_id=1, source_target_pairs={{0,192},{64,0},{128,64},{192,128},{1,193},{65,1},{129,65},{193,129... | collective-permute-start | bytes 3145736 | tf_op jit(solution)/shard_map/ppermute | solution.py:259
  55.7 2.7 %collective-permute-start.14 = (bf16[640,512]{1,0:T(8,128)(2,1)S(1)}, bf16[640,512]{1,0:T(8,128)(2,1)S(1)}, u32[]{:S(2)}, u32[]{:S(2)}) collective-permute-start(bf16[640,512]{1,0:T(8,128)(2,1)S(1)} %collective-permute-done.refs_3_.refs_6_.refs_2_), channel_id=1, source_target_pairs={{0,28},{4,0},{8,4},{12,8},{16,12},{20,16},{24,20},{28,24},{1,29},{... | collective-permute-start | bytes 1966088 | tf_op jit(solution)/shard_map/ppermute | solution.py:259
  58.4 10.6 %collective-permute-done.21.refs_5_.refs_22_.refs_14_ = bf16[320,512]{1,0:T(8,128)(2,1)S(1)} collective-permute-done((bf16[320,512]{1,0:T(8,128)(2,1)S(1)}, bf16[320,512]{1,0:T(8,128)(2,1)S(1)}, u32[]{:S(2)}, u32[]{:S(2)}) %collective-permute-start.21) | collective-permute-done | bytes 327712 | tf_op jit(solution)/shard_map/ppermute | solution.py:256
  69.0 2.4 %collective-permute-start.17 = (bf16[640,512]{1,0:T(8,128)(2,1)S(1)}, bf16[640,512]{1,0:T(8,128)(2,1)S(1)}, u32[]{:S(2)}, u32[]{:S(2)}) collective-permute-start(bf16[640,512]{1,0:T(8,128)(2,1)S(1)} %pad_maximum_fusion.2), channel_id=1, source_target_pairs={{0,1},{1,0},{2,3},{3,2},{4,5},{5,4},{6,7},{7,6},{8,9},{9,8},{10,11... | collective-permute-start | bytes 1966088 | tf_op jit(solution)/shard_map/ppermute | solution.py:286
  71.5 0.9 collective-permute-done.14.refs_1_.refs_12_.refs_4_
  72.4 3.1 %collective-permute-start.25 = (bf16[320,512]{1,0:T(8,128)(2,1)S(1)}, bf16[320,512]{1,0:T(8,128)(2,1)S(1)}, u32[]{:S(2)}, u32[]{:S(2)}) collective-permute-start(bf16[320,512]{1,0:T(8,128)(2,1)S(1)} %collective-permute-done.20.refs_2_.refs_19_.refs_12_), channel_id=1, source_target_pairs={{0,28},{4,0},{8,4},{12,8},{16,12},{20,16},{24,20},{28,24},{1,29},{... | collective-permute-start | bytes 983048 | tf_op jit(solution)/shard_map/ppermute | solution.py:259
  75.6 4.4 %collective-permute-done.17.refs_3_.refs_6_.refs_14_.refs_17_.refs_9_.refs_11_ = bf16[640,512]{1,0:T(8,128)(2,1)S(1)} collective-permute-done((bf16[640,512]{1,0:T(8,128)(2,1)S(1)}, bf16[640,512]{1,0:T(8,128)(2,1)S(1)}, u32[]{:S(2)}, u32[]{:S(2)}) %collective-permute-start.17) | collective-permute-done | bytes 655392 | tf_op jit(solution)/shard_map/ppermute | solution.py:286
  80.0 2.7 %collective-permute-start.22 = (bf16[640,512]{1,0:T(8,128)(2,1)S(1)}, bf16[640,512]{1,0:T(8,128)(2,1)S(1)}, u32[]{:S(2)}, u32[]{:S(2)}) collective-permute-start(bf16[640,512]{1,0:T(8,128)(2,1)S(1)} %pad_maximum_fusion.3), channel_id=1, source_target_pairs={{0,1},{1,0},{2,3},{3,2},{4,5},{5,4},{6,7},{7,6},{8,9},{9,8},{10,11... | collective-permute-start | bytes 1966088 | tf_op jit(solution)/shard_map/ppermute | solution.py:286
  82.7 0.1 pad_maximum_fusion
  82.8 0.1 collective-permute-start.27
  82.9 5.9 %collective-permute-start.28 = (bf16[512,1024]{1,0:T(8,128)(2,1)S(1)}, bf16[512,1024]{1,0:T(8,128)(2,1)S(1)}, u32[]{:S(2)}, u32[]{:S(2)}) collective-permute-start(bf16[512,1024]{1,0:T(8,128)(2,1)S(1)} %collective-permute-done.8.refs_12_.refs_18_.refs_10_.refs_16_.refs_27_.refs_19_.refs_11_), channel_id=1, source_target_pairs={{0,192},{64,0},{128,64},{192,128},{1,193},{65,1},{129,65},{193,129... | collective-permute-start | bytes 3145736 | tf_op jit(solution)/shard_map/ppermute | solution.py:259
  88.9 1.5 %collective-permute-start.24 = (bf16[640,512]{1,0:T(8,128)(2,1)S(1)}, bf16[640,512]{1,0:T(8,128)(2,1)S(1)}, u32[]{:S(2)}, u32[]{:S(2)}) collective-permute-start(bf16[640,512]{1,0:T(8,128)(2,1)S(1)} %collective-permute-done.23.refs_4_.refs_21_.refs_7_), channel_id=1, source_target_pairs={{0,4},{4,8},{8,12},{12,16},{16,20},{20,24},{24,28},{28,0},{1,5},{5... | collective-permute-start | bytes 1966088 | tf_op jit(solution)/shard_map/ppermute | solution.py:256
  90.4 6.3 %shard_map.28.refs_0_ = f32[2,1280,512]{2,1,0:T(8,128)S(1)} custom-call(bf16[640,512]{1,0:T(8,128)(2,1)S(1)} %slice.3.refs_0_.refs_3_.refs_1_, bf16[320,512]{1,0:T(8,128)(2,1)S(1)} %get-tuple-element.9.refs_1_.refs_4_.refs_2_, bf16[320,512]{1,0:T(8,128)(2,1)S(1)} %get-tuple-element.8.refs_2_.refs_5_.refs_3_, ...), custom_call_target="tpu_custom_call" | custom-call | flops 4026531840 | bytes 13631488 | tf_op jit(solution)/shard_map/pallas_call | solution.py:45
  96.6 1.5 %collective-permute-done.22.refs_3_.refs_6_.refs_20_.refs_23_.refs_13_.refs_15_ = bf16[640,512]{1,0:T(8,128)(2,1)S(1)} collective-permute-done((bf16[640,512]{1,0:T(8,128)(2,1)S(1)}, bf16[640,512]{1,0:T(8,128)(2,1)S(1)}, u32[]{:S(2)}, u32[]{:S(2)}) %collective-permute-start.22) | collective-permute-done | bytes 655392 | tf_op jit(solution)/shard_map/ppermute | solution.py:286
  98.1 2.2 %collective-permute-start.26 = (bf16[320,512]{1,0:T(8,128)(2,1)S(1)}, bf16[320,512]{1,0:T(8,128)(2,1)S(1)}, u32[]{:S(2)}, u32[]{:S(2)}) collective-permute-start(bf16[320,512]{1,0:T(8,128)(2,1)S(1)} %collective-permute-done.25.refs_1_.refs_0_), channel_id=1, source_target_pairs={{0,1},{1,0},{2,3},{3,2},{4,5},{5,4},{6,7},{7,6},{8,9},{9,8},{10,11... | collective-permute-start | bytes 983048 | tf_op jit(solution)/shard_map/ppermute | solution.py:288
  100.3 3.8 %shard_map.29.refs_0_ = f32[2,1280,512]{2,1,0:T(8,128)S(1)} custom-call(f32[2,1280,512]{2,1,0:T(8,128)S(1)} %shard_map.28.refs_0_, bf16[640,512]{1,0:T(8,128)(2,1)S(1)} %collective-permute-done.14.refs_1_.refs_12_.refs_4_, bf16[320,512]{1,0:T(8,128)(2,1)S(1)} %collective-permute-done.15.refs_2_.refs_13_.refs_8_, ...), custom_call_target="tpu_custom_call", output_to_operand_aliasing={{}: (0, {})} | custom-call | flops 2684354560 | bytes 9961472 | tf_op jit(solution)/shard_map/pallas_call | solution.py:45
  104.1 2.2 %shard_map.30.total_ref = f32[2,1280,512]{2,1,0:T(8,128)S(1)} custom-call(f32[2,1280,512]{2,1,0:T(8,128)S(1)} %shard_map.29.refs_0_, bf16[640,512]{1,0:T(8,128)(2,1)S(1)} %collective-permute-done.19.refs_1_.refs_18_.refs_6_, bf16[320,512]{1,0:T(8,128)(2,1)S(1)} %collective-permute-done.20.refs_2_.refs_19_.refs_12_, ...), custom_call_target="tpu_custom_call", output_to_operand_aliasing={{}: (0, {})} | custom-call | flops 2684354560 | bytes 9961472 | tf_op jit(solution)/shard_map/pallas_call | solution.py:45
  106.4 1.9 %collective-permute-done.26.refs_2_.refs_1_ = bf16[320,512]{1,0:T(8,128)(2,1)S(1)} collective-permute-done((bf16[320,512]{1,0:T(8,128)(2,1)S(1)}, bf16[320,512]{1,0:T(8,128)(2,1)S(1)}, u32[]{:S(2)}, u32[]{:S(2)}) %collective-permute-start.26) | collective-permute-done | bytes 327712 | tf_op jit(solution)/shard_map/ppermute | solution.py:288
  108.3 1.7 %shard_map.32 = f32[640,512]{1,0:T(8,128)S(1)} custom-call(f32[2,1280,512]{2,1,0:T(8,128)S(1)} %shard_map.30.total_ref, bf16[320,512]{1,0:T(8,128)(2,1)S(1)} %collective-permute-done.25.refs_1_.refs_0_, bf16[320,512]{1,0:T(8,128)(2,1)S(1)} %collective-permute-done.26.refs_2_.refs_1_, bf16[320,512]{1,0:T(8,128)(2,1)S(1)} %get-tuple-element.9.refs_1_.refs_4_.refs_2_, ...), custom_call_target="tpu_custom_call" | custom-call | flops 1006632960 | bytes 4849664 | tf_op jit(solution)/shard_map/pallas_call | solution.py:45
  110.0 14.1 %collective-permute-start.29 = (f32[640,512]{1,0:T(8,128)S(1)}, f32[640,512]{1,0:T(8,128)S(1)}, u32[]{:S(2)}, u32[]{:S(2)}) collective-permute-start(f32[640,512]{1,0:T(8,128)S(1)} %shard_map.32), channel_id=1, source_target_pairs={{0,2},{2,0},{1,3},{3,1},{4,6},{6,4},{5,7},{7,5},{8,10},{10,8},{9,1... | collective-permute-start | bytes 3932168 | tf_op jit(solution)/shard_map/ppermute | solution.py:328
  124.1 1.7 %shard_map.33 = f32[640,512]{1,0:T(8,128)S(1)} custom-call(f32[2,1280,512]{2,1,0:T(8,128)S(1)} %shard_map.30.total_ref, bf16[640,512]{1,0:T(8,128)(2,1)S(1)} %collective-permute-done.24.refs_0_, bf16[640,512]{1,0:T(8,128)(2,1)S(1)} %slice.3.refs_0_.refs_3_.refs_1_, bf16[640,512]{1,0:T(8,128)(2,1)S(1)} %collective-permute-done.refs_3_.refs_6_.refs_2_, ...), custom_call_target="tpu_custom_call" | custom-call | flops 1006632960 | bytes 4849664 | tf_op jit(solution)/shard_map/pallas_call | solution.py:45
  125.7 0.2 collective-permute-start.30
  125.9 2.8 %shard_map.31.own_ref = f32[1280,512]{1,0:T(8,128)S(1)} custom-call(f32[2,1280,512]{2,1,0:T(8,128)S(1)} %shard_map.30.total_ref, bf16[640,512]{1,0:T(8,128)(2,1)S(1)} %collective-permute-done.24.refs_0_, bf16[320,512]{1,0:T(8,128)(2,1)S(1)} %collective-permute-done.25.refs_1_.refs_0_, bf16[320,512]{1,0:T(8,128)(2,1)S(1)} %collective-permute-done.26.refs_2_.refs_1_, ...), custom_call_target="tpu_custom_call" | custom-call | flops 2013265920 | bytes 8126464 | tf_op jit(solution)/shard_map/pallas_call | solution.py:45
  128.7 0.1 collective-permute-done.30.upper_ref
  128.9 1.2 finish.1
  (32 shorter events, 0.3 us)
Async XLA Ops:
  0.0 3.7 %copy-start = (bf16[1280,512]{1,0:T(8,128)(2,1)S(1)}, bf16[1280,512]{1,0:T(8,128)(2,1)}, u32[]{:S(2)}) copy-start(bf16[1280,512]{1,0:T(8,128)(2,1)} %param.2) | copy-start | bytes 3932164
  1.6 21.6 %collective-permute-start.5 = (bf16[512,512]{1,0:T(8,128)(2,1)S(1)}, bf16[512,512]{1,0:T(8,128)(2,1)S(1)}, u32[]{:S(2)}, u32[]{:S(2)}) collective-permute-start(bf16[512,512]{1,0:T(8,128)(2,1)S(1)} %get-tuple-element.6.refs_9_.refs_7_.refs_24_), channel_id=1, source_target_pairs={{0,32},{32,0},{1,33},{33,1},{2,34},{34,2},{3,35},{35,3},{4,36},{36... | collective-permute-start | bytes 1572872 | tf_op jit(solution)/shard_map/ppermute | solution.py:293
  3.7 11.8 %collective-permute-start.1 = (bf16[320,512]{1,0:T(8,128)(2,1)S(1)}, bf16[320,512]{1,0:T(8,128)(2,1)S(1)}, u32[]{:S(2)}, u32[]{:S(2)}) collective-permute-start(bf16[320,512]{1,0:T(8,128)(2,1)S(1)} %get-tuple-element.9.refs_1_.refs_4_.refs_2_), channel_id=1, source_target_pairs={{0,28},{4,0},{8,4},{12,8},{16,12},{20,16},{24,20},{28,24},{1,29},{... | collective-permute-start | bytes 983048 | tf_op jit(solution)/shard_map/ppermute | solution.py:259
  9.4 16.8 %collective-permute-start.6 = (bf16[512,512]{1,0:T(8,128)(2,1)S(1)}, bf16[512,512]{1,0:T(8,128)(2,1)S(1)}, u32[]{:S(2)}, u32[]{:S(2)}) collective-permute-start(bf16[512,512]{1,0:T(8,128)(2,1)S(1)} %get-tuple-element.7), channel_id=1, source_target_pairs={{0,35},{1,34},{2,33},{3,32},{32,3},{33,2},{34,1},{35,0},{4,39},{5,... | collective-permute-start | bytes 1572872 | tf_op jit(solution)/shard_map/ppermute | solution.py:294
  12.3 10.7 %collective-permute-start.2 = (bf16[320,512]{1,0:T(8,128)(2,1)S(1)}, bf16[320,512]{1,0:T(8,128)(2,1)S(1)}, u32[]{:S(2)}, u32[]{:S(2)}) collective-permute-start(bf16[320,512]{1,0:T(8,128)(2,1)S(1)} %get-tuple-element.9.refs_1_.refs_4_.refs_2_), channel_id=1, source_target_pairs={{0,4},{4,8},{8,12},{12,16},{16,20},{20,24},{24,28},{28,0},{1,5},{5... | collective-permute-start | bytes 983048 | tf_op jit(solution)/shard_map/ppermute | solution.py:256
  12.3 14.4 %collective-permute-start.7 = (bf16[512,512]{1,0:T(8,128)(2,1)S(1)}, bf16[512,512]{1,0:T(8,128)(2,1)S(1)}, u32[]{:S(2)}, u32[]{:S(2)}) collective-permute-start(bf16[512,512]{1,0:T(8,128)(2,1)S(1)} %get-tuple-element.6.refs_9_.refs_7_.refs_24_), channel_id=1, source_target_pairs={{0,192},{64,0},{128,64},{192,128},{1,193},{65,1},{129,65},{193,129... | collective-permute-start | bytes 1572872 | tf_op jit(solution)/shard_map/ppermute | solution.py:259
  15.5 13.0 %collective-permute-start.9 = (bf16[512,512]{1,0:T(8,128)(2,1)S(1)}, bf16[512,512]{1,0:T(8,128)(2,1)S(1)}, u32[]{:S(2)}, u32[]{:S(2)}) collective-permute-start(bf16[512,512]{1,0:T(8,128)(2,1)S(1)} %get-tuple-element.6.refs_9_.refs_7_.refs_24_), channel_id=1, source_target_pairs={{0,64},{64,128},{128,192},{192,0},{1,65},{65,129},{129,193},{193,1... | collective-permute-start | bytes 1572872 | tf_op jit(solution)/shard_map/ppermute | solution.py:256
  23.0 9.0 %collective-permute-start.11 = (bf16[512,512]{1,0:T(8,128)(2,1)S(1)}, bf16[512,512]{1,0:T(8,128)(2,1)S(1)}, u32[]{:S(2)}, u32[]{:S(2)}) collective-permute-start(bf16[512,512]{1,0:T(8,128)(2,1)S(1)} %get-tuple-element.5), channel_id=1, source_target_pairs={{0,2},{2,0},{1,3},{3,1},{4,6},{6,4},{5,7},{7,5},{8,10},{10,8},{9,1... | collective-permute-start | bytes 1572872 | tf_op jit(solution)/shard_map/ppermute | solution.py:295
  23.1 14.4 %collective-permute-start.12 = (bf16[512,512]{1,0:T(8,128)(2,1)S(1)}, bf16[512,512]{1,0:T(8,128)(2,1)S(1)}, u32[]{:S(2)}, u32[]{:S(2)}) collective-permute-start(bf16[512,512]{1,0:T(8,128)(2,1)S(1)} %get-tuple-element.5), channel_id=1, source_target_pairs={{0,194},{2,192},{64,2},{66,0},{128,66},{130,64},{192,130},{194,128... | collective-permute-start | bytes 1572872 | tf_op jit(solution)/shard_map/ppermute | solution.py:265
  26.1 15.8 %collective-permute-start.13 = (bf16[512,512]{1,0:T(8,128)(2,1)S(1)}, bf16[512,512]{1,0:T(8,128)(2,1)S(1)}, u32[]{:S(2)}, u32[]{:S(2)}) collective-permute-start(bf16[512,512]{1,0:T(8,128)(2,1)S(1)} %get-tuple-element.5), channel_id=1, source_target_pairs={{0,66},{2,64},{64,130},{66,128},{128,194},{130,192},{192,2},{194,0... | collective-permute-start | bytes 1572872 | tf_op jit(solution)/shard_map/ppermute | solution.py:265
  26.8 25.0 %collective-permute-start.4 = (bf16[640,512]{1,0:T(8,128)(2,1)S(1)}, bf16[640,512]{1,0:T(8,128)(2,1)S(1)}, u32[]{:S(2)}, u32[]{:S(2)}) collective-permute-start(bf16[640,512]{1,0:T(8,128)(2,1)S(1)} %slice.3.refs_0_.refs_3_.refs_1_), channel_id=1, source_target_pairs={{0,4},{4,8},{8,12},{12,16},{16,20},{20,24},{24,28},{28,0},{1,5},{5... | collective-permute-start | bytes 1966088 | tf_op jit(solution)/shard_map/ppermute | solution.py:256
  28.5 24.4 %collective-permute-start = (bf16[640,512]{1,0:T(8,128)(2,1)S(1)}, bf16[640,512]{1,0:T(8,128)(2,1)S(1)}, u32[]{:S(2)}, u32[]{:S(2)}) collective-permute-start(bf16[640,512]{1,0:T(8,128)(2,1)S(1)} %slice.3.refs_0_.refs_3_.refs_1_), channel_id=1, source_target_pairs={{0,28},{4,0},{8,4},{12,8},{16,12},{20,16},{24,20},{28,24},{1,29},{... | collective-permute-start | bytes 1966088 | tf_op jit(solution)/shard_map/ppermute | solution.py:259
  32.0 23.7 %collective-permute-start.3 = (bf16[640,512]{1,0:T(8,128)(2,1)S(1)}, bf16[640,512]{1,0:T(8,128)(2,1)S(1)}, u32[]{:S(2)}, u32[]{:S(2)}) collective-permute-start(bf16[640,512]{1,0:T(8,128)(2,1)S(1)} %pad_maximum_fusion.1), channel_id=1, source_target_pairs={{0,1},{1,0},{2,3},{3,2},{4,5},{5,4},{6,7},{7,6},{8,9},{9,8},{10,11... | collective-permute-start | bytes 1966088 | tf_op jit(solution)/shard_map/ppermute | solution.py:286
  37.6 11.0 %collective-permute-start.15 = (bf16[320,512]{1,0:T(8,128)(2,1)S(1)}, bf16[320,512]{1,0:T(8,128)(2,1)S(1)}, u32[]{:S(2)}, u32[]{:S(2)}) collective-permute-start(bf16[320,512]{1,0:T(8,128)(2,1)S(1)} %collective-permute-done.1.refs_4_.refs_7_), channel_id=1, source_target_pairs={{0,28},{4,0},{8,4},{12,8},{16,12},{20,16},{24,20},{28,24},{1,29},{... | collective-permute-start | bytes 983048 | tf_op jit(solution)/shard_map/ppermute | solution.py:259
  42.0 10.8 %collective-permute-start.16 = (bf16[320,512]{1,0:T(8,128)(2,1)S(1)}, bf16[320,512]{1,0:T(8,128)(2,1)S(1)}, u32[]{:S(2)}, u32[]{:S(2)}) collective-permute-start(bf16[320,512]{1,0:T(8,128)(2,1)S(1)} %collective-permute-done.2.refs_7_.refs_10_.refs_6_), channel_id=1, source_target_pairs={{0,4},{4,8},{8,12},{12,16},{16,20},{20,24},{24,28},{28,0},{1,5},{5... | collective-permute-start | bytes 983048 | tf_op jit(solution)/shard_map/ppermute | solution.py:256
  48.6 9.8 %collective-permute-start.20 = (bf16[320,512]{1,0:T(8,128)(2,1)S(1)}, bf16[320,512]{1,0:T(8,128)(2,1)S(1)}, u32[]{:S(2)}, u32[]{:S(2)}) collective-permute-start(bf16[320,512]{1,0:T(8,128)(2,1)S(1)} %collective-permute-done.15.refs_2_.refs_13_.refs_8_), channel_id=1, source_target_pairs={{0,28},{4,0},{8,4},{12,8},{16,12},{20,16},{24,20},{28,24},{1,29},{... | collective-permute-start | bytes 983048 | tf_op jit(solution)/shard_map/ppermute | solution.py:259
  51.7 19.8 %collective-permute-start.18 = (bf16[640,512]{1,0:T(8,128)(2,1)S(1)}, bf16[640,512]{1,0:T(8,128)(2,1)S(1)}, u32[]{:S(2)}, u32[]{:S(2)}) collective-permute-start(bf16[640,512]{1,0:T(8,128)(2,1)S(1)} %collective-permute-done.4.refs_6_.refs_9_.refs_3_), channel_id=1, source_target_pairs={{0,4},{4,8},{8,12},{12,16},{16,20},{20,24},{24,28},{28,0},{1,5},{5... | collective-permute-start | bytes 1966088 | tf_op jit(solution)/shard_map/ppermute | solution.py:256
  52.8 16.2 %collective-permute-start.21 = (bf16[320,512]{1,0:T(8,128)(2,1)S(1)}, bf16[320,512]{1,0:T(8,128)(2,1)S(1)}, u32[]{:S(2)}, u32[]{:S(2)}) collective-permute-start(bf16[320,512]{1,0:T(8,128)(2,1)S(1)} %collective-permute-done.16.refs_5_.refs_16_.refs_10_), channel_id=1, source_target_pairs={{0,4},{4,8},{8,12},{12,16},{16,20},{20,24},{24,28},{28,0},{1,5},{5... | collective-permute-start | bytes 983048 | tf_op jit(solution)/shard_map/ppermute | solution.py:256
  52.9 30.1 %collective-permute-start.8 = (bf16[512,1024]{1,0:T(8,128)(2,1)S(1)}, bf16[512,1024]{1,0:T(8,128)(2,1)S(1)}, u32[]{:S(2)}, u32[]{:S(2)}) collective-permute-start(bf16[512,1024]{1,0:T(8,128)(2,1)S(1)} %constant_dynamic-update-slice_fusion.refs_10_.refs_16_.refs_8_.refs_14_.refs_25_.refs_17_.refs_9_), channel_id=1, source_target_pairs={{0,192},{64,0},{128,64},{192,128},{1,193},{65,1},{129,65},{193,129... | collective-permute-start | bytes 3145736 | tf_op jit(solution)/shard_map/ppermute | solution.py:259
  55.7 16.7 %collective-permute-start.14 = (bf16[640,512]{1,0:T(8,128)(2,1)S(1)}, bf16[640,512]{1,0:T(8,128)(2,1)S(1)}, u32[]{:S(2)}, u32[]{:S(2)}) collective-permute-start(bf16[640,512]{1,0:T(8,128)(2,1)S(1)} %collective-permute-done.refs_3_.refs_6_.refs_2_), channel_id=1, source_target_pairs={{0,28},{4,0},{8,4},{12,8},{16,12},{20,16},{24,20},{28,24},{1,29},{... | collective-permute-start | bytes 1966088 | tf_op jit(solution)/shard_map/ppermute | solution.py:259
  58.3 30.5 %collective-permute-start.10 = (bf16[512,1024]{1,0:T(8,128)(2,1)S(1)}, bf16[512,1024]{1,0:T(8,128)(2,1)S(1)}, u32[]{:S(2)}, u32[]{:S(2)}) collective-permute-start(bf16[512,1024]{1,0:T(8,128)(2,1)S(1)} %constant_dynamic-update-slice_fusion.refs_10_.refs_16_.refs_8_.refs_14_.refs_25_.refs_17_.refs_9_), channel_id=1, source_target_pairs={{0,64},{64,128},{128,192},{192,0},{1,65},{65,129},{129,193},{193,1... | collective-permute-start | bytes 3145736 | tf_op jit(solution)/shard_map/ppermute | solution.py:256
  69.0 10.9 %collective-permute-start.17 = (bf16[640,512]{1,0:T(8,128)(2,1)S(1)}, bf16[640,512]{1,0:T(8,128)(2,1)S(1)}, u32[]{:S(2)}, u32[]{:S(2)}) collective-permute-start(bf16[640,512]{1,0:T(8,128)(2,1)S(1)} %pad_maximum_fusion.2), channel_id=1, source_target_pairs={{0,1},{1,0},{2,3},{3,2},{4,5},{5,4},{6,7},{7,6},{8,9},{9,8},{10,11... | collective-permute-start | bytes 1966088 | tf_op jit(solution)/shard_map/ppermute | solution.py:286
  71.5 17.4 %collective-permute-start.23 = (bf16[640,512]{1,0:T(8,128)(2,1)S(1)}, bf16[640,512]{1,0:T(8,128)(2,1)S(1)}, u32[]{:S(2)}, u32[]{:S(2)}) collective-permute-start(bf16[640,512]{1,0:T(8,128)(2,1)S(1)} %collective-permute-done.18.refs_4_.refs_15_.refs_5_), channel_id=1, source_target_pairs={{0,4},{4,8},{8,12},{12,16},{16,20},{20,24},{24,28},{28,0},{1,5},{5... | collective-permute-start | bytes 1966088 | tf_op jit(solution)/shard_map/ppermute | solution.py:256
  72.4 10.4 %collective-permute-start.25 = (bf16[320,512]{1,0:T(8,128)(2,1)S(1)}, bf16[320,512]{1,0:T(8,128)(2,1)S(1)}, u32[]{:S(2)}, u32[]{:S(2)}) collective-permute-start(bf16[320,512]{1,0:T(8,128)(2,1)S(1)} %collective-permute-done.20.refs_2_.refs_19_.refs_12_), channel_id=1, source_target_pairs={{0,28},{4,0},{8,4},{12,8},{16,12},{20,16},{24,20},{28,24},{1,29},{... | collective-permute-start | bytes 983048 | tf_op jit(solution)/shard_map/ppermute | solution.py:259
  80.0 18.1 %collective-permute-start.22 = (bf16[640,512]{1,0:T(8,128)(2,1)S(1)}, bf16[640,512]{1,0:T(8,128)(2,1)S(1)}, u32[]{:S(2)}, u32[]{:S(2)}) collective-permute-start(bf16[640,512]{1,0:T(8,128)(2,1)S(1)} %pad_maximum_fusion.3), channel_id=1, source_target_pairs={{0,1},{1,0},{2,3},{3,2},{4,5},{5,4},{6,7},{7,6},{8,9},{9,8},{10,11... | collective-permute-start | bytes 1966088 | tf_op jit(solution)/shard_map/ppermute | solution.py:286
  82.8 23.5 %collective-permute-start.27 = (bf16[512,1024]{1,0:T(8,128)(2,1)S(1)}, bf16[512,1024]{1,0:T(8,128)(2,1)S(1)}, u32[]{:S(2)}, u32[]{:S(2)}) collective-permute-start(bf16[512,1024]{1,0:T(8,128)(2,1)S(1)} %pad_maximum_fusion), channel_id=1, source_target_pairs={{0,64},{64,128},{128,192},{192,0},{1,65},{65,129},{129,193},{193,1... | collective-permute-start | bytes 3145736 | tf_op jit(solution)/shard_map/ppermute | solution.py:256
  82.9 25.4 %collective-permute-start.28 = (bf16[512,1024]{1,0:T(8,128)(2,1)S(1)}, bf16[512,1024]{1,0:T(8,128)(2,1)S(1)}, u32[]{:S(2)}, u32[]{:S(2)}) collective-permute-start(bf16[512,1024]{1,0:T(8,128)(2,1)S(1)} %collective-permute-done.8.refs_12_.refs_18_.refs_10_.refs_16_.refs_27_.refs_19_.refs_11_), channel_id=1, source_target_pairs={{0,192},{64,0},{128,64},{192,128},{1,193},{65,1},{129,65},{193,129... | collective-permute-start | bytes 3145736 | tf_op jit(solution)/shard_map/ppermute | solution.py:259
  88.9 15.3 %collective-permute-start.19 = (bf16[640,512]{1,0:T(8,128)(2,1)S(1)}, bf16[640,512]{1,0:T(8,128)(2,1)S(1)}, u32[]{:S(2)}, u32[]{:S(2)}) collective-permute-start(bf16[640,512]{1,0:T(8,128)(2,1)S(1)} %collective-permute-done.14.refs_1_.refs_12_.refs_4_), channel_id=1, source_target_pairs={{0,28},{4,0},{8,4},{12,8},{16,12},{20,16},{24,20},{28,24},{1,29},{... | collective-permute-start | bytes 1966088 | tf_op jit(solution)/shard_map/ppermute | solution.py:259
  88.9 35.2 %collective-permute-start.24 = (bf16[640,512]{1,0:T(8,128)(2,1)S(1)}, bf16[640,512]{1,0:T(8,128)(2,1)S(1)}, u32[]{:S(2)}, u32[]{:S(2)}) collective-permute-start(bf16[640,512]{1,0:T(8,128)(2,1)S(1)} %collective-permute-done.23.refs_4_.refs_21_.refs_7_), channel_id=1, source_target_pairs={{0,4},{4,8},{8,12},{12,16},{16,20},{20,24},{24,28},{28,0},{1,5},{5... | collective-permute-start | bytes 1966088 | tf_op jit(solution)/shard_map/ppermute | solution.py:256
  98.1 10.2 %collective-permute-start.26 = (bf16[320,512]{1,0:T(8,128)(2,1)S(1)}, bf16[320,512]{1,0:T(8,128)(2,1)S(1)}, u32[]{:S(2)}, u32[]{:S(2)}) collective-permute-start(bf16[320,512]{1,0:T(8,128)(2,1)S(1)} %collective-permute-done.25.refs_1_.refs_0_), channel_id=1, source_target_pairs={{0,1},{1,0},{2,3},{3,2},{4,5},{5,4},{6,7},{7,6},{8,9},{9,8},{10,11... | collective-permute-start | bytes 983048 | tf_op jit(solution)/shard_map/ppermute | solution.py:288
  110.0 18.7 %collective-permute-start.29 = (f32[640,512]{1,0:T(8,128)S(1)}, f32[640,512]{1,0:T(8,128)S(1)}, u32[]{:S(2)}, u32[]{:S(2)}) collective-permute-start(f32[640,512]{1,0:T(8,128)S(1)} %shard_map.32), channel_id=1, source_target_pairs={{0,2},{2,0},{1,3},{3,1},{4,6},{6,4},{5,7},{7,5},{8,10},{10,8},{9,1... | collective-permute-start | bytes 3932168 | tf_op jit(solution)/shard_map/ppermute | solution.py:328
  125.7 3.1 %collective-permute-start.30 = (f32[640,512]{1,0:T(8,128)S(1)}, f32[640,512]{1,0:T(8,128)S(1)}, u32[]{:S(2)}, u32[]{:S(2)}) collective-permute-start(f32[640,512]{1,0:T(8,128)S(1)} %shard_map.33), channel_id=1, source_target_pairs={{0,2},{2,0},{1,3},{3,1},{4,6},{6,4},{5,7},{7,5},{8,10},{10,8},{9,1... | collective-permute-start | bytes 3932168 | tf_op jit(solution)/shard_map/ppermute | solution.py:327

commit v3 on v2

--- a/solution.py
+++ b/solution.py
@@ -11,6 +11,7 @@
 FIRST = (0, 1, -1)
 SECOND = (2, -2)
 THIRD = (3, -3)
+EARLIER = FIRST + SECOND
 LATE = (4,)
 
 
@@ -38,15 +39,16 @@
     )
 
 
-def call(kernel, out_shape, blocks, tokens, weights, extra, scratch, aliases):
+def call(kernel, out_shape, blocks, tokens, weights, extra, scratch, aliases, far=()):
     rows, width = out_shape[-2:]
     depth = weights[0].shape[0]
     parts = [part for block in tokens for part, _ in block]
     return pl.pallas_call(
         kernel,
-        out_shape=jax.ShapeDtypeStruct(out_shape, jnp.float32),
+        out_shape=[jax.ShapeDtypeStruct(out_shape, jnp.float32)]
+        + [jax.ShapeDtypeStruct(shape, jnp.bfloat16) for shape in far],
         in_specs=[VMEM] * (len(extra) + len(parts)) + [ANYWHERE] * len(weights),
-        out_specs=VMEM,
+        out_specs=[VMEM] * (1 + len(far)),
         input_output_aliases=aliases,
         scratch_shapes=[pltpu.VMEM((2, depth, width), jnp.bfloat16), pltpu.SemaphoreType.DMA((2,))]
         + scratch,
@@ -59,16 +61,46 @@
     )(*extra, *parts, *weights)
 
 
-def early_product(order, total, tokens, near_weights, rows, nb, zn, yn):
+def early_product(order, total, tokens, near_weights, rows, nb, zn, yn, others=None):
     width = near_weights[0][0][0].shape[1]
     arrays = [w for half in near_weights for w, _ in half]
     known = (0, 1, 2, 3, 2 * yn - 2, 2 * yn - 1)
     totals = [] if total is None else [total]
+    blocks = tokens + ([] if others is None else others)
 
     def kernel(*refs):
-        refs, (out_ref, w_buf, sem) = refs[len(totals) : -3], refs[-3:]
-        parts, w_refs = refs[: 3 * len(order)], refs[3 * len(order) :]
+        tail = 3 if others is None else 5
+        refs, tail = refs[len(totals) : -tail], refs[-tail:]
+        if others is None:
+            out_ref, w_buf, sem = tail
+        else:
+            out_ref, far_ref, w_buf, sem, far_sem = tail
+        parts, w_refs = refs[: 3 * len(blocks)], refs[3 * len(blocks) :]
         at = places(rows, nb)
+
+        def pick(j, slot):
+            return [
+                pltpu.make_async_copy(
+                    ref.at[pl.ds(first, where.size)],
+                    far_ref.at[slot, where],
+                    far_sem.at[slot, k],
+                )
+                for k, (ref, (_, first), where) in enumerate(
+                    zip(parts[3 * j : 3 * j + 3], blocks[j], at)
+                )
+            ]
+
+        found = jnp.int32(0)
+        if others is not None:
+            for d in EARLIER + order:
+                j = order.index(d) if d in order else len(order) + EARLIER.index(d)
+                far_off = meets(d, zn, yn)[0] == yn // 2
+                for slot in range(2):
+                    @pl.when(jnp.logical_and(far_off, found == slot))
+                    def _():
+                        for one in pick(j, slot):
+                            one.start()
+                found = found + jnp.where(far_off, 1, 0)
 
         def copy(half, i, slot):
             return pltpu.make_async_copy(
@@ -107,22 +139,31 @@
             return carry
 
         lax.fori_loop(0, 2, both, 0)
-
-    blocks = 2 * len(order)
+        if others is not None:
+            for slot in range(2):
+                @pl.when(found > slot)
+                def _():
+                    for one in pick(0, slot):
+                        one.wait()
+
     aliases = {i: 0 for i in range(len(totals))}
-    return call(kernel, (2, rows, width), blocks, tokens, arrays, totals, [], aliases)
-
-
-def final_product(half, used, total, late_tokens, near_tokens, weights, rows, nb, zn, yn):
-    depth, width = weights[0][0].shape[0], total.shape[2]
-    tokens = [[block[part] for part in used] for block in late_tokens + near_tokens]
+    pairs, shape, depth = 2 * len(order), (2, rows, width), near_weights[0][0][0].shape[0]
+    if others is None:
+        return call(kernel, shape, pairs, blocks, arrays, totals, [], aliases)[0]
+    far, sems = [(2, rows, depth)], [pltpu.SemaphoreType.DMA((2, 3))]
+    return call(kernel, shape, pairs, blocks, arrays, totals, sems, aliases, far)
+
+
+def final_product(half, used, total, far, late_tokens, weights, rows, nb, zn, yn):
+    width = total.shape[2]
+    tokens = [[block[part] for part in used] for block in late_tokens]
     late, n = len(LATE), len(used)
     base = 2 * nb if used == (0,) else 0
     wanted_rows = sum((rows - 2 * nb, nb, nb)[part] for part in used)
 
-    def kernel(total_ref, *refs):
-        parts, w_refs = refs[: n * len(tokens)], refs[n * len(tokens) : -5]
-        out_ref, w_buf, w_sem, t_buf, t_sem = refs[-5:]
+    def kernel(total_ref, far_ref, *refs):
+        parts, w_refs = refs[: n * len(tokens)], refs[n * len(tokens) : -3]
+        out_ref, w_buf, w_sem = refs[-3:]
         from_total = [places(rows, nb)[part] for part in used]
         at = [pl.ds(0, where.size) if base else where for where in from_total]
 
@@ -137,28 +178,13 @@
                 def _():
                     weight_copy(i, slot).start()
 
-        def token_copies(j, slot):
-            return [
-                pltpu.make_async_copy(
-                    ref.at[pl.ds(first, where.size)], t_buf.at[slot, where], t_sem.at[slot, k]
-                )
-                for k, (ref, (_, first), where) in enumerate(
-                    zip(parts[n * j : n * j + n], tokens[j], at)
-                )
-            ]
-
         start_weight(meets(LATE[0], zn, yn)[1], 0, True)
         found, side = jnp.int32(0), [jnp.int32(0)] * 2
-        for j, d in enumerate(FIRST + SECOND + THIRD):
+        for d in EARLIER + THIRD:
             across, index = meets(d, zn, yn)
             for slot in range(2):
                 here = jnp.logical_and(across == yn // 2, found == slot)
                 side[slot] = jnp.where(here, index, side[slot])
-
-                @pl.when(here)
-                def _():
-                    for copy in token_copies(late + j, slot):
-                        copy.start()
             found = found + jnp.where(across == yn // 2, 1, 0)
 
         for j in range(late):
@@ -186,13 +212,12 @@
                 start_weight(side[1], 1 - late % 2, True)
 
             weight_copy(0, slot).wait()
-            for copy in token_copies(late, k):
-                copy.wait()
 
             def rows_of(i, carry):
                 where = pl.ds(pl.multiple_of(i * (rows // 2), rows // 2), rows // 2)
+                source = pl.ds(pl.multiple_of(base + i * (rows // 2), rows // 2), rows // 2)
                 out_ref[where, :] += jnp.dot(
-                    t_buf[k, where, :], w_buf[slot], preferred_element_type=jnp.float32
+                    far_ref[k, source, :], w_buf[slot], preferred_element_type=jnp.float32
                 )
                 return carry
 
@@ -200,13 +225,9 @@
 
         lax.fori_loop(0, found, rest, 0)
 
-    scratch = [
-        pltpu.VMEM((2, wanted_rows, depth), jnp.bfloat16),
-        pltpu.SemaphoreType.DMA((2, n)),
-    ]
     arrays = [w for w, _ in weights]
     shape = (wanted_rows, width)
-    return call(kernel, shape, 3, tokens, arrays, [total], scratch, {})
+    return call(kernel, shape, 3, tokens, arrays, [total, far], [], {})[0]
 
 
 def finish(own, lower, upper):
@@ -273,7 +294,7 @@
     b[0] = lax.dynamic_slice_in_dim(tokens, xh * nb, nb, 0)
     c[0] = lax.dynamic_slice_in_dim(tokens, (1 - xh) * nb, nb, 0)
     a[0] = tokens[2 * nb :]
-    mine, given, far = quarter(core, xh), quarter(1 - core, xh), quarter(1 - core, 1 - xh)
+    mine, given, away = quarter(core, xh), quarter(1 - core, xh), quarter(1 - core, 1 - xh)
 
     b[-1], b[1] = up("z", b[0]), down("z", b[0])
     a[-1], a[1] = up("z", a[0]), down("z", a[0])
@@ -291,7 +312,7 @@
     wa[-1], wa[1] = up("y", mine), down("y", mine)
     wb[-1], wb[1] = crossed(given, 1), crossed(given, -1)
     near = lax.ppermute(mine, "xl", ring(2, 1))
-    across = lax.ppermute(far, ("xl", "core", "xh"), [(i, 7 - i) for i in range(8)])
+    across = lax.ppermute(away, ("xl", "core", "xh"), [(i, 7 - i) for i in range(8)])
     wb[0] = lax.ppermute(given, "core", ring(2, 1))
     wo[0] = jnp.concatenate([near, across], 1)
     wo[-1], wo[1] = up("y", wo[0]), down("y", wo[0])
@@ -317,12 +338,11 @@
     near_weights = [weights(half, (0, 1, -1)) for half in range(2)]
     total = early_product(FIRST, None, first, near_weights, *sizes)
     total = early_product(SECOND, total, second, near_weights, *sizes)
-    total = early_product(THIRD, total, third, near_weights, *sizes)
+    total, far = early_product(THIRD, total, third, near_weights, *sizes, first + second)
 
     def final(half, used):
-        others = first + second + third
-        far_weights = weights(half, (0, 1, 2, -1))
-        return final_product(half, used, total, late, others, far_weights, *sizes)
+        all_weights = weights(half, (0, 1, 2, -1))
+        return final_product(half, used, total, far, late, all_weights, *sizes)
 
     upper = lax.ppermute(final(1, (0,)), "core", ring(2, 1))
     lower = lax.ppermute(final(1, (1, 2)), "core", ring(2, 1))

time: 131 us -> 132 us (level)
  waiting for transfers between devices: 39.8 us -> 58.4 us
  starting transfers between devices: 68.4 us -> 50.8 us
    ppermute x10, waiting for transfers between devices: 8.01 us -> 23 us  [down(): return lax.ppermute(a, axis, ring(lax.axis_size(axis), -1))]
    ppermute x1, starting transfers between devices: 14.1 us -> 3.16 us  [per_device(): lower = lax.ppermute(final(1, (1, 2)), 'core', ring(2, 1))]
    ppermute x3, starting transfers between devices: 7.7 us -> 0.95 us  [per_device(): pair = lax.ppermute(jnp.concatenate([b[-d], b[d]], 0), 'xh', ring(2, 1))]
    ppermute x2, starting transfers between devices: 3.56 us -> 6.83 us  [crossed(): return lax.ppermute(a, ('y', 'core'), pairs)]
    ppermute x10, starting transfers between devices: 32.5 us -> 29.4 us  [down(): return lax.ppermute(a, axis, ring(lax.axis_size(axis), -1))]
    ppermute x1, starting transfers between devices: 0.16 us -> 2.72 us  [per_device(): upper = lax.ppermute(final(1, (0,)), 'core', ring(2, 1))]
    ppermute x2, waiting for transfers between devices: 4.31 us -> 6.77 us  [crossed(): return lax.ppermute(a, ('y', 'core'), pairs)]
    ppermute x1, starting transfers between devices: 2.21 us -> 0.01 us  [per_device(): c[0], c[4] = ((c[0], 0), (lax.ppermute(b[4], 'xh', ring(2, 1)), 0))]
  transfers between devices with their start and end apart: 31 -> 31, of which waited for: 13 -> 13; matrix products, arithmetic and copies ran while one was open for 0% -> 2% of each run, Pallas kernels for 14% -> 13%
where the time goes in v3:
time: 132 us
  waiting for transfers between devices  58.4 us (44%)
  starting transfers between devices  50.8 us (38%)
  Pallas kernels  19 us (14%)
  local copies, waits for them, and re-layouts  2.85 us (2%)
    ppermute x10, starting transfers between devices, down(): return lax.ppermute(a, axis, ring(lax.axis_size(axis), -1))  29.4 us
    ppermute x10, waiting for transfers between devices, down(): return lax.ppermute(a, axis, ring(lax.axis_size(axis), -1))  23 us
    ppermute x10, waiting for transfers between devices, up(): return lax.ppermute(a, axis, ring(lax.axis_size(axis), 1))  19.2 us
    pallas_call x6, Pallas kernels, call(): pl.pallas_call(kernel, out_shape=[jax.ShapeDtypeStruct(out_shape, jnp.flo...  17.7 us
    ppermute x2, starting transfers between devices, crossed(): return lax.ppermute(a, ('y', 'core'), pairs)  6.83 us
    ppermute x2, waiting for transfers between devices, crossed(): return lax.ppermute(a, ('y', 'core'), pairs)  6.77 us
    ppermute x3, waiting for transfers between devices, per_device(): pair = lax.ppermute(jnp.concatenate([b[-d], b[d]], 0), 'xh', ring(2, 1))  5.19 us
    ppermute x1, starting transfers between devices, per_device(): lower = lax.ppermute(final(1, (1, 2)), 'core', ring(2, 1))  3.16 us
  transfers between devices with their start and end apart: 31, of which 13 were waited for; matrix products, arithmetic and copies ran while one was open for 2% of the time, Pallas kernels for 13%

profile of v3, /device:TPU:1, one launch (start us, length us, event | category | flops | bytes accessed | tf_op | source)
XLA Modules:
  0.0 131.7 jit_solution(1821173206979252194)
XLA Ops:
  0.0 1.1 constant_dynamic-slice_fusion
  1.1 6.5 %collective-permute-start.1 = (bf16[320,512]{1,0:T(8,128)(2,1)S(1)}, bf16[320,512]{1,0:T(8,128)(2,1)S(1)}, u32[]{:S(2)}, u32[]{:S(2)}) collective-permute-start(bf16[320,512]{1,0:T(8,128)(2,1)S(1)} %get-tuple-element.13.refs_1_.refs_8_), channel_id=1, source_target_pairs={{0,28},{4,0},{8,4},{12,8},{16,12},{20,16},{24,20},{28,24},{1,29},{... | collective-permute-start | bytes 983048 | tf_op jit(solution)/shard_map/ppermute | solution.py:280
  7.6 1.6 %fusion = (bf16[512,512]{1,0:T(8,128)(2,1)S(1)}, bf16[512,512]{1,0:T(8,128)(2,1)S(1)}, bf16[512,512]{1,0:T(8,128)(2,1)S(1)}) fusion(bf16[1024,1024]{1,0:T(8,128)(2,1)} %param.3, s32[]{:T(128)S(6)} %select_n.24, s32[]{:T(128)S(6)} %select_n.23, s32[]{:T(128)S(6)} %select_n.22, s32[]{:T(128)S(6)} %select_n.25), kind=kLoop, calls=%fused_computation.8 | loop fusion | bytes 3145744 | tf_op jit(solution)/shard_map/dynamic_slice | solution.py:289
  9.2 1.3 collective-permute-start.5
  10.5 2.9 %collective-permute-start.6 = (bf16[512,512]{1,0:T(8,128)(2,1)S(1)}, bf16[512,512]{1,0:T(8,128)(2,1)S(1)}, u32[]{:S(2)}, u32[]{:S(2)}) collective-permute-start(bf16[512,512]{1,0:T(8,128)(2,1)S(1)} %get-tuple-element.11), channel_id=1, source_target_pairs={{0,35},{1,34},{2,33},{3,32},{32,3},{33,2},{34,1},{35,0},{4,39},{5,... | collective-permute-start | bytes 1572872 | tf_op jit(solution)/shard_map/ppermute | solution.py:315
  13.4 1.3 collective-permute-start.9
  14.7 2.0 %collective-permute-start.7 = (bf16[512,512]{1,0:T(8,128)(2,1)S(1)}, bf16[512,512]{1,0:T(8,128)(2,1)S(1)}, u32[]{:S(2)}, u32[]{:S(2)}) collective-permute-start(bf16[512,512]{1,0:T(8,128)(2,1)S(1)} %get-tuple-element.10.refs_9_.refs_7_.refs_22_.refs_3_), channel_id=1, source_target_pairs={{0,192},{64,0},{128,64},{192,128},{1,193},{65,1},{129,65},{193,129... | collective-permute-start | bytes 1572872 | tf_op jit(solution)/shard_map/ppermute | solution.py:280
  16.7 3.0 %collective-permute-done.2.refs_7_.refs_14_ = bf16[320,512]{1,0:T(8,128)(2,1)S(1)} collective-permute-done((bf16[320,512]{1,0:T(8,128)(2,1)S(1)}, bf16[320,512]{1,0:T(8,128)(2,1)S(1)}, u32[]{:S(2)}, u32[]{:S(2)}) %collective-permute-start.2) | collective-permute-done | bytes 327712 | tf_op jit(solution)/shard_map/ppermute | solution.py:277
  19.7 3.3 %collective-permute-start.13 = (bf16[512,512]{1,0:T(8,128)(2,1)S(1)}, bf16[512,512]{1,0:T(8,128)(2,1)S(1)}, u32[]{:S(2)}, u32[]{:S(2)}) collective-permute-start(bf16[512,512]{1,0:T(8,128)(2,1)S(1)} %get-tuple-element.9), channel_id=1, source_target_pairs={{0,66},{2,64},{64,130},{66,128},{128,194},{130,192},{192,2},{194,0... | collective-permute-start | bytes 1572872 | tf_op jit(solution)/shard_map/ppermute | solution.py:286
  23.0 0.6 collective-permute-start.11
  23.6 2.1 %collective-permute-done.6 = bf16[512,512]{1,0:T(8,128)(2,1)S(1)} collective-permute-done((bf16[512,512]{1,0:T(8,128)(2,1)S(1)}, bf16[512,512]{1,0:T(8,128)(2,1)S(1)}, u32[]{:S(2)}, u32[]{:S(2)}) %collective-permute-start.6) | collective-permute-done | bytes 524320 | tf_op jit(solution)/shard_map/ppermute | solution.py:315
  25.6 3.6 %collective-permute-start.12 = (bf16[512,512]{1,0:T(8,128)(2,1)S(1)}, bf16[512,512]{1,0:T(8,128)(2,1)S(1)}, u32[]{:S(2)}, u32[]{:S(2)}) collective-permute-start(bf16[512,512]{1,0:T(8,128)(2,1)S(1)} %get-tuple-element.9), channel_id=1, source_target_pairs={{0,194},{2,192},{64,2},{66,0},{128,66},{130,64},{192,130},{194,128... | collective-permute-start | bytes 1572872 | tf_op jit(solution)/shard_map/ppermute | solution.py:286
  29.3 0.1 collective-permute-start.4
  29.4 3.0 %collective-permute-start = (bf16[640,512]{1,0:T(8,128)(2,1)S(1)}, bf16[640,512]{1,0:T(8,128)(2,1)S(1)}, u32[]{:S(2)}, u32[]{:S(2)}) collective-permute-start(bf16[640,512]{1,0:T(8,128)(2,1)S(1)} %slice.3.refs_0_.refs_7_), channel_id=1, source_target_pairs={{0,28},{4,0},{8,4},{12,8},{16,12},{20,16},{24,20},{28,24},{1,29},{... | collective-permute-start | bytes 1966088 | tf_op jit(solution)/shard_map/ppermute | solution.py:280
  32.4 6.8 %collective-permute-done.13.refs_19_.refs_17_.refs_32_.refs_8_.refs_7_ = bf16[512,512]{1,0:T(8,128)(2,1)S(1)} collective-permute-done((bf16[512,512]{1,0:T(8,128)(2,1)S(1)}, bf16[512,512]{1,0:T(8,128)(2,1)S(1)}, u32[]{:S(2)}, u32[]{:S(2)}) %collective-permute-start.13) | collective-permute-done | bytes 524320 | tf_op jit(solution)/shard_map/ppermute | solution.py:286
  39.2 0.9 collective-permute-start.3
  40.1 3.0 %collective-permute-start.15 = (bf16[320,512]{1,0:T(8,128)(2,1)S(1)}, bf16[320,512]{1,0:T(8,128)(2,1)S(1)}, u32[]{:S(2)}, u32[]{:S(2)}) collective-permute-start(bf16[320,512]{1,0:T(8,128)(2,1)S(1)} %collective-permute-done.1.refs_4_.refs_11_), channel_id=1, source_target_pairs={{0,28},{4,0},{8,4},{12,8},{16,12},{20,16},{24,20},{28,24},{1,29},{... | collective-permute-start | bytes 983048 | tf_op jit(solution)/shard_map/ppermute | solution.py:280
  43.0 0.1 constant_dynamic-update-slice_fusion.1
  43.1 4.2 %collective-permute-done.4.refs_6_.refs_13_ = bf16[640,512]{1,0:T(8,128)(2,1)S(1)} collective-permute-done((bf16[640,512]{1,0:T(8,128)(2,1)S(1)}, bf16[640,512]{1,0:T(8,128)(2,1)S(1)}, u32[]{:S(2)}, u32[]{:S(2)}) %collective-permute-start.4) | collective-permute-done | bytes 655392 | tf_op jit(solution)/shard_map/ppermute | solution.py:277
  47.3 6.3 %collective-permute-done.15.refs_2_.refs_17_ = bf16[320,512]{1,0:T(8,128)(2,1)S(1)} collective-permute-done((bf16[320,512]{1,0:T(8,128)(2,1)S(1)}, bf16[320,512]{1,0:T(8,128)(2,1)S(1)}, u32[]{:S(2)}, u32[]{:S(2)}) %collective-permute-start.15) | collective-permute-done | bytes 327712 | tf_op jit(solution)/shard_map/ppermute | solution.py:280
  53.6 3.4 %collective-permute-start.20 = (bf16[320,512]{1,0:T(8,128)(2,1)S(1)}, bf16[320,512]{1,0:T(8,128)(2,1)S(1)}, u32[]{:S(2)}, u32[]{:S(2)}) collective-permute-start(bf16[320,512]{1,0:T(8,128)(2,1)S(1)} %collective-permute-done.15.refs_2_.refs_17_), channel_id=1, source_target_pairs={{0,28},{4,0},{8,4},{12,8},{16,12},{20,16},{24,20},{28,24},{1,29},{... | collective-permute-start | bytes 983048 | tf_op jit(solution)/shard_map/ppermute | solution.py:280
  57.0 0.1 constant_dynamic-update-slice_fusion.refs_10_.refs_16_.refs_8_.refs_14_.refs_23_.refs_29_.refs_4_.refs_3_.refs_2_
  57.1 0.3 collective-permute-start.8
  57.4 0.1 collective-permute-start.21
  57.5 1.4 %collective-permute-start.10 = (bf16[512,1024]{1,0:T(8,128)(2,1)S(1)}, bf16[512,1024]{1,0:T(8,128)(2,1)S(1)}, u32[]{:S(2)}, u32[]{:S(2)}) collective-permute-start(bf16[512,1024]{1,0:T(8,128)(2,1)S(1)} %constant_dynamic-update-slice_fusion.refs_10_.refs_16_.refs_8_.refs_14_.refs_23_.refs_29_.refs_4_.refs_3_.r, ...), channel_id=1, source_target_pairs={{0,64},{64,128},{128,192},{192,0},{1,65},{65,129},{129,193},{193,1... | collective-permute-start | bytes 3145736 | tf_op jit(solution)/shard_map/ppermute | solution.py:277
  59.0 4.4 %collective-permute-done.20.refs_2_ = bf16[320,512]{1,0:T(8,128)(2,1)S(1)} collective-permute-done((bf16[320,512]{1,0:T(8,128)(2,1)S(1)}, bf16[320,512]{1,0:T(8,128)(2,1)S(1)}, u32[]{:S(2)}, u32[]{:S(2)}) %collective-permute-start.20) | collective-permute-done | bytes 327712 | tf_op jit(solution)/shard_map/ppermute | solution.py:280
  63.3 12.0 %collective-permute-done.21.refs_5_ = bf16[320,512]{1,0:T(8,128)(2,1)S(1)} collective-permute-done((bf16[320,512]{1,0:T(8,128)(2,1)S(1)}, bf16[320,512]{1,0:T(8,128)(2,1)S(1)}, u32[]{:S(2)}, u32[]{:S(2)}) %collective-permute-start.21) | collective-permute-done | bytes 327712 | tf_op jit(solution)/shard_map/ppermute | solution.py:277
  75.3 1.8 %collective-permute-start.14 = (bf16[640,512]{1,0:T(8,128)(2,1)S(1)}, bf16[640,512]{1,0:T(8,128)(2,1)S(1)}, u32[]{:S(2)}, u32[]{:S(2)}) collective-permute-start(bf16[640,512]{1,0:T(8,128)(2,1)S(1)} %collective-permute-done.refs_3_.refs_10_), channel_id=1, source_target_pairs={{0,28},{4,0},{8,4},{12,8},{16,12},{20,16},{24,20},{28,24},{1,29},{... | collective-permute-start | bytes 1966088 | tf_op jit(solution)/shard_map/ppermute | solution.py:280
  77.1 2.4 %collective-permute-done.17.refs_3_.refs_6_.refs_18_.refs_21_ = bf16[640,512]{1,0:T(8,128)(2,1)S(1)} collective-permute-done((bf16[640,512]{1,0:T(8,128)(2,1)S(1)}, bf16[640,512]{1,0:T(8,128)(2,1)S(1)}, u32[]{:S(2)}, u32[]{:S(2)}) %collective-permute-start.17) | collective-permute-done | bytes 655392 | tf_op jit(solution)/shard_map/ppermute | solution.py:307
  79.5 3.4 %collective-permute-start.25 = (bf16[320,512]{1,0:T(8,128)(2,1)S(1)}, bf16[320,512]{1,0:T(8,128)(2,1)S(1)}, u32[]{:S(2)}, u32[]{:S(2)}) collective-permute-start(bf16[320,512]{1,0:T(8,128)(2,1)S(1)} %collective-permute-done.20.refs_2_), channel_id=1, source_target_pairs={{0,28},{4,0},{8,4},{12,8},{16,12},{20,16},{24,20},{28,24},{1,29},{... | collective-permute-start | bytes 983048 | tf_op jit(solution)/shard_map/ppermute | solution.py:280
  82.9 0.1 pad_maximum_fusion
  83.1 8.0 %collective-permute-done.14.refs_1_.refs_16_ = bf16[640,512]{1,0:T(8,128)(2,1)S(1)} collective-permute-done((bf16[640,512]{1,0:T(8,128)(2,1)S(1)}, bf16[640,512]{1,0:T(8,128)(2,1)S(1)}, u32[]{:S(2)}, u32[]{:S(2)}) %collective-permute-start.14) | collective-permute-done | bytes 655392 | tf_op jit(solution)/shard_map/ppermute | solution.py:280
  91.1 2.7 %collective-permute-start.28 = (bf16[512,1024]{1,0:T(8,128)(2,1)S(1)}, bf16[512,1024]{1,0:T(8,128)(2,1)S(1)}, u32[]{:S(2)}, u32[]{:S(2)}) collective-permute-start(bf16[512,1024]{1,0:T(8,128)(2,1)S(1)} %collective-permute-done.8.refs_12_.refs_18_.refs_10_.refs_16_.refs_25_.refs_31_.refs_6_.refs_5_.refs_4_), channel_id=1, source_target_pairs={{0,192},{64,0},{128,64},{192,128},{1,193},{65,1},{129,65},{193,129... | collective-permute-start | bytes 3145736 | tf_op jit(solution)/shard_map/ppermute | solution.py:280
  93.8 4.3 %collective-permute-done.25.refs_1_.refs_0_ = bf16[320,512]{1,0:T(8,128)(2,1)S(1)} collective-permute-done((bf16[320,512]{1,0:T(8,128)(2,1)S(1)}, bf16[320,512]{1,0:T(8,128)(2,1)S(1)}, u32[]{:S(2)}, u32[]{:S(2)}) %collective-permute-start.25) | collective-permute-done | bytes 327712 | tf_op jit(solution)/shard_map/ppermute | solution.py:280
  98.1 0.1 collective-permute-start.22
  98.2 3.4 %collective-permute-start.19 = (bf16[640,512]{1,0:T(8,128)(2,1)S(1)}, bf16[640,512]{1,0:T(8,128)(2,1)S(1)}, u32[]{:S(2)}, u32[]{:S(2)}) collective-permute-start(bf16[640,512]{1,0:T(8,128)(2,1)S(1)} %collective-permute-done.14.refs_1_.refs_16_), channel_id=1, source_target_pairs={{0,28},{4,0},{8,4},{12,8},{16,12},{20,16},{24,20},{28,24},{1,29},{... | collective-permute-start | bytes 1966088 | tf_op jit(solution)/shard_map/ppermute | solution.py:280
  101.6 6.3 %shard_map.28.refs_0_ = f32[2,1280,512]{2,1,0:T(8,128)S(1)} custom-call(bf16[640,512]{1,0:T(8,128)(2,1)S(1)} %slice.3.refs_0_.refs_7_, bf16[320,512]{1,0:T(8,128)(2,1)S(1)} %get-tuple-element.13.refs_1_.refs_8_, bf16[320,512]{1,0:T(8,128)(2,1)S(1)} %get-tuple-element.12.refs_2_.refs_9_, bf16[640,512]{1,0:T(8,128)(2,1)S(1)} %collective-permute-done.refs_3_.refs_10_, ...), custom_call_target="tpu_custom_call" | custom-call | flops 4026531840 | bytes 13631488 | tf_op jit(solution)/shard_map/pallas_call | solution.py:46
  107.9 3.9 %shard_map.29.refs_0_ = f32[2,1280,512]{2,1,0:T(8,128)S(1)} custom-call(f32[2,1280,512]{2,1,0:T(8,128)S(1)} %shard_map.28.refs_0_, bf16[640,512]{1,0:T(8,128)(2,1)S(1)} %collective-permute-done.14.refs_1_.refs_16_, bf16[320,512]{1,0:T(8,128)(2,1)S(1)} %collective-permute-done.15.refs_2_.refs_17_, ...), custom_call_target="tpu_custom_call", output_to_operand_aliasing={{}: (0, {})} | custom-call | flops 2684354560 | bytes 9961472 | tf_op jit(solution)/shard_map/pallas_call | solution.py:46
  111.8 2.8 %collective-permute-done.22.refs_3_.refs_6_ = bf16[640,512]{1,0:T(8,128)(2,1)S(1)} collective-permute-done((bf16[640,512]{1,0:T(8,128)(2,1)S(1)}, bf16[640,512]{1,0:T(8,128)(2,1)S(1)}, u32[]{:S(2)}, u32[]{:S(2)}) %collective-permute-start.22) | collective-permute-done | bytes 655392 | tf_op jit(solution)/shard_map/ppermute | solution.py:307
  114.5 2.7 %shard_map.30 = (f32[2,1280,512]{2,1,0:T(8,128)S(1)}, bf16[2,1280,512]{2,1,0:T(8,128)(2,1)S(1)}) custom-call(f32[2,1280,512]{2,1,0:T(8,128)S(1)} %shard_map.29.refs_0_, bf16[640,512]{1,0:T(8,128)(2,1)S(1)} %collective-permute-done.19.refs_1_, bf16[320,512]{1,0:T(8,128)(2,1)S(1)} %collective-permute-done.20.refs_2_, ...), custom_call_target="tpu_custom_call", output_to_operand_aliasing={{0}: (0, {})} | custom-call | flops 2684354560 | bytes 9961472 | tf_op jit(solution)/shard_map/pallas_call | solution.py:46
  117.3 1.4 %shard_map.33 = f32[640,512]{1,0:T(8,128)S(1)} custom-call(f32[2,1280,512]{2,1,0:T(8,128)S(1)} %get-tuple-element.7.total_ref, bf16[2,1280,512]{2,1,0:T(8,128)(2,1)S(1)} %get-tuple-element.8.far_ref, bf16[640,512]{1,0:T(8,128)(2,1)S(1)} %collective-permute-done.24.refs_0_, ...), custom_call_target="tpu_custom_call" | custom-call | flops 1006632960 | bytes 4849664 | tf_op jit(solution)/shard_map/pallas_call | solution.py:46
  118.7 2.7 %collective-permute-start.30 = (f32[640,512]{1,0:T(8,128)S(1)}, f32[640,512]{1,0:T(8,128)S(1)}, u32[]{:S(2)}, u32[]{:S(2)}) collective-permute-start(f32[640,512]{1,0:T(8,128)S(1)} %shard_map.33), channel_id=1, source_target_pairs={{0,2},{2,0},{1,3},{3,1},{4,6},{6,4},{5,7},{7,5},{8,10},{10,8},{9,1... | collective-permute-start | bytes 3932168 | tf_op jit(solution)/shard_map/ppermute | solution.py:347
  121.4 1.7 %collective-permute-done.26.refs_2_.refs_1_ = bf16[320,512]{1,0:T(8,128)(2,1)S(1)} collective-permute-done((bf16[320,512]{1,0:T(8,128)(2,1)S(1)}, bf16[320,512]{1,0:T(8,128)(2,1)S(1)}, u32[]{:S(2)}, u32[]{:S(2)}) %collective-permute-start.26) | collective-permute-done | bytes 327712 | tf_op jit(solution)/shard_map/ppermute | solution.py:309
  123.1 1.3 shard_map.32
  124.4 3.2 %collective-permute-start.29 = (f32[640,512]{1,0:T(8,128)S(1)}, f32[640,512]{1,0:T(8,128)S(1)}, u32[]{:S(2)}, u32[]{:S(2)}) collective-permute-start(f32[640,512]{1,0:T(8,128)S(1)} %shard_map.32), channel_id=1, source_target_pairs={{0,2},{2,0},{1,3},{3,1},{4,6},{6,4},{5,7},{7,5},{8,10},{10,8},{9,1... | collective-permute-start | bytes 3932168 | tf_op jit(solution)/shard_map/ppermute | solution.py:348
  127.6 2.2 %shard_map.31.own_ref = f32[1280,512]{1,0:T(8,128)S(1)} custom-call(f32[2,1280,512]{2,1,0:T(8,128)S(1)} %get-tuple-element.7.total_ref, bf16[2,1280,512]{2,1,0:T(8,128)(2,1)S(1)} %get-tuple-element.8.far_ref, bf16[640,512]{1,0:T(8,128)(2,1)S(1)} %collective-permute-done.24.refs_0_, bf16[320,512]{1,0:T(8,128)(2,1)S(1)} %collective-permute-done.25.refs_1_.refs_0_, ...), custom_call_target="tpu_custom_call" | custom-call | flops 2013265920 | bytes 8126464 | tf_op jit(solution)/shard_map/pallas_call | solution.py:46
  129.8 0.5 collective-permute-done.29.lower_ref
  130.2 1.3 finish.1
  (32 shorter events, 0.2 us)
Async XLA Ops:
  1.1 13.6 %collective-permute-start.1 = (bf16[320,512]{1,0:T(8,128)(2,1)S(1)}, bf16[320,512]{1,0:T(8,128)(2,1)S(1)}, u32[]{:S(2)}, u32[]{:S(2)}) collective-permute-start(bf16[320,512]{1,0:T(8,128)(2,1)S(1)} %get-tuple-element.13.refs_1_.refs_8_), channel_id=1, source_target_pairs={{0,28},{4,0},{8,4},{12,8},{16,12},{20,16},{24,20},{28,24},{1,29},{... | collective-permute-start | bytes 983048 | tf_op jit(solution)/shard_map/ppermute | solution.py:280
  7.6 21.6 %copy-start = (bf16[1280,512]{1,0:T(8,128)(2,1)S(1)}, bf16[1280,512]{1,0:T(8,128)(2,1)}, u32[]{:S(2)}) copy-start(bf16[1280,512]{1,0:T(8,128)(2,1)} %param.2) | copy-start | bytes 3932164
  9.2 13.8 %collective-permute-start.5 = (bf16[512,512]{1,0:T(8,128)(2,1)S(1)}, bf16[512,512]{1,0:T(8,128)(2,1)S(1)}, u32[]{:S(2)}, u32[]{:S(2)}) collective-permute-start(bf16[512,512]{1,0:T(8,128)(2,1)S(1)} %get-tuple-element.10.refs_9_.refs_7_.refs_22_.refs_3_), channel_id=1, source_target_pairs={{0,32},{32,0},{1,33},{33,1},{2,34},{34,2},{3,35},{35,3},{4,36},{36... | collective-permute-start | bytes 1572872 | tf_op jit(solution)/shard_map/ppermute | solution.py:314
  10.5 9.2 %collective-permute-start.2 = (bf16[320,512]{1,0:T(8,128)(2,1)S(1)}, bf16[320,512]{1,0:T(8,128)(2,1)S(1)}, u32[]{:S(2)}, u32[]{:S(2)}) collective-permute-start(bf16[320,512]{1,0:T(8,128)(2,1)S(1)} %get-tuple-element.13.refs_1_.refs_8_), channel_id=1, source_target_pairs={{0,4},{4,8},{8,12},{12,16},{16,20},{20,24},{24,28},{28,0},{1,5},{5... | collective-permute-start | bytes 983048 | tf_op jit(solution)/shard_map/ppermute | solution.py:277
  10.5 15.2 %collective-permute-start.6 = (bf16[512,512]{1,0:T(8,128)(2,1)S(1)}, bf16[512,512]{1,0:T(8,128)(2,1)S(1)}, u32[]{:S(2)}, u32[]{:S(2)}) collective-permute-start(bf16[512,512]{1,0:T(8,128)(2,1)S(1)} %get-tuple-element.11), channel_id=1, source_target_pairs={{0,35},{1,34},{2,33},{3,32},{32,3},{33,2},{34,1},{35,0},{4,39},{5,... | collective-permute-start | bytes 1572872 | tf_op jit(solution)/shard_map/ppermute | solution.py:315
  13.4 15.9 %collective-permute-start.9 = (bf16[512,512]{1,0:T(8,128)(2,1)S(1)}, bf16[512,512]{1,0:T(8,128)(2,1)S(1)}, u32[]{:S(2)}, u32[]{:S(2)}) collective-permute-start(bf16[512,512]{1,0:T(8,128)(2,1)S(1)} %get-tuple-element.10.refs_9_.refs_7_.refs_22_.refs_3_), channel_id=1, source_target_pairs={{0,64},{64,128},{128,192},{192,0},{1,65},{65,129},{129,193},{193,1... | collective-permute-start | bytes 1572872 | tf_op jit(solution)/shard_map/ppermute | solution.py:277
  14.7 14.7 %collective-permute-start.7 = (bf16[512,512]{1,0:T(8,128)(2,1)S(1)}, bf16[512,512]{1,0:T(8,128)(2,1)S(1)}, u32[]{:S(2)}, u32[]{:S(2)}) collective-permute-start(bf16[512,512]{1,0:T(8,128)(2,1)S(1)} %get-tuple-element.10.refs_9_.refs_7_.refs_22_.refs_3_), channel_id=1, source_target_pairs={{0,192},{64,0},{128,64},{192,128},{1,193},{65,1},{129,65},{193,129... | collective-permute-start | bytes 1572872 | tf_op jit(solution)/shard_map/ppermute | solution.py:280
  19.7 19.5 %collective-permute-start.13 = (bf16[512,512]{1,0:T(8,128)(2,1)S(1)}, bf16[512,512]{1,0:T(8,128)(2,1)S(1)}, u32[]{:S(2)}, u32[]{:S(2)}) collective-permute-start(bf16[512,512]{1,0:T(8,128)(2,1)S(1)} %get-tuple-element.9), channel_id=1, source_target_pairs={{0,66},{2,64},{64,130},{66,128},{128,194},{130,192},{192,2},{194,0... | collective-permute-start | bytes 1572872 | tf_op jit(solution)/shard_map/ppermute | solution.py:286
  23.0 17.1 %collective-permute-start.11 = (bf16[512,512]{1,0:T(8,128)(2,1)S(1)}, bf16[512,512]{1,0:T(8,128)(2,1)S(1)}, u32[]{:S(2)}, u32[]{:S(2)}) collective-permute-start(bf16[512,512]{1,0:T(8,128)(2,1)S(1)} %get-tuple-element.9), channel_id=1, source_target_pairs={{0,2},{2,0},{1,3},{3,1},{4,6},{6,4},{5,7},{7,5},{8,10},{10,8},{9,1... | collective-permute-start | bytes 1572872 | tf_op jit(solution)/shard_map/ppermute | solution.py:316
  25.6 17.4 %collective-permute-start.12 = (bf16[512,512]{1,0:T(8,128)(2,1)S(1)}, bf16[512,512]{1,0:T(8,128)(2,1)S(1)}, u32[]{:S(2)}, u32[]{:S(2)}) collective-permute-start(bf16[512,512]{1,0:T(8,128)(2,1)S(1)} %get-tuple-element.9), channel_id=1, source_target_pairs={{0,194},{2,192},{64,2},{66,0},{128,66},{130,64},{192,130},{194,128... | collective-permute-start | bytes 1572872 | tf_op jit(solution)/shard_map/ppermute | solution.py:286
  29.3 18.1 %collective-permute-start.4 = (bf16[640,512]{1,0:T(8,128)(2,1)S(1)}, bf16[640,512]{1,0:T(8,128)(2,1)S(1)}, u32[]{:S(2)}, u32[]{:S(2)}) collective-permute-start(bf16[640,512]{1,0:T(8,128)(2,1)S(1)} %slice.3.refs_0_.refs_7_), channel_id=1, source_target_pairs={{0,4},{4,8},{8,12},{12,16},{16,20},{20,24},{24,28},{28,0},{1,5},{5... | collective-permute-start | bytes 1966088 | tf_op jit(solution)/shard_map/ppermute | solution.py:277
  29.4 27.7 %collective-permute-start = (bf16[640,512]{1,0:T(8,128)(2,1)S(1)}, bf16[640,512]{1,0:T(8,128)(2,1)S(1)}, u32[]{:S(2)}, u32[]{:S(2)}) collective-permute-start(bf16[640,512]{1,0:T(8,128)(2,1)S(1)} %slice.3.refs_0_.refs_7_), channel_id=1, source_target_pairs={{0,28},{4,0},{8,4},{12,8},{16,12},{20,16},{24,20},{28,24},{1,29},{... | collective-permute-start | bytes 1966088 | tf_op jit(solution)/shard_map/ppermute | solution.py:280
  39.2 18.3 %collective-permute-start.3 = (bf16[640,512]{1,0:T(8,128)(2,1)S(1)}, bf16[640,512]{1,0:T(8,128)(2,1)S(1)}, u32[]{:S(2)}, u32[]{:S(2)}) collective-permute-start(bf16[640,512]{1,0:T(8,128)(2,1)S(1)} %pad_maximum_fusion.1), channel_id=1, source_target_pairs={{0,1},{1,0},{2,3},{3,2},{4,5},{5,4},{6,7},{7,6},{8,9},{9,8},{10,11... | collective-permute-start | bytes 1966088 | tf_op jit(solution)/shard_map/ppermute | solution.py:307
  40.1 13.5 %collective-permute-start.15 = (bf16[320,512]{1,0:T(8,128)(2,1)S(1)}, bf16[320,512]{1,0:T(8,128)(2,1)S(1)}, u32[]{:S(2)}, u32[]{:S(2)}) collective-permute-start(bf16[320,512]{1,0:T(8,128)(2,1)S(1)} %collective-permute-done.1.refs_4_.refs_11_), channel_id=1, source_target_pairs={{0,28},{4,0},{8,4},{12,8},{16,12},{20,16},{24,20},{28,24},{1,29},{... | collective-permute-start | bytes 983048 | tf_op jit(solution)/shard_map/ppermute | solution.py:280
  43.0 14.3 %collective-permute-start.16 = (bf16[320,512]{1,0:T(8,128)(2,1)S(1)}, bf16[320,512]{1,0:T(8,128)(2,1)S(1)}, u32[]{:S(2)}, u32[]{:S(2)}) collective-permute-start(bf16[320,512]{1,0:T(8,128)(2,1)S(1)} %collective-permute-done.2.refs_7_.refs_14_), channel_id=1, source_target_pairs={{0,4},{4,8},{8,12},{12,16},{16,20},{20,24},{24,28},{28,0},{1,5},{5... | collective-permute-start | bytes 983048 | tf_op jit(solution)/shard_map/ppermute | solution.py:277
  47.3 29.8 %collective-permute-start.18 = (bf16[640,512]{1,0:T(8,128)(2,1)S(1)}, bf16[640,512]{1,0:T(8,128)(2,1)S(1)}, u32[]{:S(2)}, u32[]{:S(2)}) collective-permute-start(bf16[640,512]{1,0:T(8,128)(2,1)S(1)} %collective-permute-done.4.refs_6_.refs_13_), channel_id=1, source_target_pairs={{0,4},{4,8},{8,12},{12,16},{16,20},{20,24},{24,28},{28,0},{1,5},{5... | collective-permute-start | bytes 1966088 | tf_op jit(solution)/shard_map/ppermute | solution.py:277
  53.6 9.7 %collective-permute-start.20 = (bf16[320,512]{1,0:T(8,128)(2,1)S(1)}, bf16[320,512]{1,0:T(8,128)(2,1)S(1)}, u32[]{:S(2)}, u32[]{:S(2)}) collective-permute-start(bf16[320,512]{1,0:T(8,128)(2,1)S(1)} %collective-permute-done.15.refs_2_.refs_17_), channel_id=1, source_target_pairs={{0,28},{4,0},{8,4},{12,8},{16,12},{20,16},{24,20},{28,24},{1,29},{... | collective-permute-start | bytes 983048 | tf_op jit(solution)/shard_map/ppermute | solution.py:280
  57.1 34.0 %collective-permute-start.8 = (bf16[512,1024]{1,0:T(8,128)(2,1)S(1)}, bf16[512,1024]{1,0:T(8,128)(2,1)S(1)}, u32[]{:S(2)}, u32[]{:S(2)}) collective-permute-start(bf16[512,1024]{1,0:T(8,128)(2,1)S(1)} %constant_dynamic-update-slice_fusion.refs_10_.refs_16_.refs_8_.refs_14_.refs_23_.refs_29_.refs_4_.refs_3_.re, ...), channel_id=1, source_target_pairs={{0,192},{64,0},{128,64},{192,128},{1,193},{65,1},{129,65},{193,129... | collective-permute-start | bytes 3145736 | tf_op jit(solution)/shard_map/ppermute | solution.py:280
  57.4 17.9 %collective-permute-start.21 = (bf16[320,512]{1,0:T(8,128)(2,1)S(1)}, bf16[320,512]{1,0:T(8,128)(2,1)S(1)}, u32[]{:S(2)}, u32[]{:S(2)}) collective-permute-start(bf16[320,512]{1,0:T(8,128)(2,1)S(1)} %collective-permute-done.16.refs_5_.refs_20_), channel_id=1, source_target_pairs={{0,4},{4,8},{8,12},{12,16},{16,20},{20,24},{24,28},{28,0},{1,5},{5... | collective-permute-start | bytes 983048 | tf_op jit(solution)/shard_map/ppermute | solution.py:277
  57.5 40.7 %collective-permute-start.10 = (bf16[512,1024]{1,0:T(8,128)(2,1)S(1)}, bf16[512,1024]{1,0:T(8,128)(2,1)S(1)}, u32[]{:S(2)}, u32[]{:S(2)}) collective-permute-start(bf16[512,1024]{1,0:T(8,128)(2,1)S(1)} %constant_dynamic-update-slice_fusion.refs_10_.refs_16_.refs_8_.refs_14_.refs_23_.refs_29_.refs_4_.refs_3_.r, ...), channel_id=1, source_target_pairs={{0,64},{64,128},{128,192},{192,0},{1,65},{65,129},{129,193},{193,1... | collective-permute-start | bytes 3145736 | tf_op jit(solution)/shard_map/ppermute | solution.py:277
  63.3 16.2 %collective-permute-start.17 = (bf16[640,512]{1,0:T(8,128)(2,1)S(1)}, bf16[640,512]{1,0:T(8,128)(2,1)S(1)}, u32[]{:S(2)}, u32[]{:S(2)}) collective-permute-start(bf16[640,512]{1,0:T(8,128)(2,1)S(1)} %pad_maximum_fusion.2), channel_id=1, source_target_pairs={{0,1},{1,0},{2,3},{3,2},{4,5},{5,4},{6,7},{7,6},{8,9},{9,8},{10,11... | collective-permute-start | bytes 1966088 | tf_op jit(solution)/shard_map/ppermute | solution.py:307
  75.3 15.8 %collective-permute-start.14 = (bf16[640,512]{1,0:T(8,128)(2,1)S(1)}, bf16[640,512]{1,0:T(8,128)(2,1)S(1)}, u32[]{:S(2)}, u32[]{:S(2)}) collective-permute-start(bf16[640,512]{1,0:T(8,128)(2,1)S(1)} %collective-permute-done.refs_3_.refs_10_), channel_id=1, source_target_pairs={{0,28},{4,0},{8,4},{12,8},{16,12},{20,16},{24,20},{28,24},{1,29},{... | collective-permute-start | bytes 1966088 | tf_op jit(solution)/shard_map/ppermute | solution.py:280
  77.1 24.5 %collective-permute-start.23 = (bf16[640,512]{1,0:T(8,128)(2,1)S(1)}, bf16[640,512]{1,0:T(8,128)(2,1)S(1)}, u32[]{:S(2)}, u32[]{:S(2)}) collective-permute-start(bf16[640,512]{1,0:T(8,128)(2,1)S(1)} %collective-permute-done.18.refs_4_.refs_19_), channel_id=1, source_target_pairs={{0,4},{4,8},{8,12},{12,16},{16,20},{20,24},{24,28},{28,0},{1,5},{5... | collective-permute-start | bytes 1966088 | tf_op jit(solution)/shard_map/ppermute | solution.py:277
  79.5 18.6 %collective-permute-start.25 = (bf16[320,512]{1,0:T(8,128)(2,1)S(1)}, bf16[320,512]{1,0:T(8,128)(2,1)S(1)}, u32[]{:S(2)}, u32[]{:S(2)}) collective-permute-start(bf16[320,512]{1,0:T(8,128)(2,1)S(1)} %collective-permute-done.20.refs_2_), channel_id=1, source_target_pairs={{0,28},{4,0},{8,4},{12,8},{16,12},{20,16},{24,20},{28,24},{1,29},{... | collective-permute-start | bytes 983048 | tf_op jit(solution)/shard_map/ppermute | solution.py:280
  91.1 26.2 %collective-permute-start.27 = (bf16[512,1024]{1,0:T(8,128)(2,1)S(1)}, bf16[512,1024]{1,0:T(8,128)(2,1)S(1)}, u32[]{:S(2)}, u32[]{:S(2)}) collective-permute-start(bf16[512,1024]{1,0:T(8,128)(2,1)S(1)} %pad_maximum_fusion), channel_id=1, source_target_pairs={{0,64},{64,128},{128,192},{192,0},{1,65},{65,129},{129,193},{193,1... | collective-permute-start | bytes 3145736 | tf_op jit(solution)/shard_map/ppermute | solution.py:277
  91.1 26.2 %collective-permute-start.28 = (bf16[512,1024]{1,0:T(8,128)(2,1)S(1)}, bf16[512,1024]{1,0:T(8,128)(2,1)S(1)}, u32[]{:S(2)}, u32[]{:S(2)}) collective-permute-start(bf16[512,1024]{1,0:T(8,128)(2,1)S(1)} %collective-permute-done.8.refs_12_.refs_18_.refs_10_.refs_16_.refs_25_.refs_31_.refs_6_.refs_5_.refs_4_), channel_id=1, source_target_pairs={{0,192},{64,0},{128,64},{192,128},{1,193},{65,1},{129,65},{193,129... | collective-permute-start | bytes 3145736 | tf_op jit(solution)/shard_map/ppermute | solution.py:280
  98.1 16.4 %collective-permute-start.22 = (bf16[640,512]{1,0:T(8,128)(2,1)S(1)}, bf16[640,512]{1,0:T(8,128)(2,1)S(1)}, u32[]{:S(2)}, u32[]{:S(2)}) collective-permute-start(bf16[640,512]{1,0:T(8,128)(2,1)S(1)} %pad_maximum_fusion.3), channel_id=1, source_target_pairs={{0,1},{1,0},{2,3},{3,2},{4,5},{5,4},{6,7},{7,6},{8,9},{9,8},{10,11... | collective-permute-start | bytes 1966088 | tf_op jit(solution)/shard_map/ppermute | solution.py:307
  98.2 16.4 %collective-permute-start.19 = (bf16[640,512]{1,0:T(8,128)(2,1)S(1)}, bf16[640,512]{1,0:T(8,128)(2,1)S(1)}, u32[]{:S(2)}, u32[]{:S(2)}) collective-permute-start(bf16[640,512]{1,0:T(8,128)(2,1)S(1)} %collective-permute-done.14.refs_1_.refs_16_), channel_id=1, source_target_pairs={{0,28},{4,0},{8,4},{12,8},{16,12},{20,16},{24,20},{28,24},{1,29},{... | collective-permute-start | bytes 1966088 | tf_op jit(solution)/shard_map/ppermute | solution.py:280
  101.6 15.7 %collective-permute-start.24 = (bf16[640,512]{1,0:T(8,128)(2,1)S(1)}, bf16[640,512]{1,0:T(8,128)(2,1)S(1)}, u32[]{:S(2)}, u32[]{:S(2)}) collective-permute-start(bf16[640,512]{1,0:T(8,128)(2,1)S(1)} %collective-permute-done.23.refs_4_), channel_id=1, source_target_pairs={{0,4},{4,8},{8,12},{12,16},{16,20},{20,24},{24,28},{28,0},{1,5},{5... | collective-permute-start | bytes 1966088 | tf_op jit(solution)/shard_map/ppermute | solution.py:277
  114.5 8.6 %collective-permute-start.26 = (bf16[320,512]{1,0:T(8,128)(2,1)S(1)}, bf16[320,512]{1,0:T(8,128)(2,1)S(1)}, u32[]{:S(2)}, u32[]{:S(2)}) collective-permute-start(bf16[320,512]{1,0:T(8,128)(2,1)S(1)} %collective-permute-done.25.refs_1_.refs_0_), channel_id=1, source_target_pairs={{0,1},{1,0},{2,3},{3,2},{4,5},{5,4},{6,7},{7,6},{8,9},{9,8},{10,11... | collective-permute-start | bytes 983048 | tf_op jit(solution)/shard_map/ppermute | solution.py:309
  118.7 11.1 %collective-permute-start.30 = (f32[640,512]{1,0:T(8,128)S(1)}, f32[640,512]{1,0:T(8,128)S(1)}, u32[]{:S(2)}, u32[]{:S(2)}) collective-permute-start(f32[640,512]{1,0:T(8,128)S(1)} %shard_map.33), channel_id=1, source_target_pairs={{0,2},{2,0},{1,3},{3,1},{4,6},{6,4},{5,7},{7,5},{8,10},{10,8},{9,1... | collective-permute-start | bytes 3932168 | tf_op jit(solution)/shard_map/ppermute | solution.py:347
  124.4 5.8 %collective-permute-start.29 = (f32[640,512]{1,0:T(8,128)S(1)}, f32[640,512]{1,0:T(8,128)S(1)}, u32[]{:S(2)}, u32[]{:S(2)}) collective-permute-start(f32[640,512]{1,0:T(8,128)S(1)} %shard_map.32), channel_id=1, source_target_pairs={{0,2},{2,0},{1,3},{3,1},{4,6},{6,4},{5,7},{7,5},{8,10},{10,8},{9,1... | collective-permute-start | bytes 3932168 | tf_op jit(solution)/shard_map/ppermute | solution.py:348
